TPU v7x, 32 devices: a whole 2x2x4 slice. The times are simulated.
32 devices in a mesh: dp: 16 (over z, x, core), tensor: 2 (over y).
Axes of the slice: x: 2, y: 2, z: 4, core: 2. Of those that a mesh axis runs over, the one named last changes fastest.
Arguments:
- layer_input: float32 [4096, 2048], P('dp'), may hold values from -6 to 6
- positions: int32 [4096], P('dp'), may hold values from 0 to 2047, as said below
- norm1_gain: bfloat16 [2048], P('dp'), may hold values from 0.5 to 1.5
- w_q: bfloat16 [2048, 2048], P('dp', 'tensor'), may hold values from -0.125 to 0.125
- w_k: bfloat16 [2048, 256], P('dp', 'tensor'), may hold values from -0.125 to 0.125
- w_v: bfloat16 [2048, 256], P('dp', 'tensor'), may hold values from -0.125 to 0.125
- w_o: bfloat16 [2048, 2048], P('tensor', 'dp'), may hold values from -0.5 to 0.5
- norm2_gain: bfloat16 [2048], P('dp'), may hold values from 0.5 to 1.5
- w_gate: bfloat16 [2048, 5632], P('dp', 'tensor'), may hold values from -0.125 to 0.125
- w_up: bfloat16 [2048, 5632], P('dp', 'tensor'), may hold values from -0.125 to 0.125
- w_down: bfloat16 [5632, 2048], P('tensor', 'dp'), may hold values from -0.078125 to 0.078125
- out_grad: float32 [4096, 2048], P('dp'), may hold values from -6 to 6
Outputs:
- layer_output: float32 [4096, 2048], P('dp')
- x_grad: float32 [4096, 2048], P('dp')
- grad_norm1: float32 [2048], P('dp')
- grad_w_q: float32 [2048, 2048], P('dp', 'tensor')
- grad_w_k: float32 [2048, 256], P('dp', 'tensor')
- grad_w_v: float32 [2048, 256], P('dp', 'tensor')
- grad_w_o: float32 [2048, 2048], P('tensor', 'dp')
- grad_norm2: float32 [2048], P('dp')
- grad_w_gate: float32 [2048, 5632], P('dp', 'tensor')
- grad_w_up: float32 [2048, 5632], P('dp', 'tensor')
- grad_w_down: float32 [5632, 2048], P('tensor', 'dp')
Inputs may be any that keep to these rules, and one draw needn't show every extreme that they name: Each sequence of 256 tokens packs one or two documents; positions rise by one from token to token within a document and restart at 0 where a second document begins.
All inputs are finite; a program needn't handle non-finite values.
Results may differ from a plain program's by a relative error of at most 0.015.
Values may be sent and summed in bfloat16 or wider, within the bound.
A program may use at most 256 MiB of HBM per device.

v0:
```python
import math

import jax
import jax.numpy as jnp
from jax import lax
from jax.sharding import PartitionSpec as P

HD = 64
L = 256


epsilon = 1e-05


def matmul(left_side, right_side):
    return jnp.dot(left_side, right_side, preferred_element_type=jnp.float32)


def matmul_nt(left_side, right_side):
    return lax.dot_general(
        left_side, right_side, (((1,), (1,)), ((), ())), preferred_element_type=jnp.float32
    )


def matmul_tn(left_side, right_side):
    return lax.dot_general(
        left_side, right_side, (((0,), (0,)), ((), ())), preferred_element_type=jnp.float32
    )


def rms_parts(row_values):
    inv_rms = lax.rsqrt(jnp.mean(row_values * row_values, axis=-1, keepdims=True) + epsilon)
    return (inv_rms, row_values * inv_rms)


def rope_tables(pos_rows, head_dim):
    half_dim = head_dim // 2
    frequency = jnp.exp(
        jnp.arange(half_dim, dtype=jnp.float32) * (-2.0 * math.log(10000.0) / head_dim)
    )
    angles = pos_rows.astype(jnp.float32)[:, None] * frequency[None, :]
    return (jnp.cos(angles), jnp.sin(angles))


def rotate(row_values, cos_table, sin_table, direction_sign):
    half_dim = row_values.shape[-1] // 2
    first_half = row_values[..., :half_dim]
    second = row_values[..., half_dim:]
    cos_part = cos_table[:, None, :]
    sin_part = sin_table[:, None, :] * direction_sign
    return jnp.concatenate(
        [first_half * cos_part - second * sin_part, second * cos_part + first_half * sin_part],
        axis=-1,
    )


def causal_scores(queries, key_rows):
    length, head_count, head_dim = queries.shape
    kv_count = key_rows.shape[1]
    grouped = queries.reshape(length, kv_count, head_count // kv_count, head_dim)
    scores = jnp.einsum(
        "qkgd,pkd->kgqp", grouped, key_rows, preferred_element_type=jnp.float32
    ) * head_dim ** (-0.5)
    future_mask = jnp.arange(length)[None, :] > jnp.arange(length)[:, None]
    return (grouped, jnp.where(future_mask, -jnp.inf, scores))


def attend(queries, key_rows, value_rows):
    grouped, scores = causal_scores(queries, key_rows)
    row_top = jnp.max(scores, axis=-1, keepdims=True)
    log_total = row_top + jnp.log(jnp.sum(jnp.exp(scores - row_top), axis=-1, keepdims=True))
    weights = jnp.exp(scores - log_total).astype(jnp.bfloat16)
    attended = jnp.einsum("kgqp,pkd->qkgd", weights, value_rows, preferred_element_type=jnp.float32)
    return (attended.reshape(queries.shape[0], -1).astype(jnp.bfloat16), log_total)


def attend_back(queries, key_rows, value_rows, attended, d_attended, log_total):
    length, head_count, head_dim = queries.shape
    kv_count = key_rows.shape[1]
    grouped, scores = causal_scores(queries, key_rows)
    prob_rows = jnp.exp(scores - log_total)
    d_grouped = d_attended.reshape(length, kv_count, head_count // kv_count, head_dim)
    out_grouped = attended.reshape(length, kv_count, head_count // kv_count, head_dim)
    row_delta = jnp.sum(out_grouped.astype(jnp.float32) * d_grouped.astype(jnp.float32), axis=-1)
    row_delta = jnp.transpose(row_delta, (1, 2, 0))[..., None]
    d_probs = jnp.einsum(
        "qkgd,pkd->kgqp", d_grouped, value_rows, preferred_element_type=jnp.float32
    )
    d_scores = (prob_rows * (d_probs - row_delta) * head_dim ** (-0.5)).astype(jnp.bfloat16)
    d_query = jnp.einsum("kgqp,pkd->qkgd", d_scores, key_rows, preferred_element_type=jnp.float32)
    d_keys = jnp.einsum("kgqp,qkgd->pkd", d_scores, grouped, preferred_element_type=jnp.float32)
    d_values = jnp.einsum(
        "kgqp,qkgd->pkd",
        prob_rows.astype(jnp.bfloat16),
        d_grouped,
        preferred_element_type=jnp.float32,
    )
    return (d_query.reshape(length, head_count, head_dim), d_keys, d_values)


def body(
    layer_input,
    positions,
    norm1_gain,
    w_q,
    w_k,
    w_v,
    w_o,
    norm2_gain,
    w_gate,
    w_up,
    w_down,
    out_grad,
):
    gathered = (
        lax.all_gather(norm1_gain, "dp", axis=0, tiled=True),
        lax.all_gather(w_q, "dp", axis=0, tiled=True),
        lax.all_gather(w_k, "dp", axis=0, tiled=True),
        lax.all_gather(w_v, "dp", axis=0, tiled=True),
        lax.all_gather(w_o, "dp", axis=1, tiled=True),
        lax.all_gather(norm2_gain, "dp", axis=0, tiled=True),
        lax.all_gather(w_gate, "dp", axis=0, tiled=True),
        lax.all_gather(w_up, "dp", axis=0, tiled=True),
        lax.all_gather(w_down, "dp", axis=1, tiled=True),
    )
    gain_one, query_w, key_w, value_w, out_w, gain_two, gate_w, up_w, down_w = gathered
    row_count = layer_input.shape[0]
    seq_count = row_count // L
    head_count = query_w.shape[1] // HD
    kv_count = key_w.shape[1] // HD
    inv_one, norm_one = rms_parts(layer_input)
    normed_one = (norm_one * gain_one.astype(jnp.float32)).astype(jnp.bfloat16)
    cos_table, sin_table = rope_tables(positions, HD)
    queries = rotate(
        matmul(normed_one, query_w).reshape(row_count, head_count, HD), cos_table, sin_table, 1.0
    ).astype(jnp.bfloat16)
    key_rows = rotate(
        matmul(normed_one, key_w).reshape(row_count, kv_count, HD), cos_table, sin_table, 1.0
    ).astype(jnp.bfloat16)
    value_rows = matmul(normed_one, value_w).astype(jnp.bfloat16).reshape(row_count, kv_count, HD)
    query_seq = queries.reshape(seq_count, L, head_count, HD)
    key_seq = key_rows.reshape(seq_count, L, kv_count, HD)
    value_seq = value_rows.reshape(seq_count, L, kv_count, HD)
    attended, log_total = lax.map(
        lambda block_in: attend(block_in[0], block_in[1], block_in[2]),
        (query_seq, key_seq, value_seq),
    )
    attended_rows = attended.reshape(row_count, head_count * HD)
    hidden = layer_input + lax.psum(matmul(attended_rows, out_w), "tensor")
    inv_two, norm_two = rms_parts(hidden)
    normed_two = (norm_two * gain_two.astype(jnp.float32)).astype(jnp.bfloat16)
    gate_pre = matmul(normed_two, gate_w)
    up_pre = matmul(normed_two, up_w)
    activated = (jax.nn.silu(gate_pre) * up_pre).astype(jnp.bfloat16)
    layer_output = hidden + lax.psum(
        matmul(activated, down_w).astype(jnp.bfloat16), "tensor"
    ).astype(jnp.float32)
    grad_rows = out_grad.astype(jnp.bfloat16)
    d_act = matmul_nt(grad_rows, down_w)
    sigmoid_gate = jax.nn.sigmoid(gate_pre)
    d_gate = (d_act * up_pre * sigmoid_gate * (1.0 + gate_pre * (1.0 - sigmoid_gate))).astype(
        jnp.bfloat16
    )
    d_up = (d_act * jax.nn.silu(gate_pre)).astype(jnp.bfloat16)
    grad_down = matmul_tn(activated, grad_rows)
    grad_gate = matmul_tn(normed_two, d_gate)
    grad_up = matmul_tn(normed_two, d_up)
    d_norm_two = lax.psum(matmul_nt(d_gate, gate_w) + matmul_nt(d_up, up_w), "tensor")
    grad_gain_two = jnp.sum(d_norm_two * norm_two, axis=0)
    e_two = d_norm_two * gain_two.astype(jnp.float32)
    d_hidden = out_grad + inv_two * (
        e_two - norm_two * jnp.mean(e_two * norm_two, axis=-1, keepdims=True)
    )
    hidden_rows = d_hidden.astype(jnp.bfloat16)
    grad_out = matmul_tn(attended_rows, hidden_rows)
    d_attended = matmul_nt(hidden_rows, out_w).astype(jnp.bfloat16)
    d_query, d_keys, d_values = lax.map(
        lambda block_in: attend_back(
            block_in[0], block_in[1], block_in[2], block_in[3], block_in[4], block_in[5]
        ),
        (
            query_seq,
            key_seq,
            value_seq,
            attended,
            d_attended.reshape(seq_count, L, head_count * HD),
            log_total,
        ),
    )
    dq_raw = (
        rotate(d_query.reshape(row_count, head_count, HD), cos_table, sin_table, -1.0)
        .astype(jnp.bfloat16)
        .reshape(row_count, head_count * HD)
    )
    dk_raw = (
        rotate(d_keys.reshape(row_count, kv_count, HD), cos_table, sin_table, -1.0)
        .astype(jnp.bfloat16)
        .reshape(row_count, kv_count * HD)
    )
    dv_rows = d_values.astype(jnp.bfloat16).reshape(row_count, kv_count * HD)
    grad_query = matmul_tn(normed_one, dq_raw)
    grad_key = matmul_tn(normed_one, dk_raw)
    grad_value = matmul_tn(normed_one, dv_rows)
    d_norm_one = lax.psum(
        matmul_nt(dq_raw, query_w) + matmul_nt(dk_raw, key_w) + matmul_nt(dv_rows, value_w),
        "tensor",
    )
    grad_gain_one = jnp.sum(d_norm_one * norm_one, axis=0)
    e_one = d_norm_one * gain_one.astype(jnp.float32)
    x_grad = d_hidden + inv_one * (
        e_one - norm_one * jnp.mean(e_one * norm_one, axis=-1, keepdims=True)
    )
    summed = (
        lax.psum_scatter(grad_gain_one, "dp", scatter_dimension=0, tiled=True),
        lax.psum_scatter(grad_query, "dp", scatter_dimension=0, tiled=True),
        lax.psum_scatter(grad_key, "dp", scatter_dimension=0, tiled=True),
        lax.psum_scatter(grad_value, "dp", scatter_dimension=0, tiled=True),
        lax.psum_scatter(grad_out, "dp", scatter_dimension=1, tiled=True),
        lax.psum_scatter(grad_gain_two, "dp", scatter_dimension=0, tiled=True),
        lax.psum_scatter(grad_gate, "dp", scatter_dimension=0, tiled=True),
        lax.psum_scatter(grad_up, "dp", scatter_dimension=0, tiled=True),
        lax.psum_scatter(grad_down, "dp", scatter_dimension=1, tiled=True),
    )
    (
        shard_gain_one,
        shard_query,
        shard_key,
        shard_value,
        shard_out,
        shard_gain_two,
        shard_gate,
        shard_up,
        shard_down,
    ) = summed
    return (
        layer_output,
        x_grad,
        shard_gain_one,
        shard_query,
        shard_key,
        shard_value,
        shard_out,
        shard_gain_two,
        shard_gate,
        shard_up,
        shard_down,
    )


def solution(mesh):
    in_specs = (
        P("dp", None),
        P("dp"),
        P("dp"),
        P("dp", "tensor"),
        P("dp", "tensor"),
        P("dp", "tensor"),
        P("tensor", "dp"),
        P("dp"),
        P("dp", "tensor"),
        P("dp", "tensor"),
        P("tensor", "dp"),
        P("dp", None),
    )
    out_specs = (
        P("dp", None),
        P("dp", None),
        P("dp"),
        P("dp", "tensor"),
        P("dp", "tensor"),
        P("dp", "tensor"),
        P("tensor", "dp"),
        P("dp"),
        P("dp", "tensor"),
        P("dp", "tensor"),
        P("tensor", "dp"),
    )
    return jax.shard_map(body, mesh=mesh, in_specs=in_specs, out_specs=out_specs, check_vma=False)
```

profile of v0, /device:TPU:0, one launch (start us, length us, event | category | flops | bytes accessed | tf_op | source)
XLA Modules:
  0.0 1732.3 jit_solution(12883286707525709895)
XLA Ops:
  8.7 23.3 %all-gather = bf16[16,1,128]{2,1,0:T(2,128)(2,1)S(1)} all-gather(bf16[1,1,128]{2,1,0:T(2,128)(2,1)} %bitcast.137), channel_id=1, replica_groups=mesh['dp'=16,'tensor'=2] {'dp'}, dimensions={0}, use_global_device_ids=true | all-gather | bytes 4352 | tf_op jit(solution)/shard_map/all_gather | solution.py:116
  35.4 20.6 %all_gather.29 = bf16[2048,128]{1,0:T(8,128)(2,1)S(1)} all-gather(bf16[128,128]{1,0:T(8,128)(2,1)S(1)} %copy-done.24), channel_id=1, replica_groups=mesh['dp'=16,'tensor'=2] {'dp'}, dimensions={0}, use_global_device_ids=true | all-gather | bytes 557056 | tf_op jit(solution)/shard_map/all_gather | solution.py:118
  57.4 22.4 %all_gather.28 = bf16[2048,128]{1,0:T(8,128)(2,1)S(1)} all-gather(bf16[128,128]{1,0:T(8,128)(2,1)S(1)} %copy-done.25), channel_id=1, replica_groups=mesh['dp'=16,'tensor'=2] {'dp'}, dimensions={0}, use_global_device_ids=true | all-gather | bytes 557056 | tf_op jit(solution)/shard_map/all_gather | solution.py:119
  90.7 30.0 %all-gather.10.cloned.1.call-done = bf16[1024,2048]{1,0:T(8,128)(2,1)} async-done(((bf16[1024,128]{1,0:T(8,128)(2,1)}), bf16[1024,2048]{1,0:T(8,128)(2,1)}) %all-gather.10.cloned.1.call-update) | async-done | bytes 4194320 | tf_op jit(solution)/shard_map/all_gather | solution.py:120
  120.7 4.9 fusion.27
  127.5 18.7 %all-gather.1 = bf16[16,1,128]{2,1,0:T(2,128)(2,1)S(1)} all-gather(bf16[1,1,128]{2,1,0:T(2,128)(2,1)S(1)} %bitcast.138), channel_id=1, replica_groups=mesh['dp'=16,'tensor'=2] {'dp'}, dimensions={0}, use_global_device_ids=true | all-gather | bytes 4352 | tf_op jit(solution)/shard_map/all_gather | solution.py:121
  146.2 40.8 %all-reduce.8.cloned.1.call-done = f32[256,2048]{1,0:T(8,128)} async-done(((f32[256,2048]{1,0:T(8,128)}), f32[256,2048]{1,0:T(8,128)}) %all-reduce.8.cloned.1.call-update) | async-done | bytes 2097168 | tf_op jit(solution)/shard_map/psum | solution.py:149
  191.5 91.7 %all-gather.12.cloned.1.call-done = bf16[2048,2816]{1,0:T(8,128)(2,1)} async-done(((bf16[128,2816]{1,0:T(8,128)(2,1)}), bf16[2048,2816]{1,0:T(8,128)(2,1)}) %all-gather.12.cloned.1.call-update) | async-done | bytes 11534352 | tf_op jit(solution)/shard_map/all_gather | solution.py:122
  283.1 9.3 fusion.28
  292.4 85.1 %all-gather.14.cloned.1.call-done = bf16[2048,2816]{1,0:T(8,128)(2,1)} async-done(((bf16[128,2816]{1,0:T(8,128)(2,1)}), bf16[2048,2816]{1,0:T(8,128)(2,1)}) %all-gather.14.cloned.1.call-update) | async-done | bytes 11534352 | tf_op jit(solution)/shard_map/all_gather | solution.py:123
  377.5 9.3 fusion.29
  386.8 87.9 %all-gather.16.cloned.1.call-done = bf16[2816,2048]{1,0:T(8,128)(2,1)} async-done(((bf16[2816,128]{1,0:T(8,128)(2,1)}), bf16[2816,2048]{1,0:T(8,128)(2,1)}) %all-gather.16.cloned.1.call-update) | async-done | bytes 11534352 | tf_op jit(solution)/shard_map/all_gather | solution.py:124
  474.7 11.8 multiply_convert_fusion
  486.5 7.1 fusion.30
  493.6 8.8 convolution_add_fusion.2
  502.4 9.5 convolution_convert_fusion
  512.0 51.6 %all-reduce.12.cloned.1.call-done = f32[256,2048]{1,0:T(8,128)} async-done(((f32[256,2048]{1,0:T(8,128)}), f32[256,2048]{1,0:T(8,128)}) %all-reduce.12.cloned.1.call-update) | async-done | bytes 2097168 | tf_op jit(solution)/shard_map/psum | solution.py:168
  566.5 39.6 %all-reduce.10.cloned.1.call-done = bf16[256,2048]{1,0:T(8,128)(2,1)} async-done(((bf16[256,2048]{1,0:T(8,128)(2,1)}), bf16[256,2048]{1,0:T(8,128)(2,1)}) %all-reduce.10.cloned.1.call-update) | async-done | bytes 1048592 | tf_op jit(solution)/shard_map/psum | solution.py:155
  606.1 5.2 multiply_add_fusion.1
  634.1 5.7 fusion.32
  640.8 6.2 fusion.7
  648.2 10.8 fusion.35
  659.1 11.2 fusion.36
  670.4 13.1 fusion.10
  685.3 8.7 all-reduce.14.cloned.1.call-done
  696.2 61.1 %all-reduce.2 = (f32[2048]{0:T(1024)S(1)}, f32[2048]{0:T(1024)S(1)}) all-reduce(f32[2048]{0:T(1024)S(1)} %get-tuple-element.51, f32[2048]{0:T(1024)S(1)} %get-tuple-element.49), channel_id=2, replica_groups=mesh['dp'=16,'tensor'=2] {'dp'}, use_global_device_ids=true, to_apply=%region_12.13.clone | all-reduce | flops 4096 | bytes 32768
  762.5 54.0 %reduce-scatter.12.cloned.1.call-done = f32[128,128]{1,0:T(8,128)} async-done(((f32[2048,128]{1,0:T(8,128)}), f32[128,128]{1,0:T(8,128)}) %reduce-scatter.12.cloned.1.call-update) | async-done | bytes 65552 | tf_op jit(solution)/shard_map/reduce_scatter | solution.py:217
  816.5 107.1 %reduce-scatter.8.cloned.1.call-done = f32[128,1024]{1,0:T(8,128)} async-done(((f32[2048,1024]{1,0:T(8,128)}), f32[128,1024]{1,0:T(8,128)}) %reduce-scatter.8.cloned.1.call-update) | async-done | bytes 524304 | tf_op jit(solution)/shard_map/reduce_scatter | solution.py:215
  923.5 107.9 %reduce-scatter.14.cloned.1.call-done = f32[1024,128]{1,0:T(8,128)} async-done(((f32[1024,2048]{1,0:T(8,128)}), f32[1024,128]{1,0:T(8,128)}) %reduce-scatter.14.cloned.1.call-update) | async-done | bytes 524304 | tf_op jit(solution)/shard_map/reduce_scatter | solution.py:218
  1031.4 231.7 %reduce-scatter.16.cloned.1.call-done = f32[128,2816]{1,0:T(8,128)} async-done(((f32[2048,2816]{1,0:T(8,128)}), f32[128,2816]{1,0:T(8,128)}) %reduce-scatter.16.cloned.1.call-update) | async-done | bytes 1441808 | tf_op jit(solution)/shard_map/reduce_scatter | solution.py:220
  1263.2 231.2 %reduce-scatter.18.cloned.1.call-done = f32[128,2816]{1,0:T(8,128)} async-done(((f32[2048,2816]{1,0:T(8,128)}), f32[128,2816]{1,0:T(8,128)}) %reduce-scatter.18.cloned.1.call-update) | async-done | bytes 1441808 | tf_op jit(solution)/shard_map/reduce_scatter | solution.py:221
  1494.4 230.9 %reduce-scatter.20.cloned.1.call-done = f32[2816,128]{1,0:T(8,128)} async-done(((f32[2816,2048]{1,0:T(8,128)}), f32[2816,128]{1,0:T(8,128)}) %reduce-scatter.20.cloned.1.call-update) | async-done | bytes 1441808 | tf_op jit(solution)/shard_map/reduce_scatter | solution.py:222
  (147 shorter events, 59.7 us)
Async XLA Ops:
  7.2 48.8 %copy-start = (f32[256,2048]{1,0:T(8,128)S(1)}, f32[256,2048]{1,0:T(8,128)}, u32[]{:S(2)}) copy-start(f32[256,2048]{1,0:T(8,128)} %param.12) | copy-start | bytes 6291460
  7.2 28.2 %copy-start.24 = (bf16[128,128]{1,0:T(8,128)(2,1)S(1)}, bf16[128,128]{1,0:T(8,128)(2,1)}, u32[]{:S(2)}) copy-start(bf16[128,128]{1,0:T(8,128)(2,1)} %param.16) | copy-start | bytes 98308
  7.2 74.6 %all-gather.8.cloned.1.call-start = ((), (), s32[]{:S(2)}) async-start(), calls=%async_computation.7 | async-start | bytes 4456448 | tf_op jit(solution)/shard_map/all_gather | solution.py:117
  7.9 112.8 %all-gather.10.cloned.1.call-start = ((), (), s32[]{:S(2)}) async-start(), calls=%async_computation.8 | async-start | bytes 4456448 | tf_op jit(solution)/shard_map/all_gather | solution.py:120
  8.7 178.3 %all-reduce.8.cloned.1.call-start = ((), (), s32[]{:S(2)}) async-start(), calls=%async_computation.9 | async-start | bytes 4194304 | tf_op jit(solution)/shard_map/psum | solution.py:149
  35.2 21.6 %copy-start.28 = (f32[256]{0:T(256)}, f32[256]{0:T(256)S(1)}, u32[]{:S(2)}) copy-start(f32[256]{0:T(256)S(1)} %add_rsqrt_fusion.1) | copy-start | bytes 3076
  57.4 28.5 %copy-start.19 = (bf16[256,2,32]{0,2,1:T(8,128)(2,1)}, bf16[256,2,32]{0,2,1:T(8,128)(2,1)S(1)}, u32[]{:S(2)}) copy-start(bf16[256,2,32]{0,2,1:T(8,128)(2,1)S(1)} %get-tuple-element.78) | copy-start | bytes 98308
  81.8 4.2 copy-start.17
  81.8 4.2 copy-start.21
  87.7 3.1 copy-start.26
  125.7 157.4 %all-gather.12.cloned.1.call-start = ((), (), s32[]{:S(2)}) async-start(), calls=%async_computation.10 | async-start | bytes 12255232 | tf_op jit(solution)/shard_map/all_gather | solution.py:122
  126.2 251.3 %all-gather.14.cloned.1.call-start = ((), (), s32[]{:S(2)}) async-start(), calls=%async_computation.11 | async-start | bytes 12255232 | tf_op jit(solution)/shard_map/all_gather | solution.py:123
  126.8 347.9 %all-gather.16.cloned.1.call-start = ((), (), s32[]{:S(2)}) async-start(), calls=%async_computation.12 | async-start | bytes 12255232 | tf_op jit(solution)/shard_map/all_gather | solution.py:124
  127.4 436.3 %all-reduce.12.cloned.1.call-start = ((), (), s32[]{:S(2)}) async-start(), calls=%async_computation.14 | async-start | bytes 4194304 | tf_op jit(solution)/shard_map/psum | solution.py:168
  486.4 7.1 copy-start.14
  486.5 7.1 copy-start.13
  502.4 103.7 %all-reduce.10.cloned.1.call-start = ((), (), s32[]{:S(2)}) async-start(), calls=%async_computation.13 | async-start | bytes 2097152 | tf_op jit(solution)/shard_map/psum | solution.py:155
  512.0 182.0 %all-reduce.14.cloned.1.call-start = ((), (), s32[]{:S(2)}) async-start(), calls=%async_computation.15 | async-start | bytes 4194304 | tf_op jit(solution)/shard_map/psum | solution.py:204
  606.1 6.5 copy-start.32
  614.7 3.4 copy-start.18
  618.1 3.9 copy-start.20
  618.1 3.9 copy-start.22
  618.2 4.4 copy-start.16
  625.7 2.2 copy-start.11
  630.9 131.6 %reduce-scatter.10.cloned.1.call-start = ((), (), s32[]{:S(2)}) async-start(), calls=%async_computation.17 | async-start | bytes 1114112 | tf_op jit(solution)/shard_map/reduce_scatter | solution.py:216
  632.4 184.1 %reduce-scatter.12.cloned.1.call-start = ((), (), s32[]{:S(2)}) async-start(), calls=%async_computation.18 | async-start | bytes 1114112 | tf_op jit(solution)/shard_map/reduce_scatter | solution.py:217
  634.0 289.5 %reduce-scatter.8.cloned.1.call-start = ((), (), s32[]{:S(2)}) async-start(), calls=%async_computation.16 | async-start | bytes 8912896 | tf_op jit(solution)/shard_map/reduce_scatter | solution.py:215
  639.8 391.7 %reduce-scatter.14.cloned.1.call-start = ((), (), s32[]{:S(2)}) async-start(), calls=%async_computation.19 | async-start | bytes 8912896 | tf_op jit(solution)/shard_map/reduce_scatter | solution.py:218
  647.0 616.1 %reduce-scatter.16.cloned.1.call-start = ((), (), s32[]{:S(2)}) async-start(), calls=%async_computation.20 | async-start | bytes 24510464 | tf_op jit(solution)/shard_map/reduce_scatter | solution.py:220
  659.1 835.3 %reduce-scatter.18.cloned.1.call-start = ((), (), s32[]{:S(2)}) async-start(), calls=%async_computation.21 | async-start | bytes 24510464 | tf_op jit(solution)/shard_map/reduce_scatter | solution.py:221
  670.3 1055.0 %reduce-scatter.20.cloned.1.call-start = ((), (), s32[]{:S(2)}) async-start(), calls=%async_computation.22 | async-start | bytes 24510464 | tf_op jit(solution)/shard_map/reduce_scatter | solution.py:222
  683.4 10.6 copy-start.29
  (18 other events, 26.0 us)
Sparse Core Ops, SparseCore 0:
  10.2 55.9 all-gather.7
  68.3 52.3 all-gather.9
  125.8 61.1 all-reduce.7
  189.1 93.9 all-gather.11
  285.2 92.2 all-gather.13
  379.5 95.1 all-gather.15
  502.5 61.1 all-reduce.11
  566.0 40.0 all-reduce.9
  631.0 62.9 all-reduce.13
  698.0 57.5 reduce-scatter.9
  759.9 56.5 reduce-scatter.11
  821.0 102.5 reduce-scatter.7
  928.2 103.2 reduce-scatter.13
  1036.0 227.1 reduce-scatter.15
  1267.7 226.6 reduce-scatter.17
  1498.9 226.3 reduce-scatter.19
where the time goes:
time: 1740 us; the launch traced here: 1730 us
  waiting for transfers between devices  1400 us (80%)
  blocking collectives  146 us (8%)
  matrix products  131 us (8%)
  other arithmetic  24.2 us (1%)
    reduce_scatter x1, waiting for transfers between devices, body(): lax.psum_scatter(grad_gate, 'dp', scatter_dimension=0, tiled=True)  232 us
    reduce_scatter x1, waiting for transfers between devices, body(): lax.psum_scatter(grad_up, 'dp', scatter_dimension=0, tiled=True)  231 us
    reduce_scatter x1, waiting for transfers between devices, body(): lax.psum_scatter(grad_down, 'dp', scatter_dimension=1, tiled=True)  231 us
    reduce_scatter x1, waiting for transfers between devices, body(): lax.psum_scatter(grad_out, 'dp', scatter_dimension=1, tiled=True)  108 us
    reduce_scatter x1, waiting for transfers between devices, body(): lax.psum_scatter(grad_query, 'dp', scatter_dimension=0, tiled=True)  107 us
    all_gather x1, waiting for transfers between devices, body(): lax.all_gather(w_gate, 'dp', axis=0, tiled=True)  91.7 us
    all_gather x1, waiting for transfers between devices, body(): lax.all_gather(w_down, 'dp', axis=1, tiled=True)  87.9 us
    all_gather x1, waiting for transfers between devices, body(): lax.all_gather(w_up, 'dp', axis=0, tiled=True)  85.1 us
  transfers between devices with their start and end apart: 16, of which 14 were waited for; matrix products, arithmetic and copies ran while one was open for 6% of the time, Pallas kernels for 0%

commit v1 on v0

v1 whole, which is shorter than its diff:
```python
import functools
import math

import jax
import jax.numpy as jnp
from jax import lax
from jax.experimental import pallas as pl
from jax.experimental.pallas import tpu as pltpu
from jax.sharding import PartitionSpec as P

HD = 64
L = 256
TILE = 256
VMEM_BYTES = 67043328

epsilon = 1e-05

MESH_IDS = pl.DeviceIdType.MESH
VMEM_SPEC = pl.BlockSpec(memory_space=pltpu.VMEM)
ANY_SPEC = pl.BlockSpec(memory_space=pl.ANY)


def matmul(left_side, right_side):
    return jnp.dot(left_side, right_side, preferred_element_type=jnp.float32)


def matmul_nt(left_side, right_side):
    return lax.dot_general(
        left_side, right_side, (((1,), (1,)), ((), ())), preferred_element_type=jnp.float32
    )


def rms_parts(row_values):
    inv_rms = lax.rsqrt(jnp.mean(row_values * row_values, axis=-1, keepdims=True) + epsilon)
    return (inv_rms, row_values * inv_rms)


def rope_tables(pos_rows, head_dim):
    half_dim = head_dim // 2
    frequency = jnp.exp(
        jnp.arange(half_dim, dtype=jnp.float32) * (-2.0 * math.log(10000.0) / head_dim)
    )
    angles = pos_rows.astype(jnp.float32)[:, None] * frequency[None, :]
    return (jnp.cos(angles), jnp.sin(angles))


def rotate(row_values, cos_table, sin_table, direction_sign):
    half_dim = row_values.shape[-1] // 2
    first_half = row_values[..., :half_dim]
    second = row_values[..., half_dim:]
    cos_part = cos_table[:, None, :]
    sin_part = sin_table[:, None, :] * direction_sign
    return jnp.concatenate(
        [first_half * cos_part - second * sin_part, second * cos_part + first_half * sin_part],
        axis=-1,
    )


def causal_scores(queries, key_rows):
    length, head_count, head_dim = queries.shape
    kv_count = key_rows.shape[1]
    grouped = queries.reshape(length, kv_count, head_count // kv_count, head_dim)
    scores = jnp.einsum(
        "qkgd,pkd->kgqp", grouped, key_rows, preferred_element_type=jnp.float32
    ) * head_dim ** (-0.5)
    future_mask = jnp.arange(length)[None, :] > jnp.arange(length)[:, None]
    return (grouped, jnp.where(future_mask, -jnp.inf, scores))


def attend(queries, key_rows, value_rows):
    grouped, scores = causal_scores(queries, key_rows)
    row_top = jnp.max(scores, axis=-1, keepdims=True)
    log_total = row_top + jnp.log(jnp.sum(jnp.exp(scores - row_top), axis=-1, keepdims=True))
    weights = jnp.exp(scores - log_total).astype(jnp.bfloat16)
    attended = jnp.einsum("kgqp,pkd->qkgd", weights, value_rows, preferred_element_type=jnp.float32)
    return (attended.reshape(queries.shape[0], -1).astype(jnp.bfloat16), log_total)


def attend_back(queries, key_rows, value_rows, attended, d_attended, log_total):
    length, head_count, head_dim = queries.shape
    kv_count = key_rows.shape[1]
    grouped, scores = causal_scores(queries, key_rows)
    prob_rows = jnp.exp(scores - log_total)
    d_grouped = d_attended.reshape(length, kv_count, head_count // kv_count, head_dim)
    out_grouped = attended.reshape(length, kv_count, head_count // kv_count, head_dim)
    row_delta = jnp.sum(out_grouped.astype(jnp.float32) * d_grouped.astype(jnp.float32), axis=-1)
    row_delta = jnp.transpose(row_delta, (1, 2, 0))[..., None]
    d_probs = jnp.einsum(
        "qkgd,pkd->kgqp", d_grouped, value_rows, preferred_element_type=jnp.float32
    )
    d_scores = (prob_rows * (d_probs - row_delta) * head_dim ** (-0.5)).astype(jnp.bfloat16)
    d_query = jnp.einsum("kgqp,pkd->qkgd", d_scores, key_rows, preferred_element_type=jnp.float32)
    d_keys = jnp.einsum("kgqp,qkgd->pkd", d_scores, grouped, preferred_element_type=jnp.float32)
    d_values = jnp.einsum(
        "kgqp,qkgd->pkd",
        prob_rows.astype(jnp.bfloat16),
        d_grouped,
        preferred_element_type=jnp.float32,
    )
    return (d_query.reshape(length, head_count, head_dim), d_keys, d_values)


class Ring:
    def __init__(self, shards):
        self.count = shards // 2
        me = lax.axis_index("dp")
        self.me = me
        self.core = me % 2
        chip = me // 2
        side = chip % 2
        row = chip // 2
        self.place = row + side * (self.count - 1 - 2 * row)
        self.sign = 1 - 2 * self.core
        self.following = self.device(1, self.core)
        self.previous = self.device(-1, self.core)
        self.sibling = self.device(0, 1 - self.core)

    def chip(self, steps):
        place = (self.place + self.sign * steps + 2 * self.count) % self.count
        side = place // (self.count // 2)
        row = place + side * (self.count - 1 - 2 * place)
        return 2 * row + side

    def device(self, steps, core):
        return self.chip(steps) * 2 + core

    def behind(self, steps):
        return self.device(-steps, self.core)

    def greet(self, partner):
        barrier = pltpu.get_barrier_semaphore()
        for other in (self.following, self.previous, self.sibling):
            pl.semaphore_signal(barrier, inc=1, device_id={"dp": other}, device_id_type=MESH_IDS)
        if partner:
            pl.semaphore_signal(
                barrier,
                inc=1,
                device_id={"tensor": 1 - lax.axis_index("tensor")},
                device_id_type=MESH_IDS,
            )
        pl.semaphore_wait(barrier, 4 if partner else 3)


def send_to(device, source, target, send_sem, recv_sem):
    return pltpu.make_async_remote_copy(
        src_ref=source,
        dst_ref=target,
        send_sem=send_sem,
        recv_sem=recv_sem,
        device_id=device,
        device_id_type=MESH_IDS,
    )


def partner_id():
    return {"tensor": 1 - lax.axis_index("tensor")}


def gather_kernel(shards, *refs):
    kinds = (len(refs) - 5) // 2
    locals_ = refs[:kinds]
    fulls = refs[kinds : 2 * kinds]
    ring_send, ring_recv, side_send, side_recv, own_sem = refs[2 * kinds :]
    ring = Ring(shards)
    ring.greet(False)

    def ring_copy(step, kind, shard, source):
        return send_to(
            {"dp": ring.following},
            source,
            fulls[kind].at[shard],
            ring_send.at[step, kind],
            ring_recv.at[step, kind],
        )

    def side_copy(step, kind, shard, source):
        return send_to(
            {"dp": ring.sibling},
            source,
            fulls[kind].at[shard],
            side_send.at[step, kind],
            side_recv.at[step, kind],
        )

    for kind in range(kinds):
        ring_copy(0, kind, ring.me, locals_[kind]).start()
        side_copy(0, kind, ring.me, locals_[kind]).start()
        pltpu.make_async_copy(locals_[kind], fulls[kind].at[ring.me], own_sem.at[kind]).start()

    def forward(step, carry):
        shard = ring.behind(step)
        for kind in range(kinds):
            here = fulls[kind].at[shard]
            ring_copy(step - 1, kind, shard, here).wait_recv()

            @pl.when(step < ring.count - 1)
            def _():
                ring_copy(step, kind, shard, here).start()

            side_copy(step, kind, shard, here).start()
        return carry

    lax.fori_loop(1, ring.count, forward, 0)

    def drain(step, carry):
        shard = ring.behind(step)
        for kind in range(kinds):
            here = fulls[kind].at[shard]

            @pl.when(step < ring.count - 1)
            def _():
                ring_copy(step, kind, shard, here).wait_send()

            side_copy(step, kind, shard, here).wait_send()
            side_copy(step, kind, shard, here).wait_recv()
        return carry

    lax.fori_loop(0, ring.count, drain, 0)
    for kind in range(kinds):
        pltpu.make_async_copy(locals_[kind], fulls[kind].at[ring.me], own_sem.at[kind]).wait()


def gather_shards(shards, pieces):
    steps = shards // 2
    return pl.pallas_call(
        functools.partial(gather_kernel, shards),
        out_shape=tuple(
            jax.ShapeDtypeStruct((shards,) + piece.shape, piece.dtype) for piece in pieces
        ),
        in_specs=[VMEM_SPEC] * len(pieces),
        out_specs=(ANY_SPEC,) * len(pieces),
        scratch_shapes=[
            pltpu.SemaphoreType.DMA((steps, len(pieces))),
            pltpu.SemaphoreType.DMA((steps, len(pieces))),
            pltpu.SemaphoreType.DMA((steps, len(pieces))),
            pltpu.SemaphoreType.DMA((steps, len(pieces))),
            pltpu.SemaphoreType.DMA((len(pieces),)),
        ],
        compiler_params=pltpu.CompilerParams(
            collective_id=0, has_side_effects=True, vmem_limit_bytes=VMEM_BYTES
        ),
        name="gather_attention",
    )(*pieces)


def ffn_kernel(shards, groups, *refs):
    (
        x_ref,
        part_ref,
        gain_ref,
        grad_ref,
        gate_ref,
        up_ref,
        down_ref,
        hidden_ref,
        normed_ref,
        act_ref,
        d_gate_ref,
        d_up_ref,
        out_part_ref,
        norm_part_ref,
        norm_other_ref,
    ) = refs[:15]
    count = len(groups)
    full = [refs[15 + 3 * group : 18 + 3 * group] for group in range(count)]
    (
        part_other,
        out_total,
        norm_total,
        ring_send,
        ring_recv,
        side_send,
        side_recv,
        own_sem,
        part_sem,
        norm_send,
        norm_recv,
    ) = refs[15 + 3 * count :]
    shard_refs = (gate_ref, up_ref, down_ref)
    rows = gate_ref.shape[0]
    depth = normed_ref.shape[1]
    blocks = depth // TILE
    ring = Ring(shards)
    ring.greet(True)

    def place(group, kind, shard):
        return full[group][kind].at[pl.ds(pl.multiple_of(shard * rows, rows), rows)]

    def own_part(group, kind):
        low, size = groups[group]
        return shard_refs[kind].at[:, pl.ds(low, size)]

    def ring_copy(group, step, kind, shard, source):
        return send_to(
            {"dp": ring.following},
            source,
            place(group, kind, shard),
            ring_send.at[group, step, kind],
            ring_recv.at[group, step, kind],
        )

    def side_copy(group, step, kind, shard, source):
        return send_to(
            {"dp": ring.sibling},
            source,
            place(group, kind, shard),
            side_send.at[group, step, kind],
            side_recv.at[group, step, kind],
        )

    def own_copy(group, kind):
        return pltpu.make_async_copy(
            own_part(group, kind), place(group, kind, ring.me), own_sem.at[group, kind]
        )

    def begin(group):
        for kind in range(3):
            source = own_part(group, kind)
            ring_copy(group, 0, kind, ring.me, source).start()
            side_copy(group, 0, kind, ring.me, source).start()
            own_copy(group, kind).start()

    def forward(group, step):
        shard = ring.behind(step)
        for kind in range(3):
            here = place(group, kind, shard)
            ring_copy(group, step - 1, kind, shard, here).wait_recv()

            @pl.when(step < ring.count - 1)
            def _():
                ring_copy(group, step, kind, shard, here).start()

            side_copy(group, step, kind, shard, here).start()

    def arrived(group):
        for kind in range(3):
            own_copy(group, kind).wait()

        def one(step, carry):
            for kind in range(3):
                here = place(group, kind, ring.me)
                side_copy(group, step, kind, ring.me, here).wait_recv()
            return carry

        lax.fori_loop(0, ring.count, one, 0)

    def hidden_units(group, tile):
        low, _ = groups[group]
        part = pl.ds(pl.multiple_of(tile * TILE, TILE), TILE)
        target = pl.ds(pl.multiple_of(low + tile * TILE, TILE), TILE)
        gate_pre = matmul(normed_ref[...], full[group][0][:, part])
        up_pre = matmul(normed_ref[...], full[group][1][:, part])
        d_act = matmul(grad_ref[...], full[group][2][:, part])
        sigmoid_gate = jax.nn.sigmoid(gate_pre)
        silu_gate = gate_pre * sigmoid_gate
        act_ref[:, target] = (silu_gate * up_pre).astype(jnp.bfloat16)
        d_gate_ref[:, target] = (
            d_act * up_pre * sigmoid_gate * (1.0 + gate_pre * (1.0 - sigmoid_gate))
        ).astype(jnp.bfloat16)
        d_up_ref[:, target] = (d_act * silu_gate).astype(jnp.bfloat16)

    def norm_terms(group, block):
        low, size = groups[group]
        units = pl.ds(low, size)
        features = pl.ds(pl.multiple_of(block * TILE, TILE), TILE)
        return matmul_nt(d_gate_ref[:, units], full[group][0][features, :]) + matmul_nt(
            d_up_ref[:, units], full[group][1][features, :]
        )

    def out_terms(group, block):
        low, size = groups[group]
        features = pl.ds(pl.multiple_of(block * TILE, TILE), TILE)
        return matmul_nt(act_ref[:, pl.ds(low, size)], full[group][2][features, :])

    def accumulate(group, low_block, high_block):
        def one(block, carry):
            features = pl.ds(pl.multiple_of(block * TILE, TILE), TILE)
            norm_new = norm_terms(group, block)
            out_new = out_terms(group, block)
            if group > 0:
                norm_new += norm_total[:, features]
                out_new += out_total[:, features]
            norm_total[:, features] = norm_new
            out_total[:, features] = out_new
            return carry

        lax.fori_loop(low_block, high_block, one, 0)

    part_copy = send_to(partner_id(), part_ref, part_other, part_sem.at[0], part_sem.at[1])
    part_copy.start()
    begin(0)

    def first_steps(step, carry):
        forward(0, step)
        return carry

    lax.fori_loop(1, ring.count, first_steps, 0)
    begin(1)
    part_copy.wait()

    def norm_rows(block, carry):
        here = pl.ds(pl.multiple_of(block * 32, 32), 32)
        hidden = x_ref[here, :] + (
            part_ref[here, :].astype(jnp.float32) + part_other[here, :].astype(jnp.float32)
        )
        hidden_ref[here, :] = hidden
        _, norm_two = rms_parts(hidden)
        normed_ref[here, :] = (norm_two * gain_ref[...]).astype(jnp.bfloat16)
        return carry

    lax.fori_loop(0, normed_ref.shape[0] // 32, norm_rows, 0)

    for group in range(1, count):
        before = group - 1
        tiles = groups[before][1] // TILE
        if group > 1:
            begin(group)
        arrived(before)

        def step_and_work(step, carry):
            forward(group, step)

            @pl.when(step <= tiles)
            def _():
                hidden_units(before, step - 1)

            for half in range(2):

                @pl.when(step == tiles + 1 + half)
                def _():
                    accumulate(before, half * (blocks // 2), (half + 1) * (blocks // 2))

            return carry

        lax.fori_loop(1, ring.count, step_and_work, 0)

    last = count - 1
    arrived(last)

    def last_units(tile, carry):
        hidden_units(last, tile)
        return carry

    lax.fori_loop(0, groups[last][1] // TILE, last_units, 0)

    def norm_copy(block):
        features = pl.ds(pl.multiple_of(block * TILE, TILE), TILE)
        return send_to(
            partner_id(),
            norm_part_ref.at[:, features],
            norm_other_ref.at[:, features],
            norm_send.at[block],
            norm_recv.at[block],
        )

    def last_norm(block, carry):
        features = pl.ds(pl.multiple_of(block * TILE, TILE), TILE)
        norm_part_ref[:, features] = (norm_total[:, features] + norm_terms(last, block)).astype(
            jnp.bfloat16
        )

        @pl.when(block > 0)
        def _():
            norm_copy(block - 1).start()

        return carry

    lax.fori_loop(0, blocks, last_norm, 0)

    def last_out(block, carry):
        features = pl.ds(pl.multiple_of(block * TILE, TILE), TILE)
        out_part_ref[:, features] = (out_total[:, features] + out_terms(last, block)).astype(
            jnp.bfloat16
        )

        @pl.when(block == 0)
        def _():
            norm_copy(blocks - 1).start()

        return carry

    lax.fori_loop(0, blocks, last_out, 0)

    for group in range(count):

        def drain(step, carry):
            for kind in range(3):
                here = place(group, kind, ring.me)

                @pl.when(step < ring.count - 1)
                def _():
                    ring_copy(group, step, kind, ring.me, here).wait_send()

                side_copy(group, step, kind, ring.me, here).wait_send()
            return carry

        lax.fori_loop(0, ring.count, drain, 0)

    def drain_norm(block, carry):
        norm_copy(block).wait()
        return carry

    lax.fori_loop(0, blocks, drain_norm, 0)


def ffn_groups(units, steps):
    tiles = units // TILE
    last = max(1, min(2, tiles - 2))
    first = min(steps - 3, (tiles - last) // 2)
    sizes = [first, tiles - last - first, last]
    groups = []
    low = 0
    for size in sizes:
        groups.append((low * TILE, size * TILE))
        low += size
    return tuple(groups)


def ffn_pass(shards, x_rows, part, gain, grad_rows, gate_shard, up_shard, down_shard):
    tokens, depth = x_rows.shape
    units = gate_shard.shape[1]
    steps = shards // 2
    groups = ffn_groups(units, steps)
    wide = jax.ShapeDtypeStruct((tokens, depth), jnp.bfloat16)
    inner = jax.ShapeDtypeStruct((tokens, units), jnp.bfloat16)
    full = []
    for _, size in groups:
        full += [pltpu.VMEM((depth, size), jnp.bfloat16)] * 3
    sems = pltpu.SemaphoreType.DMA((len(groups), steps, 3))
    return pl.pallas_call(
        functools.partial(ffn_kernel, shards, groups),
        out_shape=(
            jax.ShapeDtypeStruct((tokens, depth), jnp.float32),
            wide,
            inner,
            inner,
            inner,
            wide,
            wide,
            wide,
        ),
        in_specs=[VMEM_SPEC] * 7,
        out_specs=(VMEM_SPEC,) * 8,
        scratch_shapes=full
        + [
            pltpu.VMEM((tokens, depth), jnp.bfloat16),
            pltpu.VMEM((tokens, depth), jnp.float32),
            pltpu.VMEM((tokens, depth), jnp.float32),
            sems,
            sems,
            sems,
            sems,
            pltpu.SemaphoreType.DMA((len(groups), 3)),
            pltpu.SemaphoreType.DMA((2,)),
            pltpu.SemaphoreType.DMA((depth // TILE,)),
            pltpu.SemaphoreType.DMA((depth // TILE,)),
        ],
        compiler_params=pltpu.CompilerParams(
            collective_id=1, has_side_effects=True, vmem_limit_bytes=VMEM_BYTES
        ),
        name="ffn_ring",
    )(x_rows, part, gain, grad_rows, gate_shard, up_shard, down_shard)


def reduce_kernel(shards, chunks, lefts, rights, *refs):
    left_refs = refs[:lefts]
    right_refs = refs[lefts : lefts + rights]
    at = lefts + rights
    out_part_ref, norm_part_ref, scaled_ref, sums_ref = refs[at : at + 4]
    result_ref, sums_out_ref, out_other_ref, norm_other_ref = refs[at + 4 : at + 8]
    at += 8
    left_all = refs[at : at + lefts]
    right_all = refs[at + lefts : at + lefts + rights]
    (
        turned,
        slots,
        norm_here,
        norm_there,
        sums_own,
        sums_side,
        sums_slots,
        ring_send,
        ring_recv,
        sums_send,
        sums_recv,
        own_sem,
        side_send,
        side_recv,
        part_sem,
        sums_sem,
    ) = refs[at + lefts + rights :]
    ring = Ring(shards)
    ring.greet(True)
    tokens = out_part_ref.shape[0]
    rows = slots.shape[1]
    mine = pl.ds(pl.multiple_of(ring.core * tokens, tokens), tokens)

    out_copy = send_to(partner_id(), out_part_ref, out_other_ref, part_sem.at[0], part_sem.at[1])
    norm_copy = send_to(partner_id(), norm_part_ref, norm_there, part_sem.at[2], part_sem.at[3])
    norm_load = pltpu.make_async_copy(norm_part_ref, norm_here, part_sem.at[4])
    sums_load = pltpu.make_async_copy(sums_ref, sums_own, sums_sem.at[0])

    def left_copies(index):
        source = left_refs[index]
        target = left_all[index].at[:, mine]
        return (
            send_to(
                {"dp": ring.sibling},
                source.at[:, 1 - ring.core],
                target,
                side_send.at[index],
                side_recv.at[index],
            ),
            pltpu.make_async_copy(source.at[:, ring.core], target, own_sem.at[index]),
        )

    def right_copies(index):
        source = right_refs[index]
        target = right_all[index].at[mine]
        return (
            send_to(
                {"dp": ring.sibling},
                source,
                target,
                side_send.at[lefts + index],
                side_recv.at[lefts + index],
            ),
            pltpu.make_async_copy(source, target, own_sem.at[lefts + index]),
        )

    copies = [left_copies(index) for index in range(lefts)] + [
        right_copies(index) for index in range(rights)
    ]
    norm_copy.start()
    norm_load.start()
    sums_load.start()
    for side, own in copies:
        side.start()
        own.start()
    out_copy.start()

    def turn(chip):
        for index in range(lefts):
            block = left_all[index][chip].astype(jnp.float32)
            turned[index] = jnp.transpose(block).astype(jnp.bfloat16)

    def terms(chunk):
        left, right, low, size, _ = chunks[chunk]
        return matmul(turned[left], right_all[right][:, low : low + size])

    def ring_copy(step, chunk):
        _, _, _, size, target = chunks[chunk]
        columns = pl.ds(target, size)
        return send_to(
            {"dp": ring.following},
            slots.at[step, :, columns],
            slots.at[step + 1, :, columns],
            ring_send.at[step, chunk],
            ring_recv.at[step, chunk],
        )

    def sums_copy(step):
        return send_to(
            {"dp": ring.following},
            sums_slots.at[step],
            sums_slots.at[step + 1],
            sums_send.at[step],
            sums_recv.at[step],
        )

    seen = set()
    for index in range(lefts):
        copies[index][0].wait_recv()
        copies[index][1].wait()
    turn(ring.chip(-1))
    for chunk in range(len(chunks)):
        _, right, _, size, target = chunks[chunk]
        if right not in seen:
            seen.add(right)
            copies[lefts + right][0].wait_recv()
            copies[lefts + right][1].wait()
        slots[0, :, target : target + size] = terms(chunk).astype(jnp.bfloat16)
        if chunk > 0:
            ring_copy(0, chunk - 1).start()

    norm_load.wait()
    norm_copy.wait_recv()
    sums_load.wait()
    pieces = sums_own.shape[0]
    width = norm_here.shape[1] // pieces

    def column_sums(low, size):
        columns = slice(low, low + size)
        total = norm_here[:, columns].astype(jnp.float32) + norm_there[:, columns].astype(
            jnp.float32
        )
        return jnp.sum(total * scaled_ref[:, columns], axis=0, keepdims=True)

    band = max(width, 128)
    for low in range(0, pieces * width, band):
        sums = column_sums(low, band)
        for inner in range(0, band, width):
            sums_own[(low + inner) // width, 1:2, 0:width] = sums[:, inner : inner + width]
    ring_copy(0, len(chunks) - 1).start()
    store = pltpu.make_async_copy(norm_there, norm_other_ref, sums_sem.at[1])
    store.start()
    sums_side_copy = send_to(
        {"dp": ring.sibling}, sums_own, sums_side, sums_sem.at[2], sums_sem.at[3]
    )
    sums_side_copy.start()
    sums_side_copy.wait_recv()

    def own_sums(steps):
        shard = ring.device(steps, ring.core)
        return sums_own[shard] + sums_side[shard]

    sums_slots[0] = own_sums(-1)

    def one_step(step, carry):
        turn(ring.chip(-1 - step))
        for chunk in range(len(chunks)):
            _, _, _, size, target = chunks[chunk]
            total = terms(chunk)
            ring_copy(step - 1, chunk).wait_recv()
            total += slots[step, :, target : target + size].astype(jnp.float32)
            slots[step, :, target : target + size] = total.astype(jnp.bfloat16)
            if chunk > 0:
                ring_copy(step, chunk - 1).start()
            else:
                sums_copy(step - 1).start()
        sums_copy(step - 1).wait_recv()
        ring_copy(step, len(chunks) - 1).start()
        sums_slots[step] = sums_slots[step] + own_sums(-1 - step)
        return carry

    lax.fori_loop(1, ring.count - 1, one_step, 0)
    final = ring.count - 1
    turn(ring.chip(0))
    for chunk in range(len(chunks)):
        _, _, _, size, target = chunks[chunk]
        total = terms(chunk)
        if chunk == 0:
            sums_copy(final - 1).start()
        ring_copy(final - 1, chunk).wait_recv()
        result_ref[:, target : target + size] = total + slots[
            final, :, target : target + size
        ].astype(jnp.float32)
    sums_copy(final - 1).wait_recv()
    sums_out_ref[...] = sums_slots[final] + own_sums(0)

    def drain(step, carry):
        for chunk in range(len(chunks)):
            ring_copy(step, chunk).wait_send()
        sums_copy(step).wait_send()
        return carry

    lax.fori_loop(0, final, drain, 0)
    for side, _ in copies:
        side.wait_send()
    sums_side_copy.wait_send()
    store.wait()
    norm_copy.wait_send()
    out_copy.wait()


def reduce_chunks(pairs, right_widths):
    chunks = []
    target = 0
    for left, right in pairs:
        width = right_widths[right]
        low = 0
        while low < width:
            size = min(1024, width - low)
            if width - low - size < 512:
                size = width - low
            chunks.append((left, right, low, size, target))
            low += size
            target += size
    return tuple(chunks), target


def reduce_pass(shards, pairs, lefts, rights, out_part, norm_part, scaled, sums):
    tokens, depth = out_part.shape
    steps = shards // 2
    rows = lefts[0].shape[3]
    chunks, total = reduce_chunks(pairs, [right.shape[1] for right in rights])
    operands = len(lefts) + len(rights)
    sums_shape = sums.shape[1:]
    return pl.pallas_call(
        functools.partial(reduce_kernel, shards, chunks, len(lefts), len(rights)),
        out_shape=(
            jax.ShapeDtypeStruct((rows, total), jnp.float32),
            jax.ShapeDtypeStruct(sums_shape, jnp.float32),
            jax.ShapeDtypeStruct((tokens, depth), jnp.bfloat16),
            jax.ShapeDtypeStruct((tokens, depth), jnp.bfloat16),
        ),
        in_specs=[ANY_SPEC] * operands + [ANY_SPEC, ANY_SPEC, VMEM_SPEC, ANY_SPEC],
        out_specs=(VMEM_SPEC, VMEM_SPEC, ANY_SPEC, ANY_SPEC),
        scratch_shapes=[
            pltpu.VMEM((steps, 2 * tokens, rows), jnp.bfloat16) for _ in lefts
        ]
        + [pltpu.VMEM((2 * tokens, right.shape[1]), jnp.bfloat16) for right in rights]
        + [
            pltpu.VMEM((len(lefts), rows, 2 * tokens), jnp.bfloat16),
            pltpu.VMEM((steps, rows, total), jnp.bfloat16),
            pltpu.VMEM((tokens, depth), jnp.bfloat16),
            pltpu.VMEM((tokens, depth), jnp.bfloat16),
            pltpu.VMEM(sums.shape, jnp.float32),
            pltpu.VMEM(sums.shape, jnp.float32),
            pltpu.VMEM((steps,) + sums_shape, jnp.float32),
            pltpu.SemaphoreType.DMA((steps, len(chunks))),
            pltpu.SemaphoreType.DMA((steps, len(chunks))),
            pltpu.SemaphoreType.DMA((steps,)),
            pltpu.SemaphoreType.DMA((steps,)),
            pltpu.SemaphoreType.DMA((operands,)),
            pltpu.SemaphoreType.DMA((operands,)),
            pltpu.SemaphoreType.DMA((operands,)),
            pltpu.SemaphoreType.DMA((5,)),
            pltpu.SemaphoreType.DMA((4,)),
        ],
        compiler_params=pltpu.CompilerParams(
            collective_id=2, has_side_effects=True, vmem_limit_bytes=VMEM_BYTES
        ),
        name="reduce_ring",
    )(*lefts, *rights, out_part, norm_part, scaled, sums)


def body(
    shards,
    layer_input,
    positions,
    norm1_gain,
    w_q,
    w_k,
    w_v,
    w_o,
    norm2_gain,
    w_gate,
    w_up,
    w_down,
    out_grad,
):
    tokens, depth = layer_input.shape
    rows = w_q.shape[0]
    head_count = w_q.shape[1] // HD
    kv_count = w_k.shape[1] // HD
    query_cols = head_count * HD
    kv_cols = kv_count * HD
    units = w_gate.shape[1]

    qkv_shard = jnp.concatenate([w_q, w_k, w_v], axis=1)
    out_shard = w_o.T
    gains = jnp.stack([norm1_gain, norm2_gain]).astype(jnp.float32)
    gains = jnp.pad(gains, ((0, 6), (0, max(128 - rows, 0))))
    gains_all, qkv_all, out_all = gather_shards(shards, (gains, qkv_shard, out_shard))
    gain_one = gains_all[:, 0, :rows].reshape(1, depth)
    gain_two = gains_all[:, 1, :rows].reshape(1, depth)
    qkv_w = qkv_all.reshape(depth, query_cols + 2 * kv_cols)
    out_w = out_all.reshape(depth, query_cols)

    inv_one, norm_one = rms_parts(layer_input)
    normed_one = (norm_one * gain_one).astype(jnp.bfloat16)
    cos_table, sin_table = rope_tables(positions, HD)
    qkv = matmul(normed_one, qkv_w)
    queries = rotate(
        qkv[:, :query_cols].reshape(tokens, head_count, HD), cos_table, sin_table, 1.0
    ).astype(jnp.bfloat16)
    key_rows = rotate(
        qkv[:, query_cols : query_cols + kv_cols].reshape(tokens, kv_count, HD),
        cos_table,
        sin_table,
        1.0,
    ).astype(jnp.bfloat16)
    value_rows = qkv[:, query_cols + kv_cols :].astype(jnp.bfloat16).reshape(tokens, kv_count, HD)
    seq_count = tokens // L
    query_seq = queries.reshape(seq_count, L, head_count, HD)
    key_seq = key_rows.reshape(seq_count, L, kv_count, HD)
    value_seq = value_rows.reshape(seq_count, L, kv_count, HD)
    attended, log_total = lax.map(
        lambda block_in: attend(block_in[0], block_in[1], block_in[2]),
        (query_seq, key_seq, value_seq),
    )
    attended_rows = attended.reshape(tokens, query_cols)
    part = matmul_nt(attended_rows, out_w).astype(jnp.bfloat16)
    grad_rows = out_grad.astype(jnp.bfloat16)

    (
        hidden,
        normed_two,
        activated,
        d_gate,
        d_up,
        out_part,
        norm_part,
        norm_other,
    ) = ffn_pass(shards, layer_input, part, gain_two, grad_rows, w_gate, w_up, w_down.T)

    inv_two, norm_two = rms_parts(hidden)
    d_norm_two = norm_part.astype(jnp.float32) + norm_other.astype(jnp.float32)
    grad_gain_two = jnp.sum(d_norm_two * norm_two, axis=0)
    e_two = d_norm_two * gain_two
    d_hidden = out_grad + inv_two * (
        e_two - norm_two * jnp.mean(e_two * norm_two, axis=-1, keepdims=True)
    )
    hidden_rows = d_hidden.astype(jnp.bfloat16)
    d_attended = matmul(hidden_rows, out_w).astype(jnp.bfloat16)
    d_query, d_keys, d_values = lax.map(
        lambda block_in: attend_back(
            block_in[0], block_in[1], block_in[2], block_in[3], block_in[4], block_in[5]
        ),
        (
            query_seq,
            key_seq,
            value_seq,
            attended,
            d_attended.reshape(seq_count, L, query_cols),
            log_total,
        ),
    )
    dq_raw = (
        rotate(d_query.reshape(tokens, head_count, HD), cos_table, sin_table, -1.0)
        .astype(jnp.bfloat16)
        .reshape(tokens, query_cols)
    )
    dk_raw = (
        rotate(d_keys.reshape(tokens, kv_count, HD), cos_table, sin_table, -1.0)
        .astype(jnp.bfloat16)
        .reshape(tokens, kv_cols)
    )
    dv_rows = d_values.astype(jnp.bfloat16).reshape(tokens, kv_cols)
    d_qkv = jnp.concatenate([dq_raw, dk_raw, dv_rows], axis=1)
    norm_one_part = matmul_nt(d_qkv, qkv_w).astype(jnp.bfloat16)

    def blocks(row_values):
        return jnp.transpose(
            row_values.reshape(tokens, shards // 2, 2, rows), (1, 2, 0, 3)
        )

    sums = grad_gain_two.reshape(shards, 1, rows)
    sums = jnp.pad(sums, ((0, 0), (0, 7), (0, max(128 - rows, 0))))
    result, sums_out, out_other, norm_one_other = reduce_pass(
        shards,
        ((0, 0), (0, 1), (1, 2), (2, 3), (3, 4)),
        [blocks(normed_two), blocks(grad_rows), blocks(hidden_rows), blocks(normed_one)],
        [d_gate, d_up, activated, attended_rows, d_qkv],
        out_part,
        norm_one_part,
        norm_one,
        sums,
    )

    layer_output = hidden + (out_part.astype(jnp.float32) + out_other.astype(jnp.float32))
    d_norm_one = norm_one_part.astype(jnp.float32) + norm_one_other.astype(jnp.float32)
    e_one = d_norm_one * gain_one
    x_grad = d_hidden + inv_one * (
        e_one - norm_one * jnp.mean(e_one * norm_one, axis=-1, keepdims=True)
    )
    at = 3 * units
    shard_qkv = result[:, at + query_cols :]
    return (
        layer_output,
        x_grad,
        sums_out[1, :rows],
        shard_qkv[:, :query_cols],
        shard_qkv[:, query_cols : query_cols + kv_cols],
        shard_qkv[:, query_cols + kv_cols :],
        result[:, at : at + query_cols].T,
        sums_out[0, :rows],
        result[:, :units],
        result[:, units : 2 * units],
        result[:, 2 * units : 3 * units].T,
    )


def solution(mesh):
    in_specs = (
        P("dp", None),
        P("dp"),
        P("dp"),
        P("dp", "tensor"),
        P("dp", "tensor"),
        P("dp", "tensor"),
        P("tensor", "dp"),
        P("dp"),
        P("dp", "tensor"),
        P("dp", "tensor"),
        P("tensor", "dp"),
        P("dp", None),
    )
    out_specs = (
        P("dp", None),
        P("dp", None),
        P("dp"),
        P("dp", "tensor"),
        P("dp", "tensor"),
        P("dp", "tensor"),
        P("tensor", "dp"),
        P("dp"),
        P("dp", "tensor"),
        P("dp", "tensor"),
        P("tensor", "dp"),
    )
    return jax.shard_map(
        functools.partial(body, mesh.shape["dp"]),
        mesh=mesh,
        in_specs=in_specs,
        out_specs=out_specs,
        check_vma=False,
    )
```

time: 1740 us -> 585 us (0.34)
  waiting for transfers between devices: 1400 us -> 0 us
  Pallas kernels: 0 us -> 488 us
  blocking collectives: 146 us -> 0 us
  matrix products: 131 us -> 23.7 us
  local copies, waits for them, and re-layouts: 13.6 us -> 37.2 us
    reduce_scatter x7 -> x0, waiting for transfers between devices: 963 us -> none  [the longest x1 232 us: body(): lax.psum_scatter(grad_gate, 'dp', scatter_dimension=0, tiled=True)]
    pallas_call x0 -> x3, Pallas kernels: none -> 488 us  [the longest x1 223 us: reduce_pass(): pl.pallas_call(functools.partial(reduce_kernel, shards, chunks, len(lefts...]
    all_gather x5 -> x0, waiting for transfers between devices: 295 us -> none  [the longest x1 91.7 us: body(): lax.all_gather(w_gate, 'dp', axis=0, tiled=True)]
    psum x4 -> x0, waiting for transfers between devices: 141 us -> none  [the longest x1 51.6 us: body(): lax.psum(matmul_nt(d_gate, gate_w) + matmul_nt(d_up, up_w), 'tensor')]
    all_gather x4 -> x0, blocking collectives: 85 us -> none  [the longest x1 23.3 us: body(): lax.all_gather(norm1_gain, 'dp', axis=0, tiled=True)]
    unnamed x1 -> x0, blocking collectives: 61.1 us -> none
    dot_general x7 -> x0, matrix products: 49.9 us -> none  [matmul_tn(): lax.dot_general(left_side, right_side, (((0,), (0,)), ((), ())), preferre...]
    dot_general x7 -> x2, matrix products: 38.7 us -> 2.84 us  [matmul(): return jnp.dot(left_side, right_side, preferred_element_type=jnp.float32)]
  transfers between devices with their start and end apart: 16 -> 0, of which waited for: 14 -> 0; matrix products, arithmetic and copies ran while one was open for 6% -> 0% of each run, Pallas kernels for 0% -> 0%
where the time goes in v1:
time: 585 us; the launch traced here: 576 us
  Pallas kernels  488 us (83%)
  local copies, waits for them, and re-layouts  37.2 us (6%)
  other arithmetic  25.1 us (4%)
  matrix products  23.7 us (4%)
    pallas_call x1, Pallas kernels, reduce_pass(): pl.pallas_call(functools.partial(reduce_kernel, shards, chunks, len(lefts...  223 us
    pallas_call x1, Pallas kernels, ffn_pass(): pl.pallas_call(functools.partial(ffn_kernel, shards, groups), out_shape=(...  210 us
    pallas_call x1, Pallas kernels, gather_shards(): pl.pallas_call(functools.partial(gather_kernel, shards), out_shape=tuple(...  55.4 us
    unnamed x96, local copies, waits for them, and re-layouts  13.6 us

profile of v1, /device:TPU:0, one launch (start us, length us, event | category | flops | bytes accessed | tf_op | source)
XLA Modules:
  0.0 575.8 jit_solution(16003119933191325850)
XLA Ops:
  0.6 1.7 pad_maximum_fusion.5.refs_1_
  2.4 1.8 copy.48
  4.2 1.3 fusion.14.refs_0_
  5.4 55.4 %gather_attention.1 = (f32[16,8,128]{2,1,0:T(8,128)}, bf16[16,128,1280]{2,1,0:T(8,128)(2,1)}, bf16[16,128,1024]{2,1,0:T(8,128)(2,1)}) custom-call(f32[8,128]{1,0:T(8,128)} %fusion.14.refs_0_, bf16[128,1280]{1,0:T(8,128)(2,1)} %pad_maximum_fusion.5.refs_1_, bf16[128,1024]{1,0:T(8,128)(2,1)} %bitcast.118), custom_call_target="tpu_custom_call" | custom-call | tf_op jit(solution)/shard_map/gather_attention/pallas_call | solution.py:225
  60.8 1.6 fusion.24
  62.5 1.8 multiply_reduce_fusion.4
  64.3 1.6 multiply_convert_fusion
  65.9 2.0 copy-done.43
  67.9 1.5 fusion.25
  74.5 3.4 convolution_convert_fusion.3
  78.0 2.3 convolution_convert_fusion.refs_1_
  82.6 209.8 %ffn_ring.1 = (f32[256,2048]{1,0:T(8,128)}, bf16[256,2048]{1,0:T(8,128)(2,1)}, bf16[256,2816]{1,0:T(8,128)(2,1)}, bf16[256,2816]{1,0:T(8,128)(2,1)}, bf16[256,28...) custom-call(f32[256,2048]{1,0:T(8,128)} %refs_0_.1, ...), custom_call_target="tpu_custom_call" | custom-call | tf_op jit(solution)/shard_map/ffn_ring/pallas_call | solution.py:530
  292.4 2.0 multiply_reduce_fusion.3
  294.7 2.5 multiply_reduce_fusion.1
  297.5 2.1 fusion.22
  300.4 1.3 convolution_convert_fusion.2
  302.8 3.8 fusion.2
  308.4 2.0 copy.64
  310.4 1.7 convolution_bitcast_fusion.1
  312.3 3.4 fusion.6
  315.8 5.1 convolution_convert_fusion.1.refs_10_
  324.3 1.3 copy.55
  328.0 1.3 copy.80
  330.0 1.3 copy.57
  331.3 222.9 %reduce_ring.1 = (f32[128,10752]{1,0:T(8,128)}, f32[8,128]{1,0:T(8,128)}, bf16[256,2048]{1,0:T(8,128)(2,1)}, bf16[256,2048]{1,0:T(8,128)(2,1)}) custom-call(bf16[8,2,256,128]{3,2,1,0:T(8,128)(2,1)} %bitcast.109, bf16[8,2,256,128]{3,2,1,0:T(8,128)(2,1)} %bitcast.111, bf16[8,2,256,128]{3,2,1,0:T(8,128)(2,1)} %bitcast.108, bf16[8,2,256,128]{3,2,1,0:T(8,128)(2,1)} %bitcast.110, ...), custom_call_target="tpu_custom_call" | custom-call | tf_op jit(solution)/shard_map/reduce_ring/pallas_call | solution.py:789
  554.3 4.5 slice_bitcast_fusion
  558.7 3.0 copy.69
  561.8 1.9 multiply_reduce_fusion
  564.3 5.1 multiply_add_fusion
  569.5 2.1 slice_bitcast_fusion.1
  572.5 1.5 fusion.23
  574.1 1.3 slice_bitcast_fusion.2
  (130 shorter events, 19.8 us)
Async XLA Ops:
  60.8 3.5 copy-start.3
  62.5 3.5 copy-start.29
  64.3 1.6 copy-start.40
  64.3 3.6 copy-start.43
  65.9 3.6 copy-start.12
  71.4 3.1 copy-start.27
  72.3 2.1 copy-start.9
  74.3 3.6 copy-start.38
  74.5 3.4 copy-start.36
  74.5 3.5 copy-start.44
  77.9 2.3 copy-start.14
  78.0 2.3 copy-start.7
  292.4 2.2 copy-start.1
  292.4 2.2 copy-start.35
  294.6 2.5 copy-start.8
  294.7 2.6 copy-start.10
  294.7 2.8 copy-start.11
  297.5 2.9 copy-start.45
  300.4 1.5 copy-start.15
  302.8 3.8 copy-start.32
  302.8 3.8 copy-start.34
  307.1 3.3 copy-start.21
  312.3 3.5 copy-start.18
  323.8 2.5 copy-start.16
  324.3 3.0 copy-start.13
  327.3 2.0 copy-start.4
  554.2 7.5 %copy-start.5 = (bf16[256,2048]{1,0:T(8,128)(2,1)S(1)}, bf16[256,2048]{1,0:T(8,128)(2,1)}, u32[]{:S(2)}) copy-start(bf16[256,2048]{1,0:T(8,128)(2,1)} %convolution_convert_fusion.1.refs_10_) | copy-start | bytes 3145732
  558.7 3.1 copy-start
  558.7 3.1 copy-start.30
  561.8 1.9 copy-start.2
  561.8 2.5 copy-start.6
  561.8 2.5 copy-start.41
  (14 other events, 13.7 us)

commit v2 on v1

v2 whole, which is shorter than its diff:
```python
import functools
import math

import jax
import jax.numpy as jnp
from jax import lax
from jax.experimental import pallas as pl
from jax.experimental.pallas import tpu as pltpu
from jax.sharding import PartitionSpec as P

HD = 64
L = 256
TILE = 256
VMEM_BYTES = 67043328

epsilon = 1e-05

MESH_IDS = pl.DeviceIdType.MESH
VMEM_SPEC = pl.BlockSpec(memory_space=pltpu.VMEM)
ANY_SPEC = pl.BlockSpec(memory_space=pl.ANY)


def matmul(left_side, right_side):
    return jnp.dot(left_side, right_side, preferred_element_type=jnp.float32)


def matmul_nt(left_side, right_side):
    return lax.dot_general(
        left_side, right_side, (((1,), (1,)), ((), ())), preferred_element_type=jnp.float32
    )


def rms_parts(row_values):
    inv_rms = lax.rsqrt(jnp.mean(row_values * row_values, axis=-1, keepdims=True) + epsilon)
    return (inv_rms, row_values * inv_rms)


def rope_tables(pos_rows, head_dim):
    half_dim = head_dim // 2
    frequency = jnp.exp(
        jnp.arange(half_dim, dtype=jnp.float32) * (-2.0 * math.log(10000.0) / head_dim)
    )
    angles = pos_rows.astype(jnp.float32)[:, None] * frequency[None, :]
    return (jnp.cos(angles), jnp.sin(angles))


def rotate(row_values, cos_table, sin_table, direction_sign):
    half_dim = row_values.shape[-1] // 2
    first_half = row_values[..., :half_dim]
    second = row_values[..., half_dim:]
    cos_part = cos_table[:, None, :]
    sin_part = sin_table[:, None, :] * direction_sign
    return jnp.concatenate(
        [first_half * cos_part - second * sin_part, second * cos_part + first_half * sin_part],
        axis=-1,
    )


def causal_scores(queries, key_rows):
    length, head_count, head_dim = queries.shape
    kv_count = key_rows.shape[1]
    grouped = queries.reshape(length, kv_count, head_count // kv_count, head_dim)
    scores = jnp.einsum(
        "qkgd,pkd->kgqp", grouped, key_rows, preferred_element_type=jnp.float32
    ) * head_dim ** (-0.5)
    future_mask = jnp.arange(length)[None, :] > jnp.arange(length)[:, None]
    return (grouped, jnp.where(future_mask, -jnp.inf, scores))


def attend(queries, key_rows, value_rows):
    grouped, scores = causal_scores(queries, key_rows)
    row_top = jnp.max(scores, axis=-1, keepdims=True)
    log_total = row_top + jnp.log(jnp.sum(jnp.exp(scores - row_top), axis=-1, keepdims=True))
    weights = jnp.exp(scores - log_total).astype(jnp.bfloat16)
    attended = jnp.einsum("kgqp,pkd->qkgd", weights, value_rows, preferred_element_type=jnp.float32)
    return (attended.reshape(queries.shape[0], -1).astype(jnp.bfloat16), log_total)


def attend_back(queries, key_rows, value_rows, attended, d_attended, log_total):
    length, head_count, head_dim = queries.shape
    kv_count = key_rows.shape[1]
    grouped, scores = causal_scores(queries, key_rows)
    prob_rows = jnp.exp(scores - log_total)
    d_grouped = d_attended.reshape(length, kv_count, head_count // kv_count, head_dim)
    out_grouped = attended.reshape(length, kv_count, head_count // kv_count, head_dim)
    row_delta = jnp.sum(out_grouped.astype(jnp.float32) * d_grouped.astype(jnp.float32), axis=-1)
    row_delta = jnp.transpose(row_delta, (1, 2, 0))[..., None]
    d_probs = jnp.einsum(
        "qkgd,pkd->kgqp", d_grouped, value_rows, preferred_element_type=jnp.float32
    )
    d_scores = (prob_rows * (d_probs - row_delta) * head_dim ** (-0.5)).astype(jnp.bfloat16)
    d_query = jnp.einsum("kgqp,pkd->qkgd", d_scores, key_rows, preferred_element_type=jnp.float32)
    d_keys = jnp.einsum("kgqp,qkgd->pkd", d_scores, grouped, preferred_element_type=jnp.float32)
    d_values = jnp.einsum(
        "kgqp,qkgd->pkd",
        prob_rows.astype(jnp.bfloat16),
        d_grouped,
        preferred_element_type=jnp.float32,
    )
    return (d_query.reshape(length, head_count, head_dim), d_keys, d_values)


def chip_at(place, count):
    side = place // (count // 2)
    row = place + side * (count - 1 - 2 * place)
    return 2 * row + side


def place_of(chip, count):
    side = chip % 2
    row = chip // 2
    return row + side * (count - 1 - 2 * row)


def ring_pairs(shards):
    count = shards // 2
    pairs = []
    for shard in range(shards):
        chip, core = divmod(shard, 2)
        place = (place_of(chip, count) + (1 - 2 * core)) % count
        pairs.append((shard, chip_at(place, count) * 2 + core))
    return pairs


class Ring:
    def __init__(self, shards):
        self.shards = shards
        self.count = shards // 2
        self.me = lax.axis_index("dp")
        self.core = self.me % 2
        self.place = place_of(self.me // 2, self.count)
        self.sign = 1 - 2 * self.core
        self.following = self.device(1, self.core)
        self.previous = self.device(-1, self.core)
        self.sibling = self.device(0, 1 - self.core)

    def chip(self, steps):
        place = (self.place + self.sign * steps + 2 * self.count) % self.count
        return chip_at(place, self.count)

    def device(self, steps, core):
        return self.chip(steps) * 2 + core

    def behind(self, steps):
        return self.device(-steps, self.core)

    def greet(self, partner=False, everyone=False):
        barrier = pltpu.get_barrier_semaphore()

        def signal(device):
            pl.semaphore_signal(barrier, inc=1, device_id=device, device_id_type=MESH_IDS)

        if everyone:

            def one(offset, carry):
                signal({"dp": (self.me + offset) % self.shards})
                return carry

            lax.fori_loop(1, self.shards, one, 0)
            expected = self.shards - 1
        else:
            for other in (self.following, self.previous, self.sibling):
                signal({"dp": other})
            expected = 3
        if partner:
            signal(partner_id())
            expected += 1
        pl.semaphore_wait(barrier, expected)


def send_to(device, source, target, send_sem, recv_sem):
    return pltpu.make_async_remote_copy(
        src_ref=source,
        dst_ref=target,
        send_sem=send_sem,
        recv_sem=recv_sem,
        device_id=device,
        device_id_type=MESH_IDS,
    )


def partner_id():
    return {"tensor": 1 - lax.axis_index("tensor")}


def turn_block(source, target):
    target[...] = jnp.transpose(source[...].astype(jnp.float32)).astype(target.dtype)


def turn_rows(source, target):
    def one(block, carry):
        here = pl.ds(pl.multiple_of(block * TILE, TILE), TILE)
        target[:, here] = jnp.transpose(source[here, :].astype(jnp.float32)).astype(target.dtype)
        return carry

    lax.fori_loop(0, source.shape[0] // TILE, one, 0)


def gather_kernel(shards, *refs):
    (
        gains_ref,
        q_ref,
        k_ref,
        v_ref,
        out_ref,
        down_ref,
        gains_all,
        qkv_all,
        out_all,
        down_turned,
        qkv_own,
        out_load,
        out_own,
        down_load,
        ring_send,
        ring_recv,
        side_send,
        side_recv,
        own_sem,
        load_sem,
    ) = refs
    fulls = (qkv_all, out_all, gains_all)
    locals_ = (qkv_own, out_own, gains_ref)
    kinds = len(fulls)
    ring = Ring(shards)

    loads = []
    low = 0
    for index, ref in enumerate((q_ref, k_ref, v_ref)):
        size = ref.shape[1]
        loads.append(
            pltpu.make_async_copy(ref, qkv_own.at[:, pl.ds(low, size)], load_sem.at[index])
        )
        low += size
    loads.append(pltpu.make_async_copy(out_ref, out_load, load_sem.at[3]))
    loads.append(pltpu.make_async_copy(down_ref, down_load, load_sem.at[4]))
    for load in loads:
        load.start()
    ring.greet()

    def ring_copy(step, kind, shard, source):
        return send_to(
            {"dp": ring.following},
            source,
            fulls[kind].at[shard],
            ring_send.at[step, kind],
            ring_recv.at[step, kind],
        )

    def side_copy(step, kind, shard, source):
        return send_to(
            {"dp": ring.sibling},
            source,
            fulls[kind].at[shard],
            side_send.at[step, kind],
            side_recv.at[step, kind],
        )

    def own_copy(kind):
        return pltpu.make_async_copy(locals_[kind], fulls[kind].at[ring.me], own_sem.at[kind])

    def begin(kind):
        ring_copy(0, kind, ring.me, locals_[kind]).start()
        side_copy(0, kind, ring.me, locals_[kind]).start()
        own_copy(kind).start()

    for load in loads[:3]:
        load.wait()
    begin(0)
    loads[3].wait()
    turn_rows(out_load, out_own)
    begin(2)
    begin(1)
    loads[4].wait()
    turn_rows(down_load, down_turned)

    def forward(step, carry):
        shard = ring.behind(step)
        for kind in (0, 2, 1):
            here = fulls[kind].at[shard]
            ring_copy(step - 1, kind, shard, here).wait_recv()

            @pl.when(step < ring.count - 1)
            def _():
                ring_copy(step, kind, shard, here).start()

            side_copy(step, kind, shard, here).start()
        return carry

    lax.fori_loop(1, ring.count, forward, 0)

    def drain(step, carry):
        shard = ring.behind(step)
        for kind in range(kinds):
            here = fulls[kind].at[shard]

            @pl.when(step < ring.count - 1)
            def _():
                ring_copy(step, kind, shard, here).wait_send()

            side_copy(step, kind, shard, here).wait_send()
            side_copy(step, kind, shard, here).wait_recv()
        return carry

    lax.fori_loop(0, ring.count, drain, 0)
    for kind in range(kinds):
        own_copy(kind).wait()


def gather_shards(shards, gains, w_q, w_k, w_v, w_o, w_down):
    steps = shards // 2
    rows = w_q.shape[0]
    columns = w_q.shape[1] + w_k.shape[1] + w_v.shape[1]
    sems = pltpu.SemaphoreType.DMA((steps, 3))
    half = jnp.bfloat16
    return pl.pallas_call(
        functools.partial(gather_kernel, shards),
        out_shape=(
            jax.ShapeDtypeStruct((shards,) + gains.shape, gains.dtype),
            jax.ShapeDtypeStruct((shards, rows, columns), half),
            jax.ShapeDtypeStruct((shards, rows, w_o.shape[0]), half),
            jax.ShapeDtypeStruct((rows, w_down.shape[0]), half),
        ),
        in_specs=[VMEM_SPEC] + [ANY_SPEC] * 5,
        out_specs=(ANY_SPEC,) * 3 + (VMEM_SPEC,),
        scratch_shapes=[
            pltpu.VMEM((rows, columns), half),
            pltpu.VMEM(w_o.shape, half),
            pltpu.VMEM((rows, w_o.shape[0]), half),
            pltpu.VMEM(w_down.shape, half),
            sems,
            sems,
            sems,
            sems,
            pltpu.SemaphoreType.DMA((3,)),
            pltpu.SemaphoreType.DMA((5,)),
        ],
        compiler_params=pltpu.CompilerParams(
            collective_id=0, has_side_effects=True, vmem_limit_bytes=VMEM_BYTES
        ),
        name="gather_attention",
    )(gains, w_q, w_k, w_v, w_o, w_down)


def turn_left(ring, left_all, turned, index, chip):
    rows = left_all.shape[1] // ring.shards
    first = (2 * chip + ring.core) * rows
    base = pl.multiple_of(first // 128 * 128, 128)
    block = left_all[:, pl.ds(base, 128)].astype(jnp.float32)
    turned[index] = jnp.transpose(block).astype(jnp.bfloat16)


def chunk_terms(ring, turned, index, right_all, low, size, chip, rows):
    if rows % 128 == 0:
        left = turned[index]
    else:
        first = (2 * chip + ring.core) * rows % 128
        left = turned[index, pl.ds(pl.multiple_of(first, rows), rows), :]
    return matmul(left, right_all[:, low : low + size])


def cut_columns(pairs, widths):
    chunks = []
    target = 0
    for left, right in pairs:
        width = widths[right]
        low = 0
        while low < width:
            size = min(1024, width - low)
            if width - low - size < 512:
                size = width - low
            chunks.append((left, right, low, size, target))
            low += size
            target += size
    return tuple(chunks), target


FFN_PAIRS = ((1, 2), (0, 0), (0, 1))
HEAD_PAIRS = ((2, 3), (3, 4))


def ffn_kernel(shards, groups, chunks, *refs):
    (
        x_ref,
        part_ref,
        gain_ref,
        grad_ref,
        gate_ref,
        up_ref,
        down_ref,
        gate_behind,
        up_behind,
        down_behind,
        hidden_ref,
        norm_part_ref,
        norm_other_ref,
        out_part_ref,
        carry_ref,
        normed_out,
        grad_out,
        d_gate_out,
        d_up_out,
        act_out,
    ) = refs[:20]
    count = len(groups)
    full = [refs[20 + 3 * group : 23 + 3 * group] for group in range(count)]
    (
        part_other,
        out_total,
        norm_total,
        normed_all,
        grad_all,
        d_gate_all,
        d_up_all,
        act_all,
        turned,
        ring_send,
        ring_recv,
        side_send,
        side_recv,
        own_sem,
        part_sem,
        norm_send,
        norm_recv,
        left_sem,
        right_send,
        right_recv,
        sum_send,
        sum_recv,
        store_sem,
        free_sem,
    ) = refs[20 + 3 * count :]
    shard_refs = (gate_ref, up_ref, down_ref)
    behind_refs = (gate_behind, up_behind, down_behind)
    tokens = part_ref.shape[0]
    rows = gate_ref.shape[0]
    depth = normed_all.shape[1]
    blocks = depth // TILE
    ring = Ring(shards)
    mine = pl.ds(pl.multiple_of(ring.core * tokens, tokens), tokens)

    x_load = pltpu.make_async_copy(x_ref, hidden_ref, part_sem.at[2])
    grad_load = pltpu.make_async_copy(grad_ref, grad_all.at[mine], part_sem.at[3])
    x_load.start()
    grad_load.start()
    ring.greet(partner=True)

    def place(group, kind, shard):
        return full[group][kind].at[pl.ds(pl.multiple_of(shard * rows, rows), rows)]

    def cut(ref, group):
        low, size = groups[group]
        return ref.at[:, pl.ds(low, size)]

    def ring_copy(group, step, kind, shard, source):
        return send_to(
            {"dp": ring.following},
            source,
            place(group, kind, shard),
            ring_send.at[group, step, kind],
            ring_recv.at[group, step, kind],
        )

    def side_copy(group, step, kind, shard, source):
        return send_to(
            {"dp": ring.sibling},
            source,
            place(group, kind, shard),
            side_send.at[group, step, kind],
            side_recv.at[group, step, kind],
        )

    def own_copies(group, kind):
        return (
            pltpu.make_async_copy(
                cut(shard_refs[kind], group),
                place(group, kind, ring.me),
                own_sem.at[group, kind, 0],
            ),
            pltpu.make_async_copy(
                cut(behind_refs[kind], group),
                place(group, kind, ring.behind(1)),
                own_sem.at[group, kind, 1],
            ),
        )

    def begin(group):
        for kind in range(3):
            source = cut(behind_refs[kind], group)
            ring_copy(group, 1, kind, ring.behind(1), source).start()
            side_copy(group, 1, kind, ring.behind(1), source).start()
            side_copy(group, 0, kind, ring.me, cut(shard_refs[kind], group)).start()
            for copy in own_copies(group, kind):
                copy.start()

    def forward(group, step):
        shard = ring.behind(step)
        for kind in range(3):
            here = place(group, kind, shard)
            ring_copy(group, step - 1, kind, shard, here).wait_recv()

            @pl.when(step < ring.count - 1)
            def _():
                ring_copy(group, step, kind, shard, here).start()

            side_copy(group, step, kind, shard, here).start()

    def arrived(group):
        for kind in range(3):
            for copy in own_copies(group, kind):
                copy.wait()

        def one(step, carry):
            for kind in range(3):
                here = place(group, kind, ring.me)
                side_copy(group, step, kind, ring.me, here).wait_recv()
            return carry

        lax.fori_loop(0, ring.count, one, 0)

    def drain(group):
        def one(step, carry):
            for kind in range(3):
                here = place(group, kind, ring.me)

                @pl.when((step > 0) & (step < ring.count - 1))
                def _():
                    ring_copy(group, step, kind, ring.me, here).wait_send()

                side_copy(group, step, kind, ring.me, here).wait_send()
            return carry

        lax.fori_loop(0, ring.count, one, 0)

    lefts = (normed_all, grad_all)
    rights = (d_gate_all, d_up_all, act_all)

    def left_copy(index):
        here = lefts[index].at[mine]
        return send_to(
            {"dp": ring.sibling}, here, here, left_sem.at[0, index], left_sem.at[1, index]
        )

    def right_copy(group, index):
        low, size = groups[group]
        here = rights[index].at[mine, pl.ds(low, size)]
        return send_to(
            {"dp": ring.sibling},
            here,
            here,
            right_send.at[group, index],
            right_recv.at[group, index],
        )

    def hidden_units(group, tile):
        low, _ = groups[group]
        part = pl.ds(pl.multiple_of(tile * TILE, TILE), TILE)
        target = pl.ds(pl.multiple_of(low + tile * TILE, TILE), TILE)
        gate_pre = matmul(normed_all[mine, :], full[group][0][:, part])
        up_pre = matmul(normed_all[mine, :], full[group][1][:, part])
        d_act = matmul(grad_all[mine, :], full[group][2][:, part])
        sigmoid_gate = jax.nn.sigmoid(gate_pre)
        silu_gate = gate_pre * sigmoid_gate
        act_all[mine, target] = (silu_gate * up_pre).astype(jnp.bfloat16)
        d_gate_all[mine, target] = (
            d_act * up_pre * sigmoid_gate * (1.0 + gate_pre * (1.0 - sigmoid_gate))
        ).astype(jnp.bfloat16)
        d_up_all[mine, target] = (d_act * silu_gate).astype(jnp.bfloat16)

    def norm_terms(group, block):
        low, size = groups[group]
        units = pl.ds(low, size)
        features = pl.ds(pl.multiple_of(block * TILE, TILE), TILE)
        return matmul_nt(d_gate_all[mine, units], full[group][0][features, :]) + matmul_nt(
            d_up_all[mine, units], full[group][1][features, :]
        )

    def out_terms(group, block):
        low, size = groups[group]
        features = pl.ds(pl.multiple_of(block * TILE, TILE), TILE)
        return matmul_nt(act_all[mine, pl.ds(low, size)], full[group][2][features, :])

    def accumulate(group, low_block, high_block):
        def one(block, carry):
            features = pl.ds(pl.multiple_of(block * TILE, TILE), TILE)
            norm_new = norm_terms(group, block)
            out_new = out_terms(group, block)
            if group > 0:
                norm_new += norm_total[:, features]
                out_new += out_total[:, features]
            norm_total[:, features] = norm_new
            out_total[:, features] = out_new
            return carry

        lax.fori_loop(low_block, high_block, one, 0)

    part_copy = send_to(partner_id(), part_ref, part_other, part_sem.at[0], part_sem.at[1])
    part_copy.start()
    begin(0)
    grad_load.wait()
    left_copy(1).start()

    def first_steps(step, carry):
        forward(0, step)
        return carry

    lax.fori_loop(2, ring.count, first_steps, 0)
    begin(1)
    x_load.wait()
    part_copy.wait()

    def norm_rows(block, carry):
        here = pl.ds(pl.multiple_of(block * 32, 32), 32)
        there = pl.ds(pl.multiple_of(ring.core * tokens + block * 32, 32), 32)
        hidden = hidden_ref[here, :] + (
            part_ref[here, :].astype(jnp.float32) + part_other[here, :].astype(jnp.float32)
        )
        hidden_ref[here, :] = hidden
        _, norm_two = rms_parts(hidden)
        normed_all[there, :] = (norm_two * gain_ref[...]).astype(jnp.bfloat16)
        return carry

    lax.fori_loop(0, tokens // 32, norm_rows, 0)

    for group in range(1, count):
        before = group - 1
        tiles = groups[before][1] // TILE
        if group > 1:
            begin(group)
        arrived(before)

        def step_and_work(step, carry):
            forward(group, step)
            work = step - 2

            @pl.when(work < tiles)
            def _():
                hidden_units(before, work)

            if group == 1:

                @pl.when(work == 0)
                def _():
                    left_copy(0).start()

            for half in range(2):

                @pl.when(work == tiles + half)
                def _():
                    if half == 0:
                        for index in range(3):
                            right_copy(before, index).start()
                    accumulate(before, half * (blocks // 2), (half + 1) * (blocks // 2))

            return carry

        lax.fori_loop(2, ring.count, step_and_work, 0)
        if tiles + 1 > ring.count - 3:
            accumulate(before, blocks // 2, blocks)
        if group == 1:
            drain(0)
            pl.semaphore_signal(
                free_sem, inc=1, device_id={"dp": ring.previous}, device_id_type=MESH_IDS
            )

    last = count - 1
    arrived(last)

    def last_units(tile, carry):
        hidden_units(last, tile)
        return carry

    lax.fori_loop(0, groups[last][1] // TILE, last_units, 0)

    def norm_copy(block):
        features = pl.ds(pl.multiple_of(block * TILE, TILE), TILE)
        return send_to(
            partner_id(),
            norm_part_ref.at[:, features],
            norm_other_ref.at[:, features],
            norm_send.at[block],
            norm_recv.at[block],
        )

    def last_norm(block, carry):
        features = pl.ds(pl.multiple_of(block * TILE, TILE), TILE)
        norm_part_ref[:, features] = (norm_total[:, features] + norm_terms(last, block)).astype(
            jnp.bfloat16
        )

        @pl.when(block > 0)
        def _():
            norm_copy(block - 1).start()

        if True:

            @pl.when(block == 0)
            def _():
                for index in range(3):
                    right_copy(last, index).start()

        return carry

    lax.fori_loop(0, blocks, last_norm, 0)

    def last_out(block, carry):
        features = pl.ds(pl.multiple_of(block * TILE, TILE), TILE)
        out_part_ref[:, features] = (out_total[:, features] + out_terms(last, block)).astype(
            jnp.bfloat16
        )

        @pl.when(block == 0)
        def _():
            norm_copy(blocks - 1).start()

        return carry

    lax.fori_loop(0, blocks, last_out, 0)

    for index in range(2):
        left_copy(index).wait_recv()
    for group in range(count):
        for index in range(3):
            right_copy(group, index).wait_recv()
    outs = (normed_out, grad_out, d_gate_out, d_up_out, act_out)
    stores = [
        pltpu.make_async_copy(source, target, store_sem.at[index])
        for index, (source, target) in enumerate(zip(lefts + rights, outs))
    ]
    for store in stores:
        store.start()

    def sum_slot(kind, chunk):
        _, _, _, size, _ = chunks[chunk]
        return full[0][kind].at[pl.ds(chunk * rows, rows), pl.ds(0, size)]

    def sum_copy(chunk):
        return send_to(
            {"dp": ring.following},
            sum_slot(0, chunk),
            sum_slot(1, chunk),
            sum_send.at[chunk],
            sum_recv.at[chunk],
        )

    def terms(chunk, chip):
        left, right, low, size, _ = chunks[chunk]
        return chunk_terms(ring, turned, left, rights[right], low, size, chip, rows)

    chip = ring.chip(-1)
    for index in range(2):
        turn_left(ring, lefts[index], turned, index, chip)
    pl.semaphore_wait(free_sem, 1)
    for chunk in range(len(chunks)):
        size = chunks[chunk][3]
        full[0][0][chunk * rows : (chunk + 1) * rows, 0:size] = terms(chunk, chip).astype(
            jnp.bfloat16
        )
        if chunk > 0:
            sum_copy(chunk - 1).start()
    chip = ring.chip(-2)
    for index in range(2):
        turn_left(ring, lefts[index], turned, index, chip)
    sum_copy(len(chunks) - 1).start()
    for chunk in range(len(chunks)):
        _, _, _, size, target = chunks[chunk]
        total = terms(chunk, chip)
        sum_copy(chunk).wait_recv()
        total += full[0][1][chunk * rows : (chunk + 1) * rows, 0:size].astype(jnp.float32)
        carry_ref[:, target : target + size] = total.astype(jnp.bfloat16)

    for group in range(1, count):
        drain(group)
    for index in range(2):
        left_copy(index).wait_send()
    for group in range(count):
        for index in range(3):
            right_copy(group, index).wait_send()
    for chunk in range(len(chunks)):
        sum_copy(chunk).wait_send()
    for store in stores:
        store.wait()

    def drain_norm(block, carry):
        norm_copy(block).wait()
        return carry

    lax.fori_loop(0, blocks, drain_norm, 0)


def ffn_groups(units, steps):
    tiles = units // TILE
    last = max(1, min(2, tiles - 2))
    first = min(max(1, steps - 4), (tiles - last) // 2)
    sizes = [first, tiles - last - first, last]
    groups = []
    low = 0
    for size in sizes:
        groups.append((low * TILE, size * TILE))
        low += size
    return tuple(groups)


def ffn_pass(shards, x_rows, part, gain, grad_rows, own, behind):
    tokens, depth = x_rows.shape
    rows, units = own[0].shape
    steps = shards // 2
    groups = ffn_groups(units, steps)
    chunks, total = cut_columns(FFN_PAIRS, (units,) * 3)
    half = jnp.bfloat16
    wide = jax.ShapeDtypeStruct((tokens, depth), half)
    both_wide = jax.ShapeDtypeStruct((2 * tokens, depth), half)
    both_inner = jax.ShapeDtypeStruct((2 * tokens, units), half)
    full = []
    for _, size in groups:
        full += [pltpu.VMEM((depth, size), half)] * 3
    sems = pltpu.SemaphoreType.DMA((len(groups), steps, 3))
    block_sems = pltpu.SemaphoreType.DMA((depth // TILE,))
    pair_sems = pltpu.SemaphoreType.DMA((len(groups), 3))
    chunk_sems = pltpu.SemaphoreType.DMA((len(chunks),))
    return pl.pallas_call(
        functools.partial(ffn_kernel, shards, groups, chunks),
        out_shape=(
            jax.ShapeDtypeStruct((tokens, depth), jnp.float32),
            wide,
            wide,
            wide,
            jax.ShapeDtypeStruct((rows, total), half),
            both_wide,
            both_wide,
            both_inner,
            both_inner,
            both_inner,
        ),
        in_specs=[ANY_SPEC, VMEM_SPEC, VMEM_SPEC] + [ANY_SPEC] * 7,
        out_specs=(VMEM_SPEC,) * 5 + (ANY_SPEC,) * 5,
        scratch_shapes=full
        + [
            pltpu.VMEM((tokens, depth), half),
            pltpu.VMEM((tokens, depth), jnp.float32),
            pltpu.VMEM((tokens, depth), jnp.float32),
            pltpu.VMEM((2 * tokens, depth), half),
            pltpu.VMEM((2 * tokens, depth), half),
            pltpu.VMEM((2 * tokens, units), half),
            pltpu.VMEM((2 * tokens, units), half),
            pltpu.VMEM((2 * tokens, units), half),
            pltpu.VMEM((2, 128, 2 * tokens), half),
            sems,
            sems,
            sems,
            sems,
            pltpu.SemaphoreType.DMA((len(groups), 3, 2)),
            pltpu.SemaphoreType.DMA((4,)),
            block_sems,
            block_sems,
            pltpu.SemaphoreType.DMA((2, 2)),
            pair_sems,
            pair_sems,
            chunk_sems,
            chunk_sems,
            pltpu.SemaphoreType.DMA((5,)),
            pltpu.SemaphoreType.REGULAR,
        ],
        compiler_params=pltpu.CompilerParams(
            collective_id=1, has_side_effects=True, vmem_limit_bytes=VMEM_BYTES
        ),
        name="ffn_ring",
    )(x_rows, part, gain, grad_rows, *own, *behind)


def reduce_kernel(shards, ffn_chunks, head_chunks, *refs):
    (
        normed_two_ref,
        grad_ref,
        hidden_rows_ref,
        normed_one_ref,
        d_gate_ref,
        d_up_ref,
        act_ref,
        attended_ref,
        d_qkv_ref,
        carry_ref,
        out_part_ref,
        norm_part_ref,
        hidden_ref,
        d_hidden_ref,
        scaled_ref,
        inv_ref,
        gain_ref,
        sums_ref,
        layer_out,
        x_grad_out,
        gate_grad,
        up_grad,
        down_grad,
        o_grad,
        qkv_grad,
        sums_out,
        normed_two_all,
        grad_all,
        hidden_rows_all,
        normed_one_all,
        d_gate_all,
        d_up_all,
        act_all,
        attended_all,
        d_qkv_all,
        turned,
        ffn_slots,
        head_slots,
        norm_here,
        norm_there,
        out_here,
        out_there,
        hidden_buf,
        d_hidden_buf,
        scaled_buf,
        column_total,
        sums_own,
        sums_in,
        ffn_send,
        ffn_recv,
        head_send,
        head_recv,
        load_sem,
        side_send,
        side_recv,
        part_sem,
        row_sem,
        sums_send,
        sums_recv,
    ) = refs
    ring = Ring(shards)
    tokens, depth = out_part_ref.shape
    rows = head_slots.shape[1]
    mine = pl.ds(pl.multiple_of(ring.core * tokens, tokens), tokens)
    lefts = (normed_two_all, grad_all, hidden_rows_all, normed_one_all)
    rights = (d_gate_all, d_up_all, act_all, attended_all, d_qkv_all)

    head_pairs = (
        (hidden_rows_ref, hidden_rows_all),
        (attended_ref, attended_all),
        (normed_one_ref, normed_one_all),
        (d_qkv_ref, d_qkv_all),
    )
    head_loads = [
        pltpu.make_async_copy(source, target.at[mine], load_sem.at[index])
        for index, (source, target) in enumerate(head_pairs)
    ]
    ffn_loads = [
        pltpu.make_async_copy(source, target, load_sem.at[4 + index])
        for index, (source, target) in enumerate(
            (
                (carry_ref, ffn_slots.at[0]),
                (grad_ref, grad_all),
                (act_ref, act_all),
                (normed_two_ref, normed_two_all),
                (d_gate_ref, d_gate_all),
                (d_up_ref, d_up_all),
            )
        )
    ]
    row_loads = [
        pltpu.make_async_copy(source, target, row_sem.at[index])
        for index, (source, target) in enumerate(
            (
                (norm_part_ref, norm_here),
                (d_hidden_ref, d_hidden_buf),
                (scaled_ref, scaled_buf),
                (out_part_ref, out_here),
                (hidden_ref, hidden_buf),
            )
        )
    ]
    for load in head_loads + ffn_loads + row_loads:
        load.start()
    ring.greet(partner=True, everyone=True)
    sides = [
        send_to(
            {"dp": ring.sibling}, source, target.at[mine], side_send.at[index], side_recv.at[index]
        )
        for index, (source, target) in enumerate(head_pairs)
    ]
    for side in sides:
        side.start()
    norm_copy = send_to(partner_id(), norm_part_ref, norm_there, part_sem.at[0], part_sem.at[1])
    out_copy = send_to(partner_id(), out_part_ref, out_there, part_sem.at[2], part_sem.at[3])
    norm_copy.start()
    out_copy.start()

    def ffn_copy(step, chunk):
        _, _, _, size, target = ffn_chunks[chunk]
        columns = pl.ds(target, size)
        return send_to(
            {"dp": ring.following},
            ffn_slots.at[step - 2, :, columns],
            ffn_slots.at[step - 1, :, columns],
            ffn_send.at[step - 2, chunk],
            ffn_recv.at[step - 2, chunk],
        )

    def head_copy(step, chunk):
        _, _, _, size, target = head_chunks[chunk]
        columns = pl.ds(target, size)
        return send_to(
            {"dp": ring.following},
            head_slots.at[step, :, columns],
            head_slots.at[step + 1, :, columns],
            head_send.at[step, chunk],
            head_recv.at[step, chunk],
        )

    def head_terms(chunk, chip):
        left, right, low, size, _ = head_chunks[chunk]
        return chunk_terms(ring, turned, left, rights[right], low, size, chip, rows)

    def ffn_terms(chunk, chip):
        left, right, low, size, _ = ffn_chunks[chunk]
        return chunk_terms(ring, turned, left, rights[right], low, size, chip, rows)

    def turn(chip, indices):
        for index in indices:
            turn_left(ring, lefts[index], turned, index, chip)

    def sums_copy(offset):
        return send_to(
            {"dp": (ring.me + offset) % shards},
            sums_own.at[(ring.me + offset) % shards],
            sums_in.at[ring.me],
            sums_send.at[offset],
            sums_recv.at[offset],
        )

    def finish_input_grad():
        for load in row_loads[:3]:
            load.wait()
        norm_copy.wait()
        sums_own[...] = sums_ref[...]
        column_total[...] = jnp.zeros_like(column_total)

        def one(block, carry):
            here = pl.ds(pl.multiple_of(block * 16, 16), 16)
            total = norm_here[here, :].astype(jnp.float32) + norm_there[here, :].astype(
                jnp.float32
            )
            scaled = scaled_buf[here, :]
            product = total * scaled
            column_total[...] += product[0:8] + product[8:16]
            scaled_gain = total * gain_ref[...]
            mean = jnp.mean(scaled_gain * scaled, axis=-1, keepdims=True)
            d_hidden_buf[here, :] = d_hidden_buf[here, :] + inv_ref[here, :] * (
                scaled_gain - scaled * mean
            )
            return carry

        lax.fori_loop(0, tokens // 16, one, 0)
        width = depth // shards
        band = max(width, 128)
        for low in range(0, depth, band):
            sums = jnp.sum(column_total[:, low : low + band], axis=0, keepdims=True)
            for inner in range(0, band, width):
                sums_own[(low + inner) // width, 1:2, 0:width] = sums[:, inner : inner + width]

    def send_sums():
        pltpu.make_async_copy(d_hidden_buf, x_grad_out, row_sem.at[5]).start()

        def one(offset, carry):
            sums_copy(offset).start()
            return carry

        lax.fori_loop(1, shards, one, 0)

    def finish_output():
        for load in row_loads[3:]:
            load.wait()
        out_copy.wait()

        def one(block, carry):
            here = pl.ds(pl.multiple_of(block * 16, 16), 16)
            hidden_buf[here, :] = hidden_buf[here, :] + (
                out_here[here, :].astype(jnp.float32) + out_there[here, :].astype(jnp.float32)
            )
            return carry

        lax.fori_loop(0, tokens // 16, one, 0)

    heads = len(head_chunks)
    ffns = len(ffn_chunks)

    def head_step(step, chip, chunk):
        _, _, _, size, target = head_chunks[chunk]
        total = head_terms(chunk, chip)
        head_copy(step - 1, chunk).wait_recv()
        return total + head_slots[step, :, target : target + size].astype(jnp.float32)

    def ffn_step(step, chip, chunk, peeled):
        _, _, _, size, target = ffn_chunks[chunk]
        total = ffn_terms(chunk, chip)
        if peeled:
            ffn_copy(step - 1, chunk).wait_recv()
        else:

            @pl.when(step > 2)
            def _():
                ffn_copy(step - 1, chunk).wait_recv()

        return total + ffn_slots[step - 2, :, target : target + size].astype(jnp.float32)

    def store_head(step, chunk, total):
        _, _, _, size, target = head_chunks[chunk]
        head_slots[step, :, target : target + size] = total.astype(jnp.bfloat16)

    def store_ffn(step, chunk, total):
        _, _, _, size, target = ffn_chunks[chunk]
        ffn_slots[step - 2, :, target : target + size] = total.astype(jnp.bfloat16)

    for load in head_loads:
        load.wait()
    for side in sides:
        side.wait_recv()
    chip = ring.chip(-1)
    turn(chip, (2, 3))
    for chunk in range(heads):
        store_head(0, chunk, head_terms(chunk, chip))
        if chunk > 0:
            head_copy(0, chunk - 1).start()
    for load in ffn_loads:
        load.wait()

    def one_step(index, carry):
        ffn_at = index + 2
        head_at = index + 1
        ffn_chip = ring.chip(-1 - ffn_at)
        head_chip = ring.chip(-1 - head_at)
        turn(ffn_chip, (0, 1))
        head_copy(head_at - 1, heads - 1).start()
        turn(head_chip, (2, 3))
        for chunk in range(ffns):
            store_ffn(ffn_at, chunk, ffn_step(ffn_at, ffn_chip, chunk, False))
            if chunk > 0:
                ffn_copy(ffn_at, chunk - 1).start()
        for chunk in range(heads):
            store_head(head_at, chunk, head_step(head_at, head_chip, chunk))
            if chunk > 0:
                head_copy(head_at, chunk - 1).start()
            else:
                ffn_copy(ffn_at, ffns - 1).start()

        @pl.when(index == 1)
        def _():
            finish_input_grad()

        @pl.when(index == 2)
        def _():
            send_sums()
            finish_output()

        @pl.when(index == 3)
        def _():
            pltpu.make_async_copy(hidden_buf, layer_out, row_sem.at[6]).start()

        return carry

    final = ring.count - 1
    lax.fori_loop(0, ring.count - 3, one_step, 0)
    before = ring.chip(-final)
    turn(before, (2, 3))
    head_copy(final - 2, heads - 1).start()
    for chunk in range(heads):
        store_head(final - 1, chunk, head_step(final - 1, before, chunk))
        if chunk > 0:
            head_copy(final - 1, chunk - 1).start()
    chip = ring.chip(0)
    turn(chip, (0, 1))
    head_copy(final - 1, heads - 1).start()
    turn(chip, (2, 3))
    grads = (gate_grad, up_grad, down_grad, o_grad, qkv_grad)
    for chunk in range(ffns):
        _, right, low, size, _ = ffn_chunks[chunk]
        total = ffn_step(final, chip, chunk, True)
        if right == 2:
            down_grad[low : low + size, :] = jnp.transpose(total)
        else:
            grads[right][:, low : low + size] = total
    for chunk in range(heads):
        _, right, low, size, _ = head_chunks[chunk]
        total = head_step(final, chip, chunk)
        if right == 3:
            o_grad[low : low + size, :] = jnp.transpose(total)
        else:
            qkv_grad[:, low : low + size] = total

    def add_sums(offset, total):
        sums_copy(offset).wait_recv()
        return total + sums_in[(ring.me - offset + shards) % shards]

    sums_out[...] = lax.fori_loop(1, shards, add_sums, sums_own[ring.me])

    def drain_heads(step, carry):
        for chunk in range(heads):
            head_copy(step, chunk).wait_send()
        return carry

    def drain_ffn(step, carry):
        for chunk in range(ffns):
            ffn_copy(step, chunk).wait_send()
        return carry

    def drain_sums(offset, carry):
        sums_copy(offset).wait_send()
        return carry

    lax.fori_loop(0, final, drain_heads, 0)
    lax.fori_loop(2, final, drain_ffn, 0)
    lax.fori_loop(1, shards, drain_sums, 0)
    for side in sides:
        side.wait_send()
    pltpu.make_async_copy(d_hidden_buf, x_grad_out, row_sem.at[5]).wait()
    pltpu.make_async_copy(hidden_buf, layer_out, row_sem.at[6]).wait()


def reduce_pass(shards, both, heads, carry, out_part, norm_part, rows_f32, inv, gain, sums):
    normed_two, grad_rows, d_gate, d_up, activated = both
    hidden_rows, normed_one, attended, d_qkv = heads
    tokens, depth = out_part.shape
    units = d_gate.shape[1]
    steps = shards // 2
    rows = depth // shards
    widths = (units, units, units, attended.shape[1], d_qkv.shape[1])
    ffn_chunks, ffn_total = cut_columns(FFN_PAIRS, widths)
    head_chunks, head_total = cut_columns(HEAD_PAIRS, widths)
    half = jnp.bfloat16
    wide = jax.ShapeDtypeStruct((tokens, depth), jnp.float32)
    both_wide = pltpu.VMEM((2 * tokens, depth), half)
    one_half = pltpu.VMEM((tokens, depth), half)
    one_full = pltpu.VMEM((tokens, depth), jnp.float32)
    dma = pltpu.SemaphoreType.DMA
    return pl.pallas_call(
        functools.partial(reduce_kernel, shards, ffn_chunks, head_chunks),
        out_shape=(
            wide,
            wide,
            jax.ShapeDtypeStruct((rows, units), jnp.float32),
            jax.ShapeDtypeStruct((rows, units), jnp.float32),
            jax.ShapeDtypeStruct((units, rows), jnp.float32),
            jax.ShapeDtypeStruct((attended.shape[1], rows), jnp.float32),
            jax.ShapeDtypeStruct((rows, d_qkv.shape[1]), jnp.float32),
            jax.ShapeDtypeStruct(sums.shape[1:], jnp.float32),
        ),
        in_specs=[ANY_SPEC] * 15 + [VMEM_SPEC] * 3,
        out_specs=(ANY_SPEC, ANY_SPEC) + (VMEM_SPEC,) * 6,
        scratch_shapes=[both_wide] * 4
        + [pltpu.VMEM((2 * tokens, width), half) for width in widths]
        + [
            pltpu.VMEM((4, 128, 2 * tokens), half),
            pltpu.VMEM((steps - 2, rows, ffn_total), half),
            pltpu.VMEM((steps, rows, head_total), half),
            one_half,
            one_half,
            one_half,
            one_half,
            one_full,
            one_full,
            one_full,
            pltpu.VMEM((8, depth), jnp.float32),
            pltpu.VMEM(sums.shape, jnp.float32),
            pltpu.VMEM(sums.shape, jnp.float32),
            dma((steps - 3, len(ffn_chunks))),
            dma((steps - 3, len(ffn_chunks))),
            dma((steps - 1, len(head_chunks))),
            dma((steps - 1, len(head_chunks))),
            dma((10,)),
            dma((4,)),
            dma((4,)),
            dma((4,)),
            dma((7,)),
            dma((shards,)),
            dma((shards,)),
        ],
        compiler_params=pltpu.CompilerParams(
            collective_id=2, has_side_effects=True, vmem_limit_bytes=VMEM_BYTES
        ),
        name="reduce_ring",
    )(
        normed_two,
        grad_rows,
        hidden_rows,
        normed_one,
        d_gate,
        d_up,
        activated,
        attended,
        d_qkv,
        carry,
        out_part,
        norm_part,
        *rows_f32,
        inv,
        gain,
        sums,
    )


def body(
    shards,
    layer_input,
    positions,
    norm1_gain,
    w_q,
    w_k,
    w_v,
    w_o,
    norm2_gain,
    w_gate,
    w_up,
    w_down,
    out_grad,
):
    tokens, depth = layer_input.shape
    rows = w_q.shape[0]
    head_count = w_q.shape[1] // HD
    kv_count = w_k.shape[1] // HD
    query_cols = head_count * HD
    kv_cols = kv_count * HD
    pairs = ring_pairs(shards)

    gains = jnp.stack([norm1_gain, norm2_gain]).astype(jnp.float32)
    gains = jnp.pad(gains, ((0, 6), (0, max(128 - rows, 0))))
    gains_all, qkv_all, out_all, down_turned = gather_shards(
        shards, gains, w_q, w_k, w_v, w_o, w_down
    )
    gain_one = gains_all[:, 0, :rows].reshape(1, depth)
    gain_two = gains_all[:, 1, :rows].reshape(1, depth)
    qkv_w = qkv_all.reshape(depth, query_cols + 2 * kv_cols)
    out_w = out_all.reshape(depth, query_cols)
    gate_tied, up_tied, down_tied, _ = lax.optimization_barrier(
        (w_gate, w_up, down_turned, gains_all)
    )
    own = (gate_tied, up_tied, down_tied)
    behind = tuple(lax.ppermute(shard, "dp", pairs) for shard in own)

    inv_one, norm_one = rms_parts(layer_input)
    normed_one = (norm_one * gain_one).astype(jnp.bfloat16)
    cos_table, sin_table = rope_tables(positions, HD)
    qkv = matmul(normed_one, qkv_w)
    queries = rotate(
        qkv[:, :query_cols].reshape(tokens, head_count, HD), cos_table, sin_table, 1.0
    ).astype(jnp.bfloat16)
    key_rows = rotate(
        qkv[:, query_cols : query_cols + kv_cols].reshape(tokens, kv_count, HD),
        cos_table,
        sin_table,
        1.0,
    ).astype(jnp.bfloat16)
    value_rows = qkv[:, query_cols + kv_cols :].astype(jnp.bfloat16).reshape(tokens, kv_count, HD)
    seq_count = tokens // L
    query_seq = queries.reshape(seq_count, L, head_count, HD)
    key_seq = key_rows.reshape(seq_count, L, kv_count, HD)
    value_seq = value_rows.reshape(seq_count, L, kv_count, HD)
    attended, log_total = lax.map(
        lambda block_in: attend(block_in[0], block_in[1], block_in[2]),
        (query_seq, key_seq, value_seq),
    )
    attended_rows = attended.reshape(tokens, query_cols)
    part = matmul_nt(attended_rows, out_w).astype(jnp.bfloat16)
    grad_rows = out_grad.astype(jnp.bfloat16)

    hidden, norm_part, norm_other, out_part, carry, *both = ffn_pass(
        shards, layer_input, part, gain_two, grad_rows, own, behind
    )
    carry = lax.ppermute(carry, "dp", pairs)

    inv_two, norm_two = rms_parts(hidden)
    d_norm_two = norm_part.astype(jnp.float32) + norm_other.astype(jnp.float32)
    grad_gain_two = jnp.sum(d_norm_two * norm_two, axis=0)
    e_two = d_norm_two * gain_two
    d_hidden = out_grad + inv_two * (
        e_two - norm_two * jnp.mean(e_two * norm_two, axis=-1, keepdims=True)
    )
    hidden_rows = d_hidden.astype(jnp.bfloat16)
    d_attended = matmul(hidden_rows, out_w).astype(jnp.bfloat16)
    d_query, d_keys, d_values = lax.map(
        lambda block_in: attend_back(
            block_in[0], block_in[1], block_in[2], block_in[3], block_in[4], block_in[5]
        ),
        (
            query_seq,
            key_seq,
            value_seq,
            attended,
            d_attended.reshape(seq_count, L, query_cols),
            log_total,
        ),
    )
    dq_raw = (
        rotate(d_query.reshape(tokens, head_count, HD), cos_table, sin_table, -1.0)
        .astype(jnp.bfloat16)
        .reshape(tokens, query_cols)
    )
    dk_raw = (
        rotate(d_keys.reshape(tokens, kv_count, HD), cos_table, sin_table, -1.0)
        .astype(jnp.bfloat16)
        .reshape(tokens, kv_cols)
    )
    dv_rows = d_values.astype(jnp.bfloat16).reshape(tokens, kv_cols)
    d_qkv = jnp.concatenate([dq_raw, dk_raw, dv_rows], axis=1)
    norm_one_part = matmul_nt(d_qkv, qkv_w).astype(jnp.bfloat16)

    sums = grad_gain_two.reshape(shards, 1, rows)
    sums = jnp.pad(sums, ((0, 0), (0, 7), (0, max(128 - rows, 0))))
    (
        layer_output,
        x_grad,
        shard_gate,
        shard_up,
        shard_down,
        shard_out,
        shard_qkv,
        sums_out,
    ) = reduce_pass(
        shards,
        both,
        (hidden_rows, normed_one, attended_rows, d_qkv),
        carry,
        out_part,
        norm_one_part,
        (hidden, d_hidden, norm_one),
        inv_one,
        gain_one,
        sums,
    )
    return (
        layer_output,
        x_grad,
        sums_out[1, :rows],
        shard_qkv[:, :query_cols],
        shard_qkv[:, query_cols : query_cols + kv_cols],
        shard_qkv[:, query_cols + kv_cols :],
        shard_out,
        sums_out[0, :rows],
        shard_gate,
        shard_up,
        shard_down,
    )


def solution(mesh):
    in_specs = (
        P("dp", None),
        P("dp"),
        P("dp"),
        P("dp", "tensor"),
        P("dp", "tensor"),
        P("dp", "tensor"),
        P("tensor", "dp"),
        P("dp"),
        P("dp", "tensor"),
        P("dp", "tensor"),
        P("tensor", "dp"),
        P("dp", None),
    )
    out_specs = (
        P("dp", None),
        P("dp", None),
        P("dp"),
        P("dp", "tensor"),
        P("dp", "tensor"),
        P("dp", "tensor"),
        P("tensor", "dp"),
        P("dp"),
        P("dp", "tensor"),
        P("dp", "tensor"),
        P("tensor", "dp"),
    )
    return jax.shard_map(
        functools.partial(body, mesh.shape["dp"]),
        mesh=mesh,
        in_specs=in_specs,
        out_specs=out_specs,
        check_vma=False,
    )
```

time: 585 us -> 530 us (0.906)
  Pallas kernels: 488 us -> 436 us
  other arithmetic: 25.1 us -> 17 us
  waiting for transfers between devices: 0 us -> 7.59 us
    pallas_call x3, Pallas kernels: 488 us -> 436 us  [the longest x1 199 us: ffn_pass(): pl.pallas_call(functools.partial(ffn_kernel, shards, groups, chunks), out...]
    ppermute x0 -> x4, waiting for transfers between devices: none -> 7.59 us  [the longest x1 7.58 us: body(): carry = lax.ppermute(carry, 'dp', pairs)]
    reshape x6 -> x0, local copies, waits for them, and re-layouts: 6.61 us -> none  [blocks(): row_values.reshape(tokens, shards // 2, 2, rows)]
    transpose x2 -> x0, local copies, waits for them, and re-layouts: 6.55 us -> none  [the longest x1 4.46 us: body(): result[:, 2 * units:3 * units]]
    unnamed x96 -> x90, local copies, waits for them, and re-layouts: 13.6 us -> 16.8 us
  transfers between devices with their start and end apart: 0 -> 4, of which waited for: 0 -> 1; matrix products, arithmetic and copies ran while one was open for 0% -> 8% of each run, Pallas kernels for 0% -> 0%
where the time goes in v2:
time: 530 us; the launch traced here: 523 us
  Pallas kernels  436 us (82%)
  local copies, waits for them, and re-layouts  31.5 us (6%)
  matrix products  25.3 us (5%)
  other arithmetic  17 us (3%)
  waiting for transfers between devices  7.59 us (1%)
    pallas_call x1, Pallas kernels, ffn_pass(): pl.pallas_call(functools.partial(ffn_kernel, shards, groups, chunks), out...  199 us
    pallas_call x1, Pallas kernels, reduce_pass(): pl.pallas_call(functools.partial(reduce_kernel, shards, ffn_chunks, head_...  181 us
    pallas_call x1, Pallas kernels, gather_shards(): pl.pallas_call(functools.partial(gather_kernel, shards), out_shape=(jax.S...  55.9 us
    unnamed x90, local copies, waits for them, and re-layouts  16.8 us
  transfers between devices with their start and end apart: 4, of which 1 were waited for; matrix products, arithmetic and copies ran while one was open for 8% of the time, Pallas kernels for 0%

profile of v2, /device:TPU:0, one launch (start us, length us, event | category | flops | bytes accessed | tf_op | source)
XLA Modules:
  0.0 523.3 jit_solution(9576738329466089591)
XLA Ops:
  0.6 1.3 fusion.14.refs_0_
  1.9 55.9 %gather_attention.1 = (f32[16,8,128]{2,1,0:T(8,128)}, bf16[16,128,1280]{2,1,0:T(8,128)(2,1)}, bf16[16,128,1024]{2,1,0:T(8,128)(2,1)}, bf16[128,2816]{1,0:T(8,128)(2,1)}) custom-call(f32[8,128]{1,0:T(8,128)} %fusion.14.refs_0_, bf16[128,1024]{1,0:T(8,128)(2,1)} %refs_1_.1, bf16[128,128]{1,0:T(8,128)(2,1)} %refs_2_.1, bf16[128,128]{1,0:T(8,128)(2,1)} %refs_3_.1, ...), custom_call_target="tpu_custom_call" | custom-call | tf_op jit(solution)/shard_map/gather_attention/pallas_call | solution.py:316
  61.0 1.5 slice_bitcast_fusion.3
  62.5 1.8 multiply_reduce_fusion.3
  64.4 1.6 multiply_convert_fusion
  66.0 2.0 copy-done.40
  68.0 1.5 fusion.24
  76.2 1.2 copy-done.5
  77.5 1.6 copy.42
  79.1 1.1 convert_element_type.92.refs_3_
  80.2 3.3 convolution_convert_fusion.3
  85.3 4.5 convolution_convert_fusion.refs_1_
  91.5 199.3 %ffn_ring.1 = (f32[256,2048]{1,0:T(8,128)}, bf16[256,2048]{1,0:T(8,128)(2,1)}, bf16[256,2048]{1,0:T(8,128)(2,1)}, bf16[256,2048]{1,0:T(8,128)(2,1)}, bf16[128,84...) custom-call(f32[256,2048]{1,0:T(8,128)} %refs_0_.1, ...), custom_call_target="tpu_custom_call" | custom-call | tf_op jit(solution)/shard_map/ffn_ring/pallas_call | solution.py:821
  290.8 2.0 multiply_reduce_fusion.2
  293.0 2.5 multiply_reduce_fusion
  295.8 2.1 fusion.22
  298.8 1.3 convolution_convert_fusion.2
  301.6 3.6 fusion.2
  307.0 1.2 copy.50
  308.3 1.7 convolution_bitcast_fusion.1
  310.1 3.2 fusion.6
  315.0 5.0 convolution_convert_fusion.1.refs_11_
  320.0 7.6 %collective-permute-done.3.refs_9_ = bf16[128,8448]{1,0:T(8,128)(2,1)} collective-permute-done((bf16[128,8448]{1,0:T(8,128)(2,1)}, bf16[128,8448]{1,0:T(8,128)(2,1)}, u32[]{:S(2)}, u32[]{:S(2)}) %collective-permute-start.3) | collective-permute-done | bytes 2162720 | tf_op jit(solution)/shard_map/ppermute | solution.py:1371
  327.6 181.1 %reduce_ring.1 = (f32[256,2048]{1,0:T(8,128)}, f32[256,2048]{1,0:T(8,128)}, f32[128,2816]{1,0:T(8,128)}, f32[128,2816]{1,0:T(8,128)}, f32[2816,128]{1,0:T(8,128)...) custom-call(bf16[512,2048]{1,0:T(8,128)(2,1)} %get-tuple-element.91.refs_0_, ...), custom_call_target="tpu_custom_call" | custom-call | tf_op jit(solution)/shard_map/reduce_ring/pallas_call | solution.py:1238
  508.7 1.9 slice.69
  510.6 1.5 fusion.23
  512.1 1.3 slice_bitcast_fusion
  513.4 3.3 copy.69
  516.7 1.3 copy.70
  519.0 1.1 copy.72
  520.1 1.1 copy.73
  521.9 1.1 copy.74
  (120 shorter events, 21.4 us)
Async XLA Ops:
  57.8 6.5 %copy-start.1 = (f32[256,2048]{1,0:T(8,128)S(1)}, f32[256,2048]{1,0:T(8,128)}, u32[]{:S(2)}) copy-start(f32[256,2048]{1,0:T(8,128)} %refs_0_.1) | copy-start | bytes 6291460
  57.9 31.9 %collective-permute-start = (bf16[128,2816]{1,0:T(8,128)(2,1)}, bf16[128,2816]{1,0:T(8,128)(2,1)S(1)}, u32[]{:S(2)}, u32[]{:S(2)}) collective-permute-start(bf16[128,2816]{1,0:T(8,128)(2,1)} %refs_4_.2), channel_id=1, source_target_pairs={{0,8},{2,6},{4,0},{6,14},{8,16},{10,2},{12,4},{14,22},{16,24},{18,... | collective-permute-start | bytes 2162696 | tf_op jit(solution)/shard_map/ppermute | solution.py:1340
  58.9 31.7 %collective-permute-start.1 = (bf16[128,2816]{1,0:T(8,128)(2,1)}, bf16[128,2816]{1,0:T(8,128)(2,1)S(1)}, u32[]{:S(2)}, u32[]{:S(2)}) collective-permute-start(bf16[128,2816]{1,0:T(8,128)(2,1)} %refs_5_.2), channel_id=1, source_target_pairs={{0,8},{2,6},{4,0},{6,14},{8,16},{10,2},{12,4},{14,22},{16,24},{18,... | collective-permute-start | bytes 2162696 | tf_op jit(solution)/shard_map/ppermute | solution.py:1340
  60.0 31.5 %collective-permute-start.2 = (bf16[128,2816]{1,0:T(8,128)(2,1)}, bf16[128,2816]{1,0:T(8,128)(2,1)}, u32[]{:S(2)}, u32[]{:S(2)}) collective-permute-start(bf16[128,2816]{1,0:T(8,128)(2,1)} %get-tuple-element.90.refs_6_), channel_id=1, source_target_pairs={{0,8},{2,6},{4,0},{6,14},{8,16},{10,2},{12,4},{14,22},{16,24},{18,... | collective-permute-start | bytes 2162696 | tf_op jit(solution)/shard_map/ppermute | solution.py:1340
  64.3 1.6 copy-start.37
  64.4 3.6 copy-start.40
  66.0 3.6 copy-start.6
  69.5 2.5 copy-start.39
  72.0 2.5 copy-start.24
  75.3 2.1 copy-start.5
  75.3 3.7 copy-start.2
  77.5 6.0 %copy-start.35 = (f32[2,8,256]{2,1,0:T(8,128)}, f32[2,8,256]{2,1,0:T(8,128)S(1)}, u32[]{:S(2)}) copy-start(f32[2,8,256]{2,1,0:T(8,128)S(1)} %log_add_fusion) | copy-start | bytes 49156
  80.2 4.3 copy-start.38
  83.5 6.3 %copy-start.10 = (bf16[2,64,8,256]{3,1,2,0:T(8,128)(2,1)}, bf16[2,64,8,256]{3,1,2,0:T(8,128)(2,1)S(1)}, u32[]{:S(2)}) copy-start(bf16[2,64,8,256]{3,1,2,0:T(8,128)(2,1)S(1)} %convolution_convert_fusion.3) | copy-start | bytes 1572868
  290.8 2.2 copy-start
  290.8 2.2 copy-start.32
  293.0 2.5 copy-start.3
  293.0 2.6 copy-start.7
  293.0 2.8 copy-start.8
  295.8 3.0 copy-start.41
  298.8 1.5 copy-start.11
  300.1 1.5 copy-start.27
  300.1 1.5 copy-start.34
  300.1 1.5 copy-start.36
  300.5 27.1 %collective-permute-start.3 = (bf16[128,8448]{1,0:T(8,128)(2,1)}, bf16[128,8448]{1,0:T(8,128)(2,1)}, u32[]{:S(2)}, u32[]{:S(2)}) collective-permute-start(bf16[128,8448]{1,0:T(8,128)(2,1)} %get-tuple-element.99), channel_id=1, source_target_pairs={{0,8},{2,6},{4,0},{6,14},{8,16},{10,2},{12,4},{14,22},{16,24},{18,... | collective-permute-start | bytes 6488072 | tf_op jit(solution)/shard_map/ppermute | solution.py:1371
  301.6 3.6 copy-start.29
  301.6 3.7 copy-start.31
  305.8 2.5 copy-start.16
  513.4 3.3 copy-start.9
  516.7 2.3 copy-start.14
  518.0 2.0 copy-start.13
  520.1 1.9 copy-start.12
  (14 other events, 14.2 us)

commit v3 on v2

--- a/solution.py
+++ b/solution.py
@@ -7,6 +7,7 @@
 from jax.experimental import pallas as pl
 from jax.experimental.pallas import tpu as pltpu
 from jax.sharding import PartitionSpec as P
+
 
 HD = 64
 L = 256
@@ -68,7 +69,7 @@
 
 
 def attend(queries, key_rows, value_rows):
-    grouped, scores = causal_scores(queries, key_rows)
+    _, scores = causal_scores(queries, key_rows)
     row_top = jnp.max(scores, axis=-1, keepdims=True)
     log_total = row_top + jnp.log(jnp.sum(jnp.exp(scores - row_top), axis=-1, keepdims=True))
     weights = jnp.exp(scores - log_total).astype(jnp.bfloat16)
@@ -183,14 +184,11 @@
     return {"tensor": 1 - lax.axis_index("tensor")}
 
 
-def turn_block(source, target):
-    target[...] = jnp.transpose(source[...].astype(jnp.float32)).astype(target.dtype)
-
-
-def turn_rows(source, target):
+def turn_rows(source, target, low=0):
     def one(block, carry):
         here = pl.ds(pl.multiple_of(block * TILE, TILE), TILE)
-        target[:, here] = jnp.transpose(source[here, :].astype(jnp.float32)).astype(target.dtype)
+        there = pl.ds(pl.multiple_of(low + block * TILE, TILE), TILE)
+        target[:, there] = jnp.transpose(source[here, :].astype(jnp.float32)).astype(target.dtype)
         return carry
 
     lax.fori_loop(0, source.shape[0] // TILE, one, 0)
@@ -203,15 +201,18 @@
         k_ref,
         v_ref,
         out_ref,
+        gate_ref,
+        up_ref,
         down_ref,
         gains_all,
         qkv_all,
         out_all,
-        down_turned,
+        ffn_shard,
         qkv_own,
         out_load,
         out_own,
         down_load,
+        ffn_own,
         ring_send,
         ring_recv,
         side_send,
@@ -234,6 +235,10 @@
         low += size
     loads.append(pltpu.make_async_copy(out_ref, out_load, load_sem.at[3]))
     loads.append(pltpu.make_async_copy(down_ref, down_load, load_sem.at[4]))
+    units = gate_ref.shape[1]
+    for index, ref in enumerate((gate_ref, up_ref)):
+        part = ffn_own.at[:, pl.ds(index * units, units)]
+        loads.append(pltpu.make_async_copy(ref, part, load_sem.at[5 + index]))
     for load in loads:
         load.start()
     ring.greet()
@@ -272,9 +277,16 @@
     begin(2)
     begin(1)
     loads[4].wait()
-    turn_rows(down_load, down_turned)
+    turn_rows(down_load, ffn_own, 2 * units)
+    for load in loads[5:]:
+        load.wait()
+    ffn_store = pltpu.make_async_copy(ffn_own, ffn_shard, load_sem.at[7])
 
     def forward(step, carry):
+        @pl.when(step == 2)
+        def _():
+            ffn_store.start()
+
         shard = ring.behind(step)
         for kind in (0, 2, 1):
             here = fulls[kind].at[shard]
@@ -303,11 +315,12 @@
         return carry
 
     lax.fori_loop(0, ring.count, drain, 0)
+    ffn_store.wait()
     for kind in range(kinds):
         own_copy(kind).wait()
 
 
-def gather_shards(shards, gains, w_q, w_k, w_v, w_o, w_down):
+def gather_shards(shards, gains, w_q, w_k, w_v, w_o, w_gate, w_up, w_down):
     steps = shards // 2
     rows = w_q.shape[0]
     columns = w_q.shape[1] + w_k.shape[1] + w_v.shape[1]
@@ -319,27 +332,28 @@
             jax.ShapeDtypeStruct((shards,) + gains.shape, gains.dtype),
             jax.ShapeDtypeStruct((shards, rows, columns), half),
             jax.ShapeDtypeStruct((shards, rows, w_o.shape[0]), half),
-            jax.ShapeDtypeStruct((rows, w_down.shape[0]), half),
+            jax.ShapeDtypeStruct((rows, 3 * w_down.shape[0]), half),
         ),
-        in_specs=[VMEM_SPEC] + [ANY_SPEC] * 5,
-        out_specs=(ANY_SPEC,) * 3 + (VMEM_SPEC,),
+        in_specs=[VMEM_SPEC] + [ANY_SPEC] * 7,
+        out_specs=(ANY_SPEC,) * 4,
         scratch_shapes=[
             pltpu.VMEM((rows, columns), half),
             pltpu.VMEM(w_o.shape, half),
             pltpu.VMEM((rows, w_o.shape[0]), half),
             pltpu.VMEM(w_down.shape, half),
+            pltpu.VMEM((rows, 3 * w_down.shape[0]), half),
             sems,
             sems,
             sems,
             sems,
             pltpu.SemaphoreType.DMA((3,)),
-            pltpu.SemaphoreType.DMA((5,)),
+            pltpu.SemaphoreType.DMA((8,)),
         ],
         compiler_params=pltpu.CompilerParams(
             collective_id=0, has_side_effects=True, vmem_limit_bytes=VMEM_BYTES
         ),
         name="gather_attention",
-    )(gains, w_q, w_k, w_v, w_o, w_down)
+    )(gains, w_q, w_k, w_v, w_o, w_gate, w_up, w_down)
 
 
 def turn_left(ring, left_all, turned, index, chip):
@@ -385,12 +399,8 @@
         part_ref,
         gain_ref,
         grad_ref,
-        gate_ref,
-        up_ref,
-        down_ref,
-        gate_behind,
-        up_behind,
-        down_behind,
+        shard_ref,
+        behind_ref,
         hidden_ref,
         norm_part_ref,
         norm_other_ref,
@@ -401,9 +411,9 @@
         d_gate_out,
         d_up_out,
         act_out,
-    ) = refs[:20]
+    ) = refs[:16]
     count = len(groups)
-    full = [refs[20 + 3 * group : 23 + 3 * group] for group in range(count)]
+    full = refs[16 : 16 + count]
     (
         part_other,
         out_total,
@@ -429,16 +439,17 @@
         sum_recv,
         store_sem,
         free_sem,
-    ) = refs[20 + 3 * count :]
-    shard_refs = (gate_ref, up_ref, down_ref)
-    behind_refs = (gate_behind, up_behind, down_behind)
+    ) = refs[16 + count :]
     tokens = part_ref.shape[0]
-    rows = gate_ref.shape[0]
+    rows, units_all = shard_ref.shape
+    units_all //= 3
     depth = normed_all.shape[1]
     blocks = depth // TILE
     ring = Ring(shards)
     mine = pl.ds(pl.multiple_of(ring.core * tokens, tokens), tokens)
 
+    ticks = 3 * (ring.count - 2)
+    last_tick = ticks - 4
     x_load = pltpu.make_async_copy(x_ref, hidden_ref, part_sem.at[2])
     grad_load = pltpu.make_async_copy(grad_ref, grad_all.at[mine], part_sem.at[3])
     x_load.start()
@@ -446,11 +457,11 @@
     ring.greet(partner=True)
 
     def place(group, kind, shard):
-        return full[group][kind].at[pl.ds(pl.multiple_of(shard * rows, rows), rows)]
-
-    def cut(ref, group):
+        return full[group].at[kind, pl.ds(pl.multiple_of(shard * rows, rows), rows)]
+
+    def cut(ref, group, kind):
         low, size = groups[group]
-        return ref.at[:, pl.ds(low, size)]
+        return ref.at[:, pl.ds(kind * units_all + low, size)]
 
     def ring_copy(group, step, kind, shard, source):
         return send_to(
@@ -473,12 +484,12 @@
     def own_copies(group, kind):
         return (
             pltpu.make_async_copy(
-                cut(shard_refs[kind], group),
+                cut(shard_ref, group, kind),
                 place(group, kind, ring.me),
                 own_sem.at[group, kind, 0],
             ),
             pltpu.make_async_copy(
-                cut(behind_refs[kind], group),
+                cut(behind_ref, group, kind),
                 place(group, kind, ring.behind(1)),
                 own_sem.at[group, kind, 1],
             ),
@@ -486,24 +497,31 @@
 
     def begin(group):
         for kind in range(3):
-            source = cut(behind_refs[kind], group)
+            source = cut(behind_ref, group, kind)
             ring_copy(group, 1, kind, ring.behind(1), source).start()
             side_copy(group, 1, kind, ring.behind(1), source).start()
-            side_copy(group, 0, kind, ring.me, cut(shard_refs[kind], group)).start()
+            side_copy(group, 0, kind, ring.me, cut(shard_ref, group, kind)).start()
             for copy in own_copies(group, kind):
                 copy.start()
 
-    def forward(group, step):
+    def forward(group, tick):
+        step = 2 + tick // 3
+        kind = tick % 3
         shard = ring.behind(step)
-        for kind in range(3):
-            here = place(group, kind, shard)
-            ring_copy(group, step - 1, kind, shard, here).wait_recv()
-
-            @pl.when(step < ring.count - 1)
+        here = place(group, kind, shard)
+        ring_copy(group, step - 1, kind, shard, here).wait_recv()
+
+        @pl.when(step < ring.count - 1)
+        def _():
+            ring_copy(group, step, kind, shard, here).start()
+
+        side_copy(group, step, kind, shard, here).start()
+
+        if group + 1 < count:
+
+            @pl.when(tick == last_tick)
             def _():
-                ring_copy(group, step, kind, shard, here).start()
-
-            side_copy(group, step, kind, shard, here).start()
+                begin(group + 1)
 
     def arrived(group):
         for kind in range(3):
@@ -556,9 +574,9 @@
         low, _ = groups[group]
         part = pl.ds(pl.multiple_of(tile * TILE, TILE), TILE)
         target = pl.ds(pl.multiple_of(low + tile * TILE, TILE), TILE)
-        gate_pre = matmul(normed_all[mine, :], full[group][0][:, part])
-        up_pre = matmul(normed_all[mine, :], full[group][1][:, part])
-        d_act = matmul(grad_all[mine, :], full[group][2][:, part])
+        gate_pre = matmul(normed_all[mine, :], full[group][0, :, part])
+        up_pre = matmul(normed_all[mine, :], full[group][1, :, part])
+        d_act = matmul(grad_all[mine, :], full[group][2, :, part])
         sigmoid_gate = jax.nn.sigmoid(gate_pre)
         silu_gate = gate_pre * sigmoid_gate
         act_all[mine, target] = (silu_gate * up_pre).astype(jnp.bfloat16)
@@ -571,28 +589,24 @@
         low, size = groups[group]
         units = pl.ds(low, size)
         features = pl.ds(pl.multiple_of(block * TILE, TILE), TILE)
-        return matmul_nt(d_gate_all[mine, units], full[group][0][features, :]) + matmul_nt(
-            d_up_all[mine, units], full[group][1][features, :]
+        return matmul_nt(d_gate_all[mine, units], full[group][0, features, :]) + matmul_nt(
+            d_up_all[mine, units], full[group][1, features, :]
         )
 
     def out_terms(group, block):
         low, size = groups[group]
         features = pl.ds(pl.multiple_of(block * TILE, TILE), TILE)
-        return matmul_nt(act_all[mine, pl.ds(low, size)], full[group][2][features, :])
-
-    def accumulate(group, low_block, high_block):
-        def one(block, carry):
-            features = pl.ds(pl.multiple_of(block * TILE, TILE), TILE)
-            norm_new = norm_terms(group, block)
-            out_new = out_terms(group, block)
-            if group > 0:
-                norm_new += norm_total[:, features]
-                out_new += out_total[:, features]
-            norm_total[:, features] = norm_new
-            out_total[:, features] = out_new
-            return carry
-
-        lax.fori_loop(low_block, high_block, one, 0)
+        return matmul_nt(act_all[mine, pl.ds(low, size)], full[group][2, features, :])
+
+    def accumulate(group, block):
+        features = pl.ds(pl.multiple_of(block * TILE, TILE), TILE)
+        norm_new = norm_terms(group, block)
+        out_new = out_terms(group, block)
+        if group > 0:
+            norm_new += norm_total[:, features]
+            out_new += out_total[:, features]
+        norm_total[:, features] = norm_new
+        out_total[:, features] = out_new
 
     part_copy = send_to(partner_id(), part_ref, part_other, part_sem.at[0], part_sem.at[1])
     part_copy.start()
@@ -600,12 +614,11 @@
     grad_load.wait()
     left_copy(1).start()
 
-    def first_steps(step, carry):
-        forward(0, step)
+    def first_ticks(tick, carry):
+        forward(0, tick)
         return carry
 
-    lax.fori_loop(2, ring.count, first_steps, 0)
-    begin(1)
+    lax.fori_loop(0, ticks, first_ticks, 0)
     x_load.wait()
     part_copy.wait()
 
@@ -625,38 +638,31 @@
     for group in range(1, count):
         before = group - 1
         tiles = groups[before][1] // TILE
-        if group > 1:
-            begin(group)
         arrived(before)
-
-        def step_and_work(step, carry):
-            forward(group, step)
-            work = step - 2
-
-            @pl.when(work < tiles)
+        if group == 1:
+            left_copy(0).start()
+
+        def tick_and_work(tick, carry):
+            forward(group, tick)
+
+            @pl.when((tick % 2 == 0) & (tick < 2 * tiles))
             def _():
-                hidden_units(before, work)
-
-            if group == 1:
-
-                @pl.when(work == 0)
-                def _():
-                    left_copy(0).start()
-
-            for half in range(2):
-
-                @pl.when(work == tiles + half)
-                def _():
-                    if half == 0:
-                        for index in range(3):
-                            right_copy(before, index).start()
-                    accumulate(before, half * (blocks // 2), (half + 1) * (blocks // 2))
+                hidden_units(before, tick // 2)
+
+            block = tick - (2 * tiles - 1)
+
+            @pl.when(block == 0)
+            def _():
+                for index in range(3):
+                    right_copy(before, index).start()
+
+            @pl.when((block >= 0) & (block < blocks))
+            def _():
+                accumulate(before, block)
 
             return carry
 
-        lax.fori_loop(2, ring.count, step_and_work, 0)
-        if tiles + 1 > ring.count - 3:
-            accumulate(before, blocks // 2, blocks)
+        lax.fori_loop(0, ticks, tick_and_work, 0)
         if group == 1:
             drain(0)
             pl.semaphore_signal(
@@ -692,12 +698,10 @@
         def _():
             norm_copy(block - 1).start()
 
-        if True:
-
-            @pl.when(block == 0)
-            def _():
-                for index in range(3):
-                    right_copy(last, index).start()
+        @pl.when(block == 0)
+        def _():
+            for index in range(3):
+                right_copy(last, index).start()
 
         return carry
 
@@ -732,7 +736,7 @@
 
     def sum_slot(kind, chunk):
         _, _, _, size, _ = chunks[chunk]
-        return full[0][kind].at[pl.ds(chunk * rows, rows), pl.ds(0, size)]
+        return full[0].at[kind, pl.ds(chunk * rows, rows), pl.ds(0, size)]
 
     def sum_copy(chunk):
         return send_to(
@@ -753,7 +757,7 @@
     pl.semaphore_wait(free_sem, 1)
     for chunk in range(len(chunks)):
         size = chunks[chunk][3]
-        full[0][0][chunk * rows : (chunk + 1) * rows, 0:size] = terms(chunk, chip).astype(
+        full[0][0, chunk * rows : (chunk + 1) * rows, 0:size] = terms(chunk, chip).astype(
             jnp.bfloat16
         )
         if chunk > 0:
@@ -766,7 +770,7 @@
         _, _, _, size, target = chunks[chunk]
         total = terms(chunk, chip)
         sum_copy(chunk).wait_recv()
-        total += full[0][1][chunk * rows : (chunk + 1) * rows, 0:size].astype(jnp.float32)
+        total += full[0][1, chunk * rows : (chunk + 1) * rows, 0:size].astype(jnp.float32)
         carry_ref[:, target : target + size] = total.astype(jnp.bfloat16)
 
     for group in range(1, count):
@@ -803,7 +807,8 @@
 
 def ffn_pass(shards, x_rows, part, gain, grad_rows, own, behind):
     tokens, depth = x_rows.shape
-    rows, units = own[0].shape
+    rows, units = own.shape
+    units //= 3
     steps = shards // 2
     groups = ffn_groups(units, steps)
     chunks, total = cut_columns(FFN_PAIRS, (units,) * 3)
@@ -813,7 +818,7 @@
     both_inner = jax.ShapeDtypeStruct((2 * tokens, units), half)
     full = []
     for _, size in groups:
-        full += [pltpu.VMEM((depth, size), half)] * 3
+        full.append(pltpu.VMEM((3, depth, size), half))
     sems = pltpu.SemaphoreType.DMA((len(groups), steps, 3))
     block_sems = pltpu.SemaphoreType.DMA((depth // TILE,))
     pair_sems = pltpu.SemaphoreType.DMA((len(groups), 3))
@@ -832,7 +837,7 @@
             both_inner,
             both_inner,
         ),
-        in_specs=[ANY_SPEC, VMEM_SPEC, VMEM_SPEC] + [ANY_SPEC] * 7,
+        in_specs=[ANY_SPEC, VMEM_SPEC, VMEM_SPEC] + [ANY_SPEC] * 3,
         out_specs=(VMEM_SPEC,) * 5 + (ANY_SPEC,) * 5,
         scratch_shapes=full
         + [
@@ -865,7 +870,7 @@
             collective_id=1, has_side_effects=True, vmem_limit_bytes=VMEM_BYTES
         ),
         name="ffn_ring",
-    )(x_rows, part, gain, grad_rows, *own, *behind)
+    )(x_rows, part, gain, grad_rows, own, behind)
 
 
 def reduce_kernel(shards, ffn_chunks, head_chunks, *refs):
@@ -1301,6 +1306,61 @@
     )
 
 
+def emit_kernel(cuts, *refs):
+    ins = refs[: len(cuts)]
+    count = sum(len(cut) for cut in cuts)
+    outs = refs[len(cuts) : len(cuts) + count]
+    sums_ref, sums_one, sums_two = refs[len(cuts) + count : len(cuts) + count + 3]
+    bufs = refs[len(cuts) + count + 3 : -2]
+    load_sem, store_sem = refs[-2:]
+    loads = [
+        pltpu.make_async_copy(source, buf, load_sem.at[index])
+        for index, (source, buf) in enumerate(zip(ins, bufs))
+    ]
+    for load in loads:
+        load.start()
+    stores = []
+    for index, cut in enumerate(cuts):
+        loads[index].wait()
+        for low, size in cut:
+            at = len(stores)
+            source = bufs[index] if len(cut) == 1 else bufs[index].at[:, pl.ds(low, size)]
+            stores.append(pltpu.make_async_copy(source, outs[at], store_sem.at[at]))
+            stores[-1].start()
+    sums_one[...] = sums_ref[1, : sums_one.shape[0]]
+    sums_two[...] = sums_ref[0, : sums_two.shape[0]]
+    for store in stores:
+        store.wait()
+
+
+def emit(arrays, cuts, sums, rows):
+    outs = []
+    for array, cut in zip(arrays, cuts):
+        for _, size in cut:
+            outs.append(jax.ShapeDtypeStruct((array.shape[0], size), array.dtype))
+    count = len(outs)
+    line = jax.ShapeDtypeStruct((rows,), jnp.float32)
+
+    def kernel(*refs):
+        ins = refs[: len(arrays)]
+        sums_ref = refs[len(arrays)]
+        rest = refs[len(arrays) + 1 :]
+        emit_kernel(
+            cuts, *ins, *rest[:count], sums_ref, rest[count], rest[count + 1], *rest[count + 2 :]
+        )
+
+    return pl.pallas_call(
+        kernel,
+        out_shape=tuple(outs) + (line, line),
+        in_specs=[ANY_SPEC] * len(arrays) + [VMEM_SPEC],
+        out_specs=(ANY_SPEC,) * count + (VMEM_SPEC, VMEM_SPEC),
+        scratch_shapes=[pltpu.VMEM(array.shape, array.dtype) for array in arrays]
+        + [pltpu.SemaphoreType.DMA((len(arrays),)), pltpu.SemaphoreType.DMA((count,))],
+        compiler_params=pltpu.CompilerParams(vmem_limit_bytes=VMEM_BYTES),
+        name="emit_results",
+    )(*arrays, sums)
+
+
 def body(
     shards,
     layer_input,
@@ -1326,18 +1386,14 @@
 
     gains = jnp.stack([norm1_gain, norm2_gain]).astype(jnp.float32)
     gains = jnp.pad(gains, ((0, 6), (0, max(128 - rows, 0))))
-    gains_all, qkv_all, out_all, down_turned = gather_shards(
-        shards, gains, w_q, w_k, w_v, w_o, w_down
+    gains_all, qkv_all, out_all, own = gather_shards(
+        shards, gains, w_q, w_k, w_v, w_o, w_gate, w_up, w_down
     )
     gain_one = gains_all[:, 0, :rows].reshape(1, depth)
     gain_two = gains_all[:, 1, :rows].reshape(1, depth)
     qkv_w = qkv_all.reshape(depth, query_cols + 2 * kv_cols)
     out_w = out_all.reshape(depth, query_cols)
-    gate_tied, up_tied, down_tied, _ = lax.optimization_barrier(
-        (w_gate, w_up, down_turned, gains_all)
-    )
-    own = (gate_tied, up_tied, down_tied)
-    behind = tuple(lax.ppermute(shard, "dp", pairs) for shard in own)
+    behind = lax.ppermute(own, "dp", pairs)
 
     inv_one, norm_one = rms_parts(layer_input)
     normed_one = (norm_one * gain_one).astype(jnp.bfloat16)
@@ -1429,15 +1485,38 @@
         gain_one,
         sums,
     )
+    cuts = [((0, array.shape[1]),) for array in (layer_output, x_grad)]
+    cuts.append(
+        ((0, query_cols), (query_cols, kv_cols), (query_cols + kv_cols, kv_cols))
+    )
+    cuts += [((0, array.shape[1]),) for array in (shard_out, shard_gate, shard_up, shard_down)]
+    (
+        layer_output,
+        x_grad,
+        shard_query,
+        shard_key,
+        shard_value,
+        shard_out,
+        shard_gate,
+        shard_up,
+        shard_down,
+        sums_one,
+        sums_two,
+    ) = emit(
+        (layer_output, x_grad, shard_qkv, shard_out, shard_gate, shard_up, shard_down),
+        cuts,
+        sums_out,
+        rows,
+    )
     return (
         layer_output,
         x_grad,
-        sums_out[1, :rows],
-        shard_qkv[:, :query_cols],
-        shard_qkv[:, query_cols : query_cols + kv_cols],
-        shard_qkv[:, query_cols + kv_cols :],
+        sums_one,
+        shard_query,
+        shard_key,
+        shard_value,
         shard_out,
-        sums_out[0, :rows],
+        sums_two,
         shard_gate,
         shard_up,
         shard_down,
@@ -1472,10 +1551,10 @@
         P("dp", "tensor"),
         P("tensor", "dp"),
     )
+
+    def layer(*args):
+        return body(mesh.shape["dp"], *args)
+
     return jax.shard_map(
-        functools.partial(body, mesh.shape["dp"]),
-        mesh=mesh,
-        in_specs=in_specs,
-        out_specs=out_specs,
-        check_vma=False,
-    )
+        layer, mesh=mesh, in_specs=in_specs, out_specs=out_specs, check_vma=False
+    )

time: 530 us -> 497 us (0.938); the launches traced: 523 us -> 496 us
  local copies, waits for them, and re-layouts: 31.5 us -> 14.3 us
  Pallas kernels: 436 us -> 430 us
    pallas_call x1, Pallas kernels: 199 us -> 185 us  [ffn_pass(): pl.pallas_call(functools.partial(ffn_kernel, shards, groups, chunks), out...]
    unnamed x90 -> x64, local copies, waits for them, and re-layouts: 16.8 us -> 5.62 us
    pallas_call x0 -> x1, Pallas kernels: none -> 8.62 us  [emit(): pl.pallas_call(kernel, out_shape=tuple(outs) + (line, line), in_specs=[AN...]
  transfers between devices with their start and end apart: 4 -> 2, of which waited for: 1 -> 2; matrix products, arithmetic and copies ran while one was open for 8% -> 8% of each run, Pallas kernels for 0% -> 0%
where the time goes in v3:
time: 497 us; the launch traced here: 496 us
  Pallas kernels  430 us (87%)
  matrix products  23.2 us (5%)
  other arithmetic  16.3 us (3%)
  local copies, waits for them, and re-layouts  14.3 us (3%)
  waiting for transfers between devices  8.88 us (2%)
    pallas_call x1, Pallas kernels, ffn_pass(): pl.pallas_call(functools.partial(ffn_kernel, shards, groups, chunks), out...  185 us
    pallas_call x1, Pallas kernels, reduce_pass(): pl.pallas_call(functools.partial(reduce_kernel, shards, ffn_chunks, head_...  181 us
    pallas_call x1, Pallas kernels, gather_shards(): pl.pallas_call(functools.partial(gather_kernel, shards), out_shape=(jax.S...  55.1 us
  transfers between devices with their start and end apart: 2, of which 2 were waited for; matrix products, arithmetic and copies ran while one was open for 8% of the time, Pallas kernels for 0%

profile of v3, /device:TPU:0, one launch (start us, length us, event | category | flops | bytes accessed | tf_op | source)
XLA Modules:
  0.0 496.0 jit_solution(4761123497918798255)
XLA Ops:
  0.6 1.3 fusion.14.refs_0_
  1.9 55.1 %gather_attention.1 = (f32[16,8,128]{2,1,0:T(8,128)}, bf16[16,128,1280]{2,1,0:T(8,128)(2,1)}, bf16[16,128,1024]{2,1,0:T(8,128)(2,1)}, bf16[128,8448]{1,0:T(8,128)(2,1)}) custom-call(f32[8,128]{1,0:T(8,128)} %fusion.14.refs_0_, bf16[128,1024]{1,0:T(8,128)(2,1)} %refs_1_.1, bf16[128,128]{1,0:T(8,128)(2,1)} %refs_2_.1, bf16[128,128]{1,0:T(8,128)(2,1)} %refs_3_.1, ...), custom_call_target="tpu_custom_call" | custom-call | tf_op jit(solution)/shard_map/gather_attention/pallas_call | solution.py:329
  57.0 1.1 collective-permute-start
  58.1 1.5 slice_bitcast_fusion.1
  59.6 1.8 multiply_reduce_fusion.3
  61.5 1.6 multiply_convert_fusion
  63.1 2.0 copy-done.30
  65.1 1.5 fusion.23
  66.7 1.1 slice.57
  68.1 1.7 copy.44
  70.0 1.1 convert_element_type.92.refs_3_
  74.3 1.2 copy-done.5
  75.5 1.1 convolution_convert_fusion.3
  76.6 1.0 copy.53.refs_7_
  78.4 4.5 convolution_convert_fusion.refs_1_
  82.8 1.3 collective-permute-done.refs_5_
  84.1 185.5 %ffn_ring.1 = (f32[256,2048]{1,0:T(8,128)}, bf16[256,2048]{1,0:T(8,128)(2,1)}, bf16[256,2048]{1,0:T(8,128)(2,1)}, bf16[256,2048]{1,0:T(8,128)(2,1)}, bf16[128,84...) custom-call(f32[256,2048]{1,0:T(8,128)} %refs_0_.1, ...), custom_call_target="tpu_custom_call" | custom-call | tf_op jit(solution)/shard_map/ffn_ring/pallas_call | solution.py:826
  269.6 2.0 multiply_reduce_fusion.2
  271.9 2.5 multiply_reduce_fusion
  274.6 2.1 fusion.22
  276.7 1.0 copy-done.4
  277.7 1.3 convolution_convert_fusion.2
  279.4 1.1 collective-permute-start.1
  280.5 3.6 fusion.2
  285.9 1.2 copy.50
  287.2 1.7 convolution_bitcast_fusion.1
  289.0 3.2 fusion.6
  293.0 0.9 pad_maximum_fusion.refs_8_
  293.9 5.0 %convolution_convert_fusion.1.refs_11_ = bf16[256,2048]{1,0:T(8,128)(2,1)} fusion(bf16[2048,1280]{1,0:T(8,128)(2,1)} %bitcast.111, bf16[256,128]{1,0:T(8,128)(2,1)S(1)} %copy.52, bf16[256,128]{1,0:T(8,128)(2,1)S(1)} %copy.51, bf16[256,1024]{1,0:T(8,128)(2,1)S(1)} %copy.50), kind=kOutput, calls=%fused_computation.10 | convolution fusion | flops 1344667648 | bytes 6946816 | tf_op jit(solution)/shard_map/dot_general | solution.py:29
  298.9 7.6 %collective-permute-done.1.refs_9_ = bf16[128,8448]{1,0:T(8,128)(2,1)} collective-permute-done((bf16[128,8448]{1,0:T(8,128)(2,1)}, bf16[128,8448]{1,0:T(8,128)(2,1)}, u32[]{:S(2)}, u32[]{:S(2)}) %collective-permute-start.1) | collective-permute-done | bytes 2162720 | tf_op jit(solution)/shard_map/ppermute | solution.py:1427
  306.5 180.6 %reduce_ring.1 = (f32[256,2048]{1,0:T(8,128)}, f32[256,2048]{1,0:T(8,128)}, f32[128,2816]{1,0:T(8,128)}, f32[128,2816]{1,0:T(8,128)}, f32[2816,128]{1,0:T(8,128)...) custom-call(bf16[512,2048]{1,0:T(8,128)(2,1)} %get-tuple-element.96.refs_0_, ...), custom_call_target="tpu_custom_call" | custom-call | tf_op jit(solution)/shard_map/reduce_ring/pallas_call | solution.py:1243
  487.1 8.6 %emit_results.1 = (f32[256,2048]{1,0:T(8,128)}, f32[256,2048]{1,0:T(8,128)}, f32[128,1024]{1,0:T(8,128)}, f32[128,128]{1,0:T(8,128)}, f32[128,128]{1,0:T(8,128)}...) custom-call(f32[256,2048]{1,0:T(8,128)} %get-tuple-element.106.refs_, ...), custom_call_target="tpu_custom_call" | custom-call | tf_op jit(solution)/shard_map/emit_results/pallas_call | solution.py:1352
  (89 shorter events, 7.9 us)
Async XLA Ops:
  57.0 4.5 copy-start.1
  57.0 27.1 %collective-permute-start = (bf16[128,8448]{1,0:T(8,128)(2,1)}, bf16[128,8448]{1,0:T(8,128)(2,1)}, u32[]{:S(2)}, u32[]{:S(2)}) collective-permute-start(bf16[128,8448]{1,0:T(8,128)(2,1)} %get-tuple-element.95.refs_4_), channel_id=1, source_target_pairs={{0,8},{2,6},{4,0},{6,14},{8,16},{10,2},{12,4},{14,22},{16,24},{18,... | collective-permute-start | bytes 6488072 | tf_op jit(solution)/shard_map/ppermute | solution.py:1396
  61.5 3.6 copy-start.30
  63.1 3.6 copy-start.6
  66.7 1.4 copy-start.11
  66.7 3.1 copy-start.29
  66.7 3.3 copy-start.2
  68.1 6.2 %copy-start.18 = (pred[256,256]{0,1:T(8,128)(4,1)}, pred[256,256]{0,1:T(8,128)(4,1)S(1)}, u32[]{:S(2)}) copy-start(pred[256,256]{0,1:T(8,128)(4,1)S(1)} %iota_compare_fusion) | copy-start | bytes 196612
  68.1 1.7 slice-start
  70.0 4.3 copy-start.25
  72.0 1.4 copy-start.20
  72.0 1.4 copy-start.22
  72.2 1.2 copy-start.12
  72.2 1.2 copy-start.14
  73.4 2.1 copy-start.5
  74.3 2.3 copy-start.27
  76.6 6.3 %copy-start.9 = (bf16[2,64,8,256]{3,1,2,0:T(8,128)(2,1)}, bf16[2,64,8,256]{3,1,2,0:T(8,128)(2,1)S(1)}, u32[]{:S(2)}) copy-start(bf16[2,64,8,256]{3,1,2,0:T(8,128)(2,1)S(1)} %convolution_convert_fusion.3) | copy-start | bytes 1572868
  269.6 2.2 copy-start
  269.6 2.2 copy-start.24
  271.8 2.5 copy-start.3
  271.8 2.6 copy-start.7
  271.8 2.8 copy-start.8
  274.6 3.0 copy-start.31
  276.7 1.0 copy-start.4
  277.7 1.5 copy-start.10
  279.0 1.5 copy-start.19
  279.0 1.5 copy-start.26
  279.0 1.5 copy-start.28
  279.4 27.1 %collective-permute-start.1 = (bf16[128,8448]{1,0:T(8,128)(2,1)}, bf16[128,8448]{1,0:T(8,128)(2,1)}, u32[]{:S(2)}, u32[]{:S(2)}) collective-permute-start(bf16[128,8448]{1,0:T(8,128)(2,1)} %get-tuple-element.104), channel_id=1, source_target_pairs={{0,8},{2,6},{4,0},{6,14},{8,16},{10,2},{12,4},{14,22},{16,24},{18,... | collective-permute-start | bytes 6488072 | tf_op jit(solution)/shard_map/ppermute | solution.py:1427
  280.5 3.6 copy-start.21
  280.5 3.7 copy-start.23
  284.6 2.5 copy-start.13
  (3 other events, 2.1 us)

commit v4 on v3

v4 whole, which is shorter than its diff:
```python
import functools
import math

import jax
import jax.numpy as jnp
from jax import lax
from jax.experimental import pallas as pl
from jax.experimental.pallas import tpu as pltpu
from jax.sharding import PartitionSpec as P


HD = 64
L = 256
TILE = 256
VMEM_BYTES = 67043328

epsilon = 1e-05

MESH_IDS = pl.DeviceIdType.MESH
VMEM_SPEC = pl.BlockSpec(memory_space=pltpu.VMEM)
ANY_SPEC = pl.BlockSpec(memory_space=pl.ANY)


def matmul(left_side, right_side):
    return jnp.dot(left_side, right_side, preferred_element_type=jnp.float32)


def matmul_nt(left_side, right_side):
    return lax.dot_general(
        left_side, right_side, (((1,), (1,)), ((), ())), preferred_element_type=jnp.float32
    )


def rms_parts(row_values):
    inv_rms = lax.rsqrt(jnp.mean(row_values * row_values, axis=-1, keepdims=True) + epsilon)
    return (inv_rms, row_values * inv_rms)


def rope_tables(pos_rows, head_dim):
    half_dim = head_dim // 2
    frequency = jnp.exp(
        jnp.arange(half_dim, dtype=jnp.float32) * (-2.0 * math.log(10000.0) / head_dim)
    )
    angles = pos_rows.astype(jnp.float32)[:, None] * frequency[None, :]
    return (jnp.cos(angles), jnp.sin(angles))


def rotate(row_values, cos_table, sin_table, direction_sign):
    half_dim = row_values.shape[-1] // 2
    first_half = row_values[..., :half_dim]
    second = row_values[..., half_dim:]
    cos_part = cos_table[:, None, :]
    sin_part = sin_table[:, None, :] * direction_sign
    return jnp.concatenate(
        [first_half * cos_part - second * sin_part, second * cos_part + first_half * sin_part],
        axis=-1,
    )


def causal_scores(queries, key_rows):
    length, head_count, head_dim = queries.shape
    kv_count = key_rows.shape[1]
    grouped = queries.reshape(length, kv_count, head_count // kv_count, head_dim)
    scores = jnp.einsum(
        "qkgd,pkd->kgqp", grouped, key_rows, preferred_element_type=jnp.float32
    ) * head_dim ** (-0.5)
    future_mask = jnp.arange(length)[None, :] > jnp.arange(length)[:, None]
    return (grouped, jnp.where(future_mask, -jnp.inf, scores))


def attend(queries, key_rows, value_rows):
    _, scores = causal_scores(queries, key_rows)
    row_top = jnp.max(scores, axis=-1, keepdims=True)
    log_total = row_top + jnp.log(jnp.sum(jnp.exp(scores - row_top), axis=-1, keepdims=True))
    weights = jnp.exp(scores - log_total).astype(jnp.bfloat16)
    attended = jnp.einsum("kgqp,pkd->qkgd", weights, value_rows, preferred_element_type=jnp.float32)
    return (attended.reshape(queries.shape[0], -1).astype(jnp.bfloat16), log_total)


def attend_back(queries, key_rows, value_rows, attended, d_attended, log_total):
    length, head_count, head_dim = queries.shape
    kv_count = key_rows.shape[1]
    grouped, scores = causal_scores(queries, key_rows)
    prob_rows = jnp.exp(scores - log_total)
    d_grouped = d_attended.reshape(length, kv_count, head_count // kv_count, head_dim)
    out_grouped = attended.reshape(length, kv_count, head_count // kv_count, head_dim)
    row_delta = jnp.sum(out_grouped.astype(jnp.float32) * d_grouped.astype(jnp.float32), axis=-1)
    row_delta = jnp.transpose(row_delta, (1, 2, 0))[..., None]
    d_probs = jnp.einsum(
        "qkgd,pkd->kgqp", d_grouped, value_rows, preferred_element_type=jnp.float32
    )
    d_scores = (prob_rows * (d_probs - row_delta) * head_dim ** (-0.5)).astype(jnp.bfloat16)
    d_query = jnp.einsum("kgqp,pkd->qkgd", d_scores, key_rows, preferred_element_type=jnp.float32)
    d_keys = jnp.einsum("kgqp,qkgd->pkd", d_scores, grouped, preferred_element_type=jnp.float32)
    d_values = jnp.einsum(
        "kgqp,qkgd->pkd",
        prob_rows.astype(jnp.bfloat16),
        d_grouped,
        preferred_element_type=jnp.float32,
    )
    return (d_query.reshape(length, head_count, head_dim), d_keys, d_values)


def chip_at(place, count):
    side = place // (count // 2)
    row = place + side * (count - 1 - 2 * place)
    return 2 * row + side


def place_of(chip, count):
    side = chip % 2
    row = chip // 2
    return row + side * (count - 1 - 2 * row)


class Ring:
    def __init__(self, shards):
        self.shards = shards
        self.count = shards // 2
        self.me = lax.axis_index("dp")
        self.core = self.me % 2
        self.place = place_of(self.me // 2, self.count)
        self.sign = 1 - 2 * self.core
        self.rows = shards // 4
        self.row = self.me // 4
        self.side = self.me // 2 % 2
        self.following = self.device(1, self.core)
        self.previous = self.device(-1, self.core)
        self.sibling = self.device(0, 1 - self.core)

    def chip(self, steps):
        place = (self.place + self.sign * steps + 2 * self.count) % self.count
        return chip_at(place, self.count)

    def device(self, steps, core):
        return self.chip(steps) * 2 + core

    def at(self, row, side):
        return (2 * row + side) * 2 + self.core

    def owner(self, slot):
        short = jnp.minimum(self.row, self.rows - 1 - self.row)
        far = self.rows - 1 - short
        way = 1 - 2 * (self.row // (self.rows // 2))
        turn = slot - (far - short)
        return jnp.where(
            turn < 0, way * (far - slot), (1 - 2 * (turn % 2)) * way * (short - turn // 2)
        )

    def behind(self, steps):
        return self.device(-steps, self.core)

    def greet(self, partner=False, everyone=False):
        barrier = pltpu.get_barrier_semaphore()

        def signal(device):
            pl.semaphore_signal(barrier, inc=1, device_id=device, device_id_type=MESH_IDS)

        if everyone:

            def one(offset, carry):
                signal({"dp": (self.me + offset) % self.shards})
                return carry

            lax.fori_loop(1, self.shards, one, 0)
            expected = self.shards - 1
        else:
            for other in (self.following, self.previous, self.sibling):
                signal({"dp": other})
            expected = 3
        if partner:
            signal(partner_id())
            expected += 1
        pl.semaphore_wait(barrier, expected)


def send_to(device, source, target, send_sem, recv_sem):
    return pltpu.make_async_remote_copy(
        src_ref=source,
        dst_ref=target,
        send_sem=send_sem,
        recv_sem=recv_sem,
        device_id=device,
        device_id_type=MESH_IDS,
    )


def partner_id():
    return {"tensor": 1 - lax.axis_index("tensor")}


def turn_rows(source, target, low=0):
    def one(block, carry):
        here = pl.ds(pl.multiple_of(block * TILE, TILE), TILE)
        there = pl.ds(pl.multiple_of(low + block * TILE, TILE), TILE)
        target[:, there] = jnp.transpose(source[here, :].astype(jnp.float32)).astype(target.dtype)
        return carry

    lax.fori_loop(0, source.shape[0] // TILE, one, 0)


def gather_kernel(shards, *refs):
    (
        gains_ref,
        q_ref,
        k_ref,
        v_ref,
        out_ref,
        gate_ref,
        up_ref,
        down_ref,
        gains_all,
        qkv_all,
        out_all,
        same_shard,
        other_shard,
        qkv_own,
        out_load,
        out_own,
        down_load,
        ffn_own,
        ring_send,
        ring_recv,
        side_send,
        side_recv,
        own_sem,
        load_sem,
    ) = refs
    fulls = (qkv_all, out_all, gains_all)
    locals_ = (qkv_own, out_own, gains_ref)
    kinds = len(fulls)
    ring = Ring(shards)

    loads = []
    low = 0
    for index, ref in enumerate((q_ref, k_ref, v_ref)):
        size = ref.shape[1]
        loads.append(
            pltpu.make_async_copy(ref, qkv_own.at[:, pl.ds(low, size)], load_sem.at[index])
        )
        low += size
    loads.append(pltpu.make_async_copy(out_ref, out_load, load_sem.at[3]))
    loads.append(pltpu.make_async_copy(down_ref, down_load, load_sem.at[4]))
    part = gate_ref.shape[1] // 2
    sets = (ring.row % 2, 1 - ring.row % 2)
    for index, ref in enumerate((gate_ref, up_ref)):
        for which in range(2):
            source = ref.at[:, pl.ds(pl.multiple_of(sets[which] * part, 128), part)]
            target = ffn_own.at[which, :, pl.ds(index * part, part)]
            loads.append(
                pltpu.make_async_copy(source, target, load_sem.at[5 + 2 * index + which])
            )
    for load in loads:
        load.start()
    ring.greet()

    def ring_copy(step, kind, shard, source):
        return send_to(
            {"dp": ring.following},
            source,
            fulls[kind].at[shard],
            ring_send.at[step, kind],
            ring_recv.at[step, kind],
        )

    def side_copy(step, kind, shard, source):
        return send_to(
            {"dp": ring.sibling},
            source,
            fulls[kind].at[shard],
            side_send.at[step, kind],
            side_recv.at[step, kind],
        )

    def own_copy(kind):
        return pltpu.make_async_copy(locals_[kind], fulls[kind].at[ring.me], own_sem.at[kind])

    def begin(kind):
        ring_copy(0, kind, ring.me, locals_[kind]).start()
        side_copy(0, kind, ring.me, locals_[kind]).start()
        own_copy(kind).start()

    for load in loads[:3]:
        load.wait()
    begin(0)
    loads[3].wait()
    turn_rows(out_load, out_own)
    begin(2)
    begin(1)
    loads[4].wait()

    def turn_down(block, carry):
        for which in range(2):
            here = pl.ds(pl.multiple_of(sets[which] * part + block * 128, 128), 128)
            there = pl.ds(pl.multiple_of(2 * part + block * 128, 128), 128)
            piece = jnp.transpose(down_load[here, :].astype(jnp.float32))
            ffn_own[which, :, there] = piece.astype(jnp.bfloat16)
        return carry

    lax.fori_loop(0, part // 128, turn_down, 0)
    for load in loads[5:]:
        load.wait()
    ffn_stores = [
        pltpu.make_async_copy(ffn_own.at[which], target, load_sem.at[9 + which])
        for which, target in enumerate((same_shard, other_shard))
    ]

    def forward(step, carry):
        @pl.when(step == 2)
        def _():
            for store in ffn_stores:
                store.start()

        shard = ring.behind(step)
        for kind in (0, 2, 1):
            here = fulls[kind].at[shard]
            ring_copy(step - 1, kind, shard, here).wait_recv()

            @pl.when(step < ring.count - 1)
            def _():
                ring_copy(step, kind, shard, here).start()

            side_copy(step, kind, shard, here).start()
        return carry

    lax.fori_loop(1, ring.count, forward, 0)

    def drain(step, carry):
        shard = ring.behind(step)
        for kind in range(kinds):
            here = fulls[kind].at[shard]

            @pl.when(step < ring.count - 1)
            def _():
                ring_copy(step, kind, shard, here).wait_send()

            side_copy(step, kind, shard, here).wait_send()
            side_copy(step, kind, shard, here).wait_recv()
        return carry

    lax.fori_loop(0, ring.count, drain, 0)
    for store in ffn_stores:
        store.wait()
    for kind in range(kinds):
        own_copy(kind).wait()


def gather_shards(shards, gains, w_q, w_k, w_v, w_o, w_gate, w_up, w_down):
    steps = shards // 2
    rows = w_q.shape[0]
    columns = w_q.shape[1] + w_k.shape[1] + w_v.shape[1]
    sems = pltpu.SemaphoreType.DMA((steps, 3))
    half = jnp.bfloat16
    return pl.pallas_call(
        functools.partial(gather_kernel, shards),
        out_shape=(
            jax.ShapeDtypeStruct((shards,) + gains.shape, gains.dtype),
            jax.ShapeDtypeStruct((shards, rows, columns), half),
            jax.ShapeDtypeStruct((shards, rows, w_o.shape[0]), half),
            jax.ShapeDtypeStruct((rows, 3 * w_down.shape[0] // 2), half),
            jax.ShapeDtypeStruct((rows, 3 * w_down.shape[0] // 2), half),
        ),
        in_specs=[VMEM_SPEC] + [ANY_SPEC] * 7,
        out_specs=(ANY_SPEC,) * 5,
        scratch_shapes=[
            pltpu.VMEM((rows, columns), half),
            pltpu.VMEM(w_o.shape, half),
            pltpu.VMEM((rows, w_o.shape[0]), half),
            pltpu.VMEM(w_down.shape, half),
            pltpu.VMEM((2, rows, 3 * w_down.shape[0] // 2), half),
            sems,
            sems,
            sems,
            sems,
            pltpu.SemaphoreType.DMA((3,)),
            pltpu.SemaphoreType.DMA((11,)),
        ],
        compiler_params=pltpu.CompilerParams(
            collective_id=0, has_side_effects=True, vmem_limit_bytes=VMEM_BYTES
        ),
        name="gather_attention",
    )(gains, w_q, w_k, w_v, w_o, w_gate, w_up, w_down)


def turn_left(ring, left_all, target, shard):
    rows = left_all.shape[1] // ring.shards
    base = pl.multiple_of(shard * rows // 128 * 128, 128)
    block = left_all[:, pl.ds(base, 128)].astype(jnp.float32)
    target[...] = jnp.transpose(block).astype(jnp.bfloat16)


def shard_terms(turned, right_all, low, size, shard, rows):
    if rows % 128 == 0:
        left = turned[...]
    else:
        first = shard * rows % 128
        left = turned[pl.ds(pl.multiple_of(first, rows), rows), :]
    return matmul(left, right_all[:, low : low + size])


def cut_columns(pairs, widths, limit, least):
    chunks = []
    target = 0
    for left, right in pairs:
        width = widths[right]
        low = 0
        while low < width:
            size = min(limit, width - low)
            if width - low - size < least:
                size = width - low
            chunks.append((left, right, low, size, target))
            low += size
            target += size
    return tuple(chunks), target


FFN_PAIRS = ((1, 2), (0, 0), (0, 1))
HEAD_PAIRS = ((2, 3), (3, 4))


def ffn_chunks_of(units):
    return cut_columns(FFN_PAIRS, (units,) * 3, 768, 384)


def early_columns(chunks):
    return chunks[len(chunks) // 2][4]


def ffn_kernel(shards, groups, chunks, *refs):
    (
        x_ref,
        part_ref,
        gain_ref,
        grad_ref,
        same_ref,
        below_ref,
        above_ref,
        across_ref,
        hidden_ref,
        norm_part_ref,
        norm_other_ref,
        out_own_ref,
        out_pair_ref,
        partial_ref,
        sum_early_ref,
        sum_late_ref,
        normed_out,
        grad_out,
        d_gate_out,
        d_up_out,
        act_out,
    ) = refs[:21]
    count = len(groups)
    full = refs[21 : 21 + count]
    (
        part_other,
        out_total,
        norm_total,
        normed_all,
        grad_all,
        d_gate_all,
        d_up_all,
        act_all,
        turned,
        pair_send_buf,
        pair_recv_buf,
        across_send_buf,
        across_recv_buf,
        far_send,
        far_recv,
        across_send,
        across_recv,
        side_send,
        side_recv,
        own_sem,
        part_send,
        part_recv,
        load_sem,
        normed_send,
        normed_recv,
        pair_send,
        pair_recv,
        norm_send,
        norm_recv,
        left_sem,
        right_send,
        right_recv,
        sum_send,
        sum_recv,
        store_sem,
    ) = refs[21 + count :]
    tokens, depth = part_ref.shape
    rows, units = same_ref.shape
    units //= 3
    blocks = depth // TILE
    early = early_columns(chunks)
    ring = Ring(shards)
    line = ring.rows
    row, side = ring.row, ring.side
    pair = {"dp": ring.at(row + 1 - 2 * (row % 2), side)}
    across = {"dp": ring.at(row, 1 - side)}
    base = ring.core * (2 * tokens)
    mine = pl.ds(pl.multiple_of(base, 2 * tokens), 2 * tokens)
    has_far = (row + 2 < line, row >= 2)
    far = ({"dp": ring.at(row + 2, side)}, {"dp": ring.at(row - 2, side)})

    def half_rows(half):
        return pl.ds(pl.multiple_of(base + half * tokens, tokens), tokens)

    x_load = pltpu.make_async_copy(x_ref, hidden_ref, load_sem.at[0])
    grad_load = pltpu.make_async_copy(grad_ref, grad_all.at[half_rows(0)], load_sem.at[1])
    x_load.start()
    grad_load.start()
    barrier = pltpu.get_barrier_semaphore()

    def greet(device):
        pl.semaphore_signal(barrier, inc=1, device_id=device, device_id_type=MESH_IDS)

    for device in (pair, across, {"dp": ring.sibling}, partner_id()):
        greet(device)
    for way in range(2):

        @pl.when(has_far[way])
        def _():
            greet(far[way])

    pl.semaphore_wait(
        barrier, 4 + has_far[0].astype(jnp.int32) + has_far[1].astype(jnp.int32)
    )

    def place(group, kind, shard):
        return full[group].at[kind, pl.ds(pl.multiple_of(shard * rows, rows), rows)]

    def cut(ref, group, kind):
        low, size = groups[group]
        return ref.at[:, pl.ds(kind * units + low, size)]

    def far_copy(group, way, distance, kind, shard, source):
        return send_to(
            far[way],
            source,
            place(group, kind, shard),
            far_send.at[group, way, distance - 2, kind],
            far_recv.at[group, way, distance - 2, kind],
        )

    def across_copy(group, source_row, kind, shard, source):
        return send_to(
            across,
            source,
            place(group, kind, shard),
            across_send.at[group, source_row, kind],
            across_recv.at[group, source_row, kind],
        )

    def side_copy(group, index, kind, shard, source):
        return send_to(
            {"dp": ring.sibling},
            source,
            place(group, kind, shard),
            side_send.at[group, index, kind],
            side_recv.at[group, index, kind],
        )

    def own_copy(group, which, kind):
        source, shard = (
            (same_ref, ring.me),
            (below_ref, ring.at(row - 1, side)),
            (above_ref, ring.at(row + 1, side)),
            (across_ref, ring.at(row, 1 - side)),
        )[which]
        return pltpu.make_async_copy(
            cut(source, group, kind), place(group, kind, shard), own_sem.at[group, which, kind]
        )

    has_near = (row >= 1, row + 1 < line)

    def begin(group):
        for kind in range(3):
            source = cut(same_ref, group, kind)
            for way in range(2):

                @pl.when(has_far[way])
                def _():
                    far_copy(group, way, 2, kind, ring.me, source).start()

            own_copy(group, 0, kind).start()
            side_copy(group, row, kind, ring.me, source).start()
            for way, near in enumerate((below_ref, above_ref)):
                near_row = row - 1 + 2 * way
                shard = ring.at(near_row, side)

                @pl.when(has_near[way])
                def _():
                    here = cut(near, group, kind)

                    @pl.when(has_far[way])
                    def _():
                        far_copy(group, way, 3, kind, shard, here).start()

                    across_copy(group, near_row, kind, shard, here).start()
                    own_copy(group, 1 + way, kind).start()
                    side_copy(group, near_row, kind, shard, here).start()

            own_copy(group, 3, kind).start()
            side_copy(
                group, line + row, kind, ring.at(row, 1 - side), cut(across_ref, group, kind)
            ).start()

    events = 4 * (line - 1) - 2
    ticks = 3 * events

    def forward(group, tick):
        event = tick // 3 + 2
        kind = tick % 3
        distance = 1 + event // 4
        what = event % 4
        for way in range(2):
            source_row = row - distance * (1 - 2 * way)
            reachable = (source_row >= 0) & (source_row < line)

            @pl.when(reachable & (what == way))
            def _():
                shard = ring.at(source_row, side)
                here = place(group, kind, shard)
                far_copy(group, way, distance, kind, shard, here).wait_recv()

                @pl.when(has_far[way])
                def _():
                    far_copy(group, way, distance + 2, kind, shard, here).start()

                across_copy(group, source_row, kind, shard, here).start()
                side_copy(group, source_row, kind, shard, here).start()

            @pl.when(reachable & (what == 2 + way))
            def _():
                shard = ring.at(source_row, 1 - side)
                here = place(group, kind, shard)
                across_copy(group, source_row, kind, shard, here).wait_recv()
                side_copy(group, line + source_row, kind, shard, here).start()

        if group + 1 < count:

            @pl.when(tick == ticks - 12)
            def _():
                begin(group + 1)

    def arrived(group):
        for kind in range(3):
            for which in (0, 3):
                own_copy(group, which, kind).wait()
            for way in range(2):

                @pl.when(has_near[way])
                def _():
                    own_copy(group, 1 + way, kind).wait()

        def one(index, carry):
            for kind in range(3):
                here = place(group, kind, ring.me)
                side_copy(group, index, kind, ring.me, here).wait_recv()
            return carry

        lax.fori_loop(0, 2 * line, one, 0)

    def drain(group):
        def sides(index, carry):
            for kind in range(3):
                here = place(group, kind, ring.me)
                side_copy(group, index, kind, ring.me, here).wait_send()
            return carry

        def columns(source_row, carry):
            for kind in range(3):
                here = place(group, kind, ring.me)

                @pl.when(source_row != row)
                def _():
                    across_copy(group, source_row, kind, ring.me, here).wait_send()

            return carry

        def distances(distance, carry):
            reach = (row + 2, line + 1 - row)
            for way in range(2):

                @pl.when(has_far[way] & (distance <= reach[way]))
                def _():
                    for kind in range(3):
                        here = place(group, kind, ring.me)
                        far_copy(group, way, distance, kind, ring.me, here).wait_send()

            return carry

        lax.fori_loop(0, 2 * line, sides, 0)
        lax.fori_loop(0, line, columns, 0)
        lax.fori_loop(2, line, distances, 0)

    lefts = (normed_all, grad_all)
    rights = (d_gate_all, d_up_all, act_all)

    def left_copy(index):
        here = lefts[index].at[mine]
        return send_to(
            {"dp": ring.sibling}, here, here, left_sem.at[0, index], left_sem.at[1, index]
        )

    def right_copy(group, half, index):
        low, size = groups[group]
        here = rights[index].at[half_rows(half), pl.ds(low, size)]
        return send_to(
            {"dp": ring.sibling},
            here,
            here,
            right_send.at[group, half, index],
            right_recv.at[group, half, index],
        )

    def share_rights(group, half):
        for index in range(3):
            right_copy(group, half, index).start()

    def tile_of(group):
        return TILE if groups[group][1] % TILE == 0 else TILE // 2

    def hidden_units(group, tile, half):
        low, _ = groups[group]
        wide = tile_of(group)
        here = half_rows(half)
        part = pl.ds(pl.multiple_of(tile * wide, wide), wide)
        target = pl.ds(pl.multiple_of(low + tile * wide, 128), wide)
        gate_pre = matmul(normed_all[here, :], full[group][0, :, part])
        up_pre = matmul(normed_all[here, :], full[group][1, :, part])
        d_act = matmul(grad_all[here, :], full[group][2, :, part])
        sigmoid_gate = jax.nn.sigmoid(gate_pre)
        silu_gate = gate_pre * sigmoid_gate
        act_all[here, target] = (silu_gate * up_pre).astype(jnp.bfloat16)
        d_gate_all[here, target] = (
            d_act * up_pre * sigmoid_gate * (1.0 + gate_pre * (1.0 - sigmoid_gate))
        ).astype(jnp.bfloat16)
        d_up_all[here, target] = (d_act * silu_gate).astype(jnp.bfloat16)

    def feature_block(block):
        if isinstance(block, int):
            return slice(block * TILE, (block + 1) * TILE)
        return pl.ds(pl.multiple_of(block * TILE, TILE), TILE)

    def norm_terms(group, block, here):
        low, size = groups[group]
        cols = slice(low, low + size)
        features = feature_block(block)
        return matmul_nt(d_gate_all[here, cols], full[group][0, features, :]) + matmul_nt(
            d_up_all[here, cols], full[group][1, features, :]
        )

    def out_terms(group, block, here):
        low, size = groups[group]
        features = feature_block(block)
        return matmul_nt(act_all[here, low : low + size], full[group][2, features, :])

    def accumulate(group, block):
        features = feature_block(block)
        norm_new = norm_terms(group, block, half_rows(0))
        out_new = out_terms(group, block, half_rows(0))
        if group > 0:
            norm_new += norm_total[:, features]
            out_new += out_total[:, features]
        norm_total[:, features] = norm_new
        out_total[:, features] = out_new

    quarter = tokens // 4

    def part_copy(piece):
        here = pl.ds(piece * quarter, quarter)
        return send_to(
            partner_id(),
            part_ref.at[here],
            part_other.at[here],
            part_send.at[piece],
            part_recv.at[piece],
        )

    def normed_copy(piece):
        here = pl.ds(pl.multiple_of(base + piece * quarter, quarter), quarter)
        there = pl.ds(pl.multiple_of(base + tokens + piece * quarter, quarter), quarter)
        return send_to(
            pair,
            normed_all.at[here],
            normed_all.at[there],
            normed_send.at[piece],
            normed_recv.at[piece],
        )

    grad_copy = send_to(
        pair,
        grad_all.at[half_rows(0)],
        grad_all.at[half_rows(1)],
        load_sem.at[2],
        load_sem.at[3],
    )

    for piece in range(4):
        part_copy(piece).start()
    begin(0)
    x_load.wait()
    grad_load.wait()

    def norm_rows(piece):
        part_copy(piece).wait_recv()

        def one(block, carry):
            first = piece * quarter + block * 32
            here = pl.ds(pl.multiple_of(first, 32), 32)
            there = pl.ds(pl.multiple_of(base + first, 32), 32)
            hidden = hidden_ref[here, :] + (
                part_ref[here, :].astype(jnp.float32) + part_other[here, :].astype(jnp.float32)
            )
            hidden_ref[here, :] = hidden
            _, norm_two = rms_parts(hidden)
            normed_all[there, :] = (norm_two * gain_ref[...]).astype(jnp.bfloat16)
            return carry

        lax.fori_loop(0, quarter // 32, one, 0)

    pause = ticks // 4

    def first_ticks(tick, carry):
        forward(0, tick)
        for piece in range(4):

            @pl.when(tick == pause * (piece + 1))
            def _():
                norm_rows(piece)
                if piece > 0:
                    normed_copy(piece - 1).start()

        return carry

    grad_copy.start()
    lax.fori_loop(0, ticks, first_ticks, 0)
    arrived(0)
    normed_copy(3).start()

    first_tiles = groups[0][1] // tile_of(0)

    def wait_pair():
        for piece in range(4):
            normed_copy(piece).wait_recv()
        grad_copy.wait_recv()

    for group in range(1, count):
        before = group - 1
        tiles = groups[before][1] // tile_of(before)
        if group > 1:
            arrived(before)

        later = ticks - 10

        def tick_and_work(tick, carry):
            forward(group, tick)

            @pl.when(tick < tiles)
            def _():
                hidden_units(before, tick, 0)

            block = tick - tiles

            @pl.when(block == 0)
            def _():
                share_rights(before, 0)

            @pl.when((block >= 0) & (block < blocks))
            def _():
                accumulate(before, block)

            if group == count - 1:

                @pl.when(tick == later)
                def _():
                    wait_pair()

                @pl.when((tick >= later) & (tick < later + first_tiles))
                def _():
                    hidden_units(0, tick - later, 1)

            return carry

        lax.fori_loop(0, ticks, tick_and_work, 0)

    last = count - 1
    share_rights(0, 1)
    for index in range(2):
        left_copy(index).start()

    def loop_units(group, half):
        def one(tile, carry):
            hidden_units(group, tile, half)
            return carry

        lax.fori_loop(0, groups[group][1] // tile_of(group), one, 0)
        share_rights(group, half)

    for group in range(1, last):
        loop_units(group, 1)
    arrived(last)
    loop_units(last, 1)

    def pair_copy(block):
        features = pl.ds(pl.multiple_of(block * TILE, TILE), TILE)
        return send_to(
            pair,
            pair_send_buf.at[:, features],
            pair_recv_buf.at[:, features],
            pair_send.at[block],
            pair_recv.at[block],
        )

    def pair_norm(block, carry):
        features = feature_block(block)
        total = norm_terms(0, block, half_rows(1))
        for group in range(1, count):
            total += norm_terms(group, block, half_rows(1))
        pair_send_buf[:, features] = total.astype(jnp.bfloat16)

        @pl.when(block > 0)
        def _():
            pair_copy(block - 1).start()

        return carry

    lax.fori_loop(0, blocks, pair_norm, 0)
    loop_units(last, 0)
    pair_copy(blocks - 1).start()

    def norm_copy(block):
        features = pl.ds(block * TILE, TILE)
        return send_to(
            partner_id(),
            norm_part_ref.at[:, features],
            norm_other_ref.at[:, features],
            norm_send.at[block],
            norm_recv.at[block],
        )

    def turn(shard):
        for index in range(2):
            turn_left(ring, lefts[index], turned.at[index], shard)

    def terms(chunk, shard):
        left, right, low, size, _ = chunks[chunk]
        return shard_terms(turned.at[left], rights[right], low, size, shard, rows)

    def sum_copy(chunk):
        _, _, _, size, target = chunks[chunk]
        columns = pl.ds(target, size)
        return send_to(
            across,
            across_send_buf.at[:, columns],
            across_recv_buf.at[:, columns],
            sum_send.at[chunk],
            sum_recv.at[chunk],
        )

    for index in range(2):
        left_copy(index).wait_recv()
    for group in range(count):
        for half in range(2):
            for index in range(3):
                right_copy(group, half, index).wait_recv()
    outs = (normed_out, grad_out, d_gate_out, d_up_out, act_out)
    stores = [
        pltpu.make_async_copy(source, target, store_sem.at[index])
        for index, (source, target) in enumerate(zip(lefts + rights, outs))
    ]
    for store in stores:
        store.start()

    first_owner = row + ring.owner(0)
    second_owner = row + ring.owner(1)
    shard = ring.at(first_owner, 1 - side)
    turn(shard)
    for block in range(max(blocks, len(chunks))):
        if block < len(chunks):
            _, _, _, size, target = chunks[block]
            across_send_buf[:, target : target + size] = terms(block, shard).astype(jnp.bfloat16)
            if block > 0:
                sum_copy(block - 1).start()
        if block < blocks:
            features = feature_block(block)
            total = norm_total[0:tokens, features] + norm_terms(last, block, half_rows(0))
            pair_copy(block).wait_recv()
            total += pair_recv_buf[:, features].astype(jnp.float32)
            norm_part_ref[:, features] = total.astype(jnp.bfloat16)
            if block > 0:
                norm_copy(block - 1).start()
    sum_copy(len(chunks) - 1).start()

    def last_out(block, carry):
        features = feature_block(block)
        total = out_total[:, features] + out_terms(last, block, half_rows(0))
        out_own_ref[:, features] = total.astype(jnp.bfloat16)
        total = out_terms(0, block, half_rows(1))
        for group in range(1, count):
            total += out_terms(group, block, half_rows(1))
        out_pair_ref[:, features] = total.astype(jnp.bfloat16)
        return carry

    lax.fori_loop(0, blocks, last_out, 0)
    norm_copy(blocks - 1).start()
    shard = ring.at(second_owner, 1 - side)
    turn(shard)
    for chunk in range(len(chunks)):
        _, _, _, size, target = chunks[chunk]
        partial_ref[:, target : target + size] = terms(chunk, shard).astype(jnp.bfloat16)
    shard = ring.at(first_owner, side)
    turn(shard)
    for chunk in range(len(chunks)):
        _, _, _, size, target = chunks[chunk]
        total = terms(chunk, shard)
        sum_copy(chunk).wait_recv()
        total += across_recv_buf[:, target : target + size].astype(jnp.float32)
        if target < early:
            sum_early_ref[:, target : target + size] = total.astype(jnp.bfloat16)
        else:
            at = target - early
            sum_late_ref[:, at : at + size] = total.astype(jnp.bfloat16)

    for group in range(count):
        drain(group)
    for piece in range(4):
        part_copy(piece).wait_send()
        normed_copy(piece).wait_send()
    grad_copy.wait_send()
    for index in range(2):
        left_copy(index).wait_send()
    for group in range(count):
        for half in range(2):
            for index in range(3):
                right_copy(group, half, index).wait_send()
    for chunk in range(len(chunks)):
        sum_copy(chunk).wait_send()
    for block in range(blocks):
        pair_copy(block).wait_send()
    for store in stores:
        store.wait()
    for block in range(blocks):
        norm_copy(block).wait()


def ffn_groups(units):
    tiles = units // 128
    last = 2
    second = (tiles - last) // 4 * 2
    sizes = [tiles - last - second, second, last]
    groups = []
    low = 0
    for size in sizes:
        groups.append((low * 128, size * 128))
        low += size
    return tuple(groups)


def ffn_pass(shards, x_rows, part, gain, grad_rows, pieces):
    tokens, depth = x_rows.shape
    rows, units = pieces[0].shape
    units //= 3
    line = shards // 4
    groups = ffn_groups(units)
    chunks, total = ffn_chunks_of(units)
    half = jnp.bfloat16
    dma = pltpu.SemaphoreType.DMA
    wide = jax.ShapeDtypeStruct((tokens, depth), half)
    all_wide = (4 * tokens, depth)
    all_inner = (4 * tokens, units)
    blocks = depth // TILE
    full = [pltpu.VMEM((3, depth, size), half) for _, size in groups]
    return pl.pallas_call(
        functools.partial(ffn_kernel, shards, groups, chunks),
        out_shape=(
            jax.ShapeDtypeStruct((tokens, depth), jnp.float32),
            wide,
            wide,
            wide,
            wide,
            jax.ShapeDtypeStruct((rows, total), half),
            jax.ShapeDtypeStruct((rows, early_columns(chunks)), half),
            jax.ShapeDtypeStruct((rows, total - early_columns(chunks)), half),
            jax.ShapeDtypeStruct(all_wide, half),
            jax.ShapeDtypeStruct(all_wide, half),
            jax.ShapeDtypeStruct(all_inner, half),
            jax.ShapeDtypeStruct(all_inner, half),
            jax.ShapeDtypeStruct(all_inner, half),
        ),
        in_specs=[ANY_SPEC, VMEM_SPEC, VMEM_SPEC] + [ANY_SPEC] * 5,
        out_specs=(VMEM_SPEC,) * 8 + (ANY_SPEC,) * 5,
        scratch_shapes=full
        + [
            pltpu.VMEM((tokens, depth), half),
            pltpu.VMEM((tokens, depth), jnp.float32),
            pltpu.VMEM((tokens, depth), jnp.float32),
            pltpu.VMEM(all_wide, half),
            pltpu.VMEM(all_wide, half),
            pltpu.VMEM(all_inner, half),
            pltpu.VMEM(all_inner, half),
            pltpu.VMEM(all_inner, half),
            pltpu.VMEM((2, 128, 4 * tokens), half),
            pltpu.VMEM((tokens, depth), half),
            pltpu.VMEM((tokens, depth), half),
            pltpu.VMEM((rows, total), half),
            pltpu.VMEM((rows, total), half),
            dma((len(groups), 2, line - 2, 3)),
            dma((len(groups), 2, line - 2, 3)),
            dma((len(groups), line, 3)),
            dma((len(groups), line, 3)),
            dma((len(groups), 2 * line, 3)),
            dma((len(groups), 2 * line, 3)),
            dma((len(groups), 4, 3)),
            dma((4,)),
            dma((4,)),
            dma((4,)),
            dma((4,)),
            dma((4,)),
            dma((blocks,)),
            dma((blocks,)),
            dma((blocks,)),
            dma((blocks,)),
            dma((2, 2)),
            dma((len(groups), 2, 3)),
            dma((len(groups), 2, 3)),
            dma((len(chunks),)),
            dma((len(chunks),)),
            dma((5,)),
        ],
        compiler_params=pltpu.CompilerParams(
            collective_id=1, has_side_effects=True, vmem_limit_bytes=VMEM_BYTES
        ),
        name="ffn_pairs",
    )(x_rows, part, gain, grad_rows, *pieces)


def reduce_kernel(shards, ffn_chunks, head_chunks, *refs):
    (
        normed_two_ref,
        grad_ref,
        hidden_rows_ref,
        normed_one_ref,
        d_gate_ref,
        d_up_ref,
        act_ref,
        attended_ref,
        d_qkv_ref,
        across_ref,
        sum_ref,
        up_ref,
        down_ref,
        out_part_ref,
        out_pair_ref,
        norm_part_ref,
        hidden_ref,
        d_hidden_ref,
        scaled_ref,
        inv_ref,
        gain_ref,
        sums_ref,
        layer_out,
        x_grad_out,
        gate_grad,
        up_grad,
        down_grad,
        o_grad,
        qkv_grad,
        sums_out,
        normed_two_all,
        grad_all,
        hidden_rows_all,
        normed_one_all,
        d_gate_all,
        d_up_all,
        act_all,
        attended_all,
        d_qkv_all,
        ffn_turned,
        head_turned,
        total_buf,
        partials,
        across_in,
        ffn_sums,
        relay,
        other_in,
        head_slots,
        norm_here,
        norm_there,
        out_here,
        out_pair,
        out_there,
        hidden_buf,
        d_hidden_buf,
        scaled_buf,
        column_total,
        sums_own,
        sums_in,
        across_send,
        across_recv,
        sum_send,
        relay_recv,
        other_recv,
        head_send,
        head_recv,
        load_sem,
        side_send,
        side_recv,
        part_sem,
        row_sem,
        sums_send,
        sums_recv,
    ) = refs
    ring = Ring(shards)
    line = ring.rows
    row, side = ring.row, ring.side
    tokens, depth = out_part_ref.shape
    rows = head_slots.shape[1]
    mine = pl.ds(pl.multiple_of(ring.core * tokens, tokens), tokens)
    rights = (d_gate_all, d_up_all, act_all, attended_all, d_qkv_all)
    heads = len(head_chunks)
    ffns = len(ffn_chunks)
    early = early_columns(ffn_chunks)

    head_pairs = (
        (hidden_rows_ref, hidden_rows_all),
        (attended_ref, attended_all),
        (normed_one_ref, normed_one_all),
        (d_qkv_ref, d_qkv_all),
    )
    head_loads = [
        pltpu.make_async_copy(source, target.at[mine], load_sem.at[index])
        for index, (source, target) in enumerate(head_pairs)
    ]
    ffn_loads = [
        pltpu.make_async_copy(source, target, load_sem.at[4 + index])
        for index, (source, target) in enumerate(
            (
                (sum_ref, ffn_sums.at[0, :, pl.ds(early, sum_ref.shape[1])]),
                (grad_ref, grad_all),
                (act_ref, act_all),
                (normed_two_ref, normed_two_all),
                (d_gate_ref, d_gate_all),
                (d_up_ref, d_up_all),
                (across_ref, across_in.at[0]),
            )
        )
    ]
    row_loads = [
        pltpu.make_async_copy(source, target, row_sem.at[index])
        for index, (source, target) in enumerate(
            (
                (norm_part_ref, norm_here),
                (d_hidden_ref, d_hidden_buf),
                (scaled_ref, scaled_buf),
                (out_part_ref, out_here),
                (hidden_ref, hidden_buf),
            )
        )
    ]
    half_line = line // 2
    preloaded = (
        (row >= 2) & (row - 2 < half_line),
        (row + 2 < line) & (row + 2 >= half_line),
    )
    early_at = (line - 1 - row, row)
    early_loads = [
        pltpu.make_async_copy(
            source,
            relay.at[way, jnp.minimum(early_at[way], line - 3), :, pl.ds(0, early)],
            load_sem.at[11 + way],
        )
        for way, source in enumerate((up_ref, down_ref))
    ]
    for load in head_loads + ffn_loads[:1]:
        load.start()
    for way in range(2):

        @pl.when(preloaded[way])
        def _():
            early_loads[way].start()

    for load in ffn_loads[1:] + row_loads:
        load.start()
    ring.greet(partner=True, everyone=True)
    sides = [
        send_to(
            {"dp": ring.sibling}, source, target.at[mine], side_send.at[index], side_recv.at[index]
        )
        for index, (source, target) in enumerate(head_pairs)
    ]
    for copy in sides:
        copy.start()
    norm_copy = send_to(partner_id(), norm_part_ref, norm_there, part_sem.at[0], part_sem.at[1])
    out_copy = send_to(partner_id(), out_here, out_there, part_sem.at[2], part_sem.at[3])
    pair_copy = send_to(
        {"dp": ring.at(row + 1 - 2 * (row % 2), side)},
        out_pair_ref,
        out_pair,
        part_sem.at[4],
        part_sem.at[5],
    )
    norm_copy.start()

    def columns_of(chunk):
        _, _, _, size, target = ffn_chunks[chunk]
        return pl.ds(target, size)

    def across_copy(slot, chunk):
        columns = columns_of(chunk)
        return send_to(
            {"dp": ring.at(row, 1 - side)},
            partials.at[slot % 2, :, columns],
            across_in.at[slot - 1, :, columns],
            across_send.at[slot, chunk],
            across_recv.at[slot, chunk],
        )

    def near_copy(slot, way, chunk):
        columns = columns_of(chunk)
        return send_to(
            {"dp": ring.at(row + 1 - 2 * way, side)},
            ffn_sums.at[slot, :, columns],
            other_in.at[way, :, columns],
            sum_send.at[slot, chunk],
            other_recv.at[way, chunk],
        )

    def far_copy(slot, way, distance, chunk):
        columns = columns_of(chunk)
        return send_to(
            {"dp": ring.at(row + 2 - 4 * way, side)},
            ffn_sums.at[slot, :, columns],
            relay.at[way, distance, :, columns],
            sum_send.at[slot, chunk],
            relay_recv.at[way, distance, chunk],
        )

    def send_sum(slot, chunk):
        offset = ring.owner(slot)
        for way in range(2):
            distance = offset * (1 - 2 * way)

            @pl.when(distance == 1)
            def _():
                near_copy(slot, way, chunk).start()

            @pl.when(distance >= 2)
            def _():
                far_copy(slot, way, distance - 2, chunk).start()

    def head_copy(step, chunk):
        _, _, _, size, target = head_chunks[chunk]
        columns = pl.ds(target, size)
        return send_to(
            {"dp": ring.following},
            head_slots.at[step, :, columns],
            head_slots.at[step + 1, :, columns],
            head_send.at[step, chunk],
            head_recv.at[step, chunk],
        )

    def turn_ffn(shard):
        turn_left(ring, normed_two_all, ffn_turned.at[0], shard)
        turn_left(ring, grad_all, ffn_turned.at[1], shard)

    def turn_head(chip):
        shard = 2 * chip + ring.core
        turn_left(ring, hidden_rows_all, head_turned.at[0], shard)
        turn_left(ring, normed_one_all, head_turned.at[1], shard)

    def head_terms(chunk, chip):
        left, right, low, size, _ = head_chunks[chunk]
        shard = 2 * chip + ring.core
        return shard_terms(head_turned.at[left - 2], rights[right], low, size, shard, rows)

    def ffn_terms(chunk, shard):
        left, right, low, size, _ = ffn_chunks[chunk]
        return shard_terms(ffn_turned.at[left], rights[right], low, size, shard, rows)

    def sums_copy(offset):
        return send_to(
            {"dp": (ring.me + offset) % shards},
            sums_own.at[(ring.me + offset) % shards],
            sums_in.at[ring.me],
            sums_send.at[offset],
            sums_recv.at[offset],
        )

    def finish_input_grad():
        for load in row_loads[:3]:
            load.wait()
        norm_copy.wait()
        sums_own[...] = sums_ref[...]
        column_total[...] = jnp.zeros_like(column_total)

        def one(block, carry):
            here = pl.ds(pl.multiple_of(block * 16, 16), 16)
            total = norm_here[here, :].astype(jnp.float32) + norm_there[here, :].astype(
                jnp.float32
            )
            scaled = scaled_buf[here, :]
            product = total * scaled
            column_total[...] += product[0:8] + product[8:16]
            scaled_gain = total * gain_ref[...]
            mean = jnp.mean(scaled_gain * scaled, axis=-1, keepdims=True)
            d_hidden_buf[here, :] = d_hidden_buf[here, :] + inv_ref[here, :] * (
                scaled_gain - scaled * mean
            )
            return carry

        lax.fori_loop(0, tokens // 16, one, 0)
        width = depth // shards
        band = max(width, 128)
        for low in range(0, depth, band):
            sums = jnp.sum(column_total[:, low : low + band], axis=0, keepdims=True)
            for inner in range(0, band, width):
                sums_own[(low + inner) // width, 1:2, 0:width] = sums[:, inner : inner + width]

    def send_sums():
        pltpu.make_async_copy(d_hidden_buf, x_grad_out, row_sem.at[5]).start()

        def one(offset, carry):
            sums_copy(offset).start()
            return carry

        lax.fori_loop(1, shards, one, 0)

    def join_pair():
        row_loads[3].wait()
        pair_copy.wait_recv()

        def one(block, carry):
            here = pl.ds(pl.multiple_of(block * 16, 16), 16)
            total = out_here[here, :].astype(jnp.float32) + out_pair[here, :].astype(jnp.float32)
            out_here[here, :] = total.astype(jnp.bfloat16)
            return carry

        lax.fori_loop(0, tokens // 16, one, 0)

    def finish_output():
        row_loads[4].wait()
        out_copy.wait_recv()

        def one(block, carry):
            here = pl.ds(pl.multiple_of(block * 16, 16), 16)
            hidden_buf[here, :] = hidden_buf[here, :] + (
                out_here[here, :].astype(jnp.float32) + out_there[here, :].astype(jnp.float32)
            )
            return carry

        lax.fori_loop(0, tokens // 16, one, 0)

    def head_total(step, chip, chunk):
        _, _, _, size, target = head_chunks[chunk]
        total = head_terms(chunk, chip)
        head_copy(step - 1, chunk).wait_recv()
        return total + head_slots[step, :, target : target + size].astype(jnp.float32)

    def head_step(step, chip):
        for chunk in range(heads):
            _, _, _, size, target = head_chunks[chunk]
            head_slots[step, :, target : target + size] = head_total(step, chip, chunk).astype(
                jnp.bfloat16
            )
            if chunk > 0:
                head_copy(step, chunk - 1).start()

    def head_end(step):
        head_copy(step, heads - 1).start()

    def send_partials(slot):
        shard = ring.at(row + ring.owner(slot), 1 - side)
        turn_ffn(shard)
        for chunk in range(ffns):
            _, _, _, size, target = ffn_chunks[chunk]

            @pl.when(slot >= 4)
            def _():
                across_copy(slot - 2, chunk).wait_send()

            partials[slot % 2, :, target : target + size] = ffn_terms(chunk, shard).astype(
                jnp.bfloat16
            )
            if chunk > 0:
                across_copy(slot, chunk - 1).start()

        @pl.when(slot == 2)
        def _():
            pair_copy.start()

    def sum_up(slot, chunk, shard, offset):
        _, _, _, size, target = ffn_chunks[chunk]
        total = ffn_terms(chunk, shard)

        @pl.when(slot >= 2)
        def _():
            across_copy(slot, chunk).wait_recv()

        total_buf[:, 0:size] = total + across_in[slot - 1, :, target : target + size].astype(
            jnp.float32
        )
        for way in range(2):
            distance = offset * (1 - 2 * way)
            source_row = row - 2 + 4 * way

            @pl.when((distance >= 0) & (source_row >= 0) & (source_row < line))
            def _():
                if target < early:

                    @pl.when(jnp.logical_not(preloaded[way] & (distance == early_at[way])))
                    def _():
                        far_copy(0, way, distance, chunk).wait_recv()

                else:
                    far_copy(0, way, distance, chunk).wait_recv()
                total_buf[:, 0:size] += relay[way, distance, :, target : target + size].astype(
                    jnp.float32
                )

    grads = (gate_grad, up_grad, down_grad)
    part = down_grad.shape[0] // 2

    def store_final(chunk, which):
        _, right, low, size, _ = ffn_chunks[chunk]
        first = pl.multiple_of(which * part + low, 128)
        if right == 2:
            down_grad[pl.ds(first, size), :] = jnp.transpose(total_buf[:, 0:size])
        else:
            grads[right][:, pl.ds(first, size)] = total_buf[:, 0:size]

    ffn_loads[0].wait()
    for chunk in range(ffns):
        if ffn_chunks[chunk][4] >= early:
            send_sum(0, chunk)
    for load in head_loads:
        load.wait()
    for copy in sides:
        copy.wait_recv()
    chip = ring.chip(-1)
    turn_head(chip)
    for chunk in range(heads):
        _, _, _, size, target = head_chunks[chunk]
        head_slots[0, :, target : target + size] = head_terms(chunk, chip).astype(jnp.bfloat16)
        if chunk > 0:
            head_copy(0, chunk - 1).start()
    for load in ffn_loads[1:]:
        load.wait()
    for way in range(2):

        @pl.when(preloaded[way])
        def _():
            early_loads[way].wait()

    def one_slot(slot, carry):
        send_partials(slot + 1)

        @pl.when(slot == 1)
        def _():
            head_end(0)

        offset = ring.owner(slot)
        shard = ring.at(row + offset, side)
        turn_ffn(shard)
        across_copy(slot + 1, ffns - 1).start()
        for chunk in range(ffns):
            _, _, _, size, target = ffn_chunks[chunk]
            sum_up(slot, chunk, shard, offset)
            ffn_sums[slot, :, target : target + size] = total_buf[:, 0:size].astype(jnp.bfloat16)
            if chunk > 0:
                send_sum(slot, chunk - 1)
        chip = ring.chip(-2 * slot)
        turn_head(chip)
        send_sum(slot, ffns - 1)
        head_step(2 * slot - 1, chip)
        chip = ring.chip(-1 - 2 * slot)
        turn_head(chip)
        head_end(2 * slot - 1)
        head_step(2 * slot, chip)

        @pl.when(slot == 1)
        def _():
            finish_input_grad()

        head_end(2 * slot)

        @pl.when(slot == 2)
        def _():
            send_sums()
            join_pair()

        return carry

    own = line - 1
    lax.fori_loop(1, own, one_slot, 0)
    out_copy.start()
    final = ring.count - 1
    chip = ring.chip(1 - final)
    turn_head(chip)
    head_step(final - 2, chip)
    shard = ring.at(row, side)
    turn_ffn(shard)
    head_end(final - 2)
    for chunk in range(ffns):
        sum_up(own, chunk, shard, 0)
        store_final(chunk, row % 2)
    chip = ring.chip(-final)
    turn_head(chip)
    head_step(final - 1, chip)
    chip = ring.chip(0)
    turn_head(chip)
    head_end(final - 1)
    finish_output()
    pltpu.make_async_copy(hidden_buf, layer_out, row_sem.at[6]).start()
    for chunk in range(ffns):
        _, _, _, size, target = ffn_chunks[chunk]
        total_buf[...] = jnp.zeros_like(total_buf)
        for way in range(2):
            source_row = row - 1 + 2 * way

            @pl.when((source_row >= 0) & (source_row < line))
            def _():
                near_copy(0, way, chunk).wait_recv()
                total_buf[:, 0:size] += other_in[way, :, target : target + size].astype(
                    jnp.float32
                )

        store_final(chunk, 1 - row % 2)
    for chunk in range(heads):
        _, right, low, size, _ = head_chunks[chunk]
        total = head_total(final, chip, chunk)
        if right == 3:
            o_grad[low : low + size, :] = jnp.transpose(total)
        else:
            qkv_grad[:, low : low + size] = total

    def add_sums(offset, total):
        sums_copy(offset).wait_recv()
        return total + sums_in[(ring.me - offset + shards) % shards]

    sums_out[...] = lax.fori_loop(1, shards, add_sums, sums_own[ring.me])

    def drain_heads(step, carry):
        for chunk in range(heads):
            head_copy(step, chunk).wait_send()
        return carry

    def drain_sums(offset, carry):
        sums_copy(offset).wait_send()
        return carry

    def drain_slots(slot, carry):
        for chunk in range(ffns):
            near_copy(slot, 0, chunk).wait_send()
        return carry

    lax.fori_loop(0, final, drain_heads, 0)
    lax.fori_loop(1, shards, drain_sums, 0)
    lax.fori_loop(1, own, drain_slots, 0)
    for chunk in range(ffns):
        if ffn_chunks[chunk][4] >= early:
            near_copy(0, 0, chunk).wait_send()
        for slot in range(max(2, line - 2), line):
            across_copy(slot, chunk).wait_send()
    for copy in sides:
        copy.wait_send()
    pair_copy.wait_send()
    out_copy.wait_send()
    pltpu.make_async_copy(d_hidden_buf, x_grad_out, row_sem.at[5]).wait()
    pltpu.make_async_copy(hidden_buf, layer_out, row_sem.at[6]).wait()


def reduce_pass(shards, both, heads, travelled, out_part, out_pair, norm_part, rows_f32, inv, gain, sums):
    normed_two, grad_rows, d_gate, d_up, activated = both
    hidden_rows, normed_one, attended, d_qkv = heads
    tokens, depth = out_part.shape
    units = d_gate.shape[1]
    line = shards // 4
    steps = shards // 2
    rows = depth // shards
    widths = (units, units, units, attended.shape[1], d_qkv.shape[1])
    ffn_chunks, ffn_total = ffn_chunks_of(units)
    head_chunks, head_total = cut_columns(HEAD_PAIRS, widths, 1024, 512)
    half = jnp.bfloat16
    wide = jax.ShapeDtypeStruct((tokens, depth), jnp.float32)
    one_half = pltpu.VMEM((tokens, depth), half)
    one_full = pltpu.VMEM((tokens, depth), jnp.float32)
    dma = pltpu.SemaphoreType.DMA
    ffns, heads_count = len(ffn_chunks), len(head_chunks)
    return pl.pallas_call(
        functools.partial(reduce_kernel, shards, ffn_chunks, head_chunks),
        out_shape=(
            wide,
            wide,
            jax.ShapeDtypeStruct((rows, 2 * units), jnp.float32),
            jax.ShapeDtypeStruct((rows, 2 * units), jnp.float32),
            jax.ShapeDtypeStruct((2 * units, rows), jnp.float32),
            jax.ShapeDtypeStruct((attended.shape[1], rows), jnp.float32),
            jax.ShapeDtypeStruct((rows, d_qkv.shape[1]), jnp.float32),
            jax.ShapeDtypeStruct(sums.shape[1:], jnp.float32),
        ),
        in_specs=[ANY_SPEC] * 19 + [VMEM_SPEC] * 3,
        out_specs=(ANY_SPEC, ANY_SPEC) + (VMEM_SPEC,) * 6,
        scratch_shapes=[pltpu.VMEM((4 * tokens, depth), half)] * 2
        + [pltpu.VMEM((2 * tokens, depth), half)] * 2
        + [pltpu.VMEM((4 * tokens, units), half)] * 3
        + [pltpu.VMEM((2 * tokens, width), half) for width in widths[3:]]
        + [
            pltpu.VMEM((2, 128, 4 * tokens), half),
            pltpu.VMEM((2, 128, 2 * tokens), half),
            pltpu.VMEM((rows, max(chunk[3] for chunk in ffn_chunks)), jnp.float32),
            pltpu.VMEM((2, rows, ffn_total), half),
            pltpu.VMEM((line - 1, rows, ffn_total), half),
            pltpu.VMEM((line - 1, rows, ffn_total), half),
            pltpu.VMEM((2, line - 2, rows, ffn_total), half),
            pltpu.VMEM((2, rows, ffn_total), half),
            pltpu.VMEM((steps, rows, head_total), half),
            one_half,
            one_half,
            one_half,
            one_half,
            one_half,
            one_full,
            one_full,
            one_full,
            pltpu.VMEM((8, depth), jnp.float32),
            pltpu.VMEM(sums.shape, jnp.float32),
            pltpu.VMEM(sums.shape, jnp.float32),
            dma((line, ffns)),
            dma((line, ffns)),
            dma((line, ffns)),
            dma((2, line - 2, ffns)),
            dma((2, ffns)),
            dma((steps - 1, heads_count)),
            dma((steps - 1, heads_count)),
            dma((13,)),
            dma((4,)),
            dma((4,)),
            dma((6,)),
            dma((7,)),
            dma((shards,)),
            dma((shards,)),
        ],
        compiler_params=pltpu.CompilerParams(
            collective_id=2, has_side_effects=True, vmem_limit_bytes=VMEM_BYTES
        ),
        name="reduce_pairs",
    )(
        normed_two,
        grad_rows,
        hidden_rows,
        normed_one,
        d_gate,
        d_up,
        activated,
        attended,
        d_qkv,
        *travelled,
        out_part,
        out_pair,
        norm_part,
        *rows_f32,
        inv,
        gain,
        sums,
    )


def emit_kernel(cuts, *refs):
    ins = refs[: len(cuts)]
    count = sum(len(cut) for cut in cuts)
    outs = refs[len(cuts) : len(cuts) + count]
    sums_ref, sums_one, sums_two = refs[len(cuts) + count : len(cuts) + count + 3]
    bufs = refs[len(cuts) + count + 3 : -2]
    load_sem, store_sem = refs[-2:]
    loads = [
        pltpu.make_async_copy(source, buf, load_sem.at[index])
        for index, (source, buf) in enumerate(zip(ins, bufs))
    ]
    for load in loads:
        load.start()
    stores = []
    for index, cut in enumerate(cuts):
        loads[index].wait()
        for low, size in cut:
            at = len(stores)
            source = bufs[index] if len(cut) == 1 else bufs[index].at[:, pl.ds(low, size)]
            stores.append(pltpu.make_async_copy(source, outs[at], store_sem.at[at]))
            stores[-1].start()
    sums_one[...] = sums_ref[1, : sums_one.shape[0]]
    sums_two[...] = sums_ref[0, : sums_two.shape[0]]
    for store in stores:
        store.wait()


def emit(arrays, cuts, sums, rows):
    outs = []
    for array, cut in zip(arrays, cuts):
        for _, size in cut:
            outs.append(jax.ShapeDtypeStruct((array.shape[0], size), array.dtype))
    count = len(outs)
    line = jax.ShapeDtypeStruct((rows,), jnp.float32)

    def kernel(*refs):
        ins = refs[: len(arrays)]
        sums_ref = refs[len(arrays)]
        rest = refs[len(arrays) + 1 :]
        emit_kernel(
            cuts, *ins, *rest[:count], sums_ref, rest[count], rest[count + 1], *rest[count + 2 :]
        )

    return pl.pallas_call(
        kernel,
        out_shape=tuple(outs) + (line, line),
        in_specs=[ANY_SPEC] * len(arrays) + [VMEM_SPEC],
        out_specs=(ANY_SPEC,) * count + (VMEM_SPEC, VMEM_SPEC),
        scratch_shapes=[pltpu.VMEM(array.shape, array.dtype) for array in arrays]
        + [pltpu.SemaphoreType.DMA((len(arrays),)), pltpu.SemaphoreType.DMA((count,))],
        compiler_params=pltpu.CompilerParams(vmem_limit_bytes=VMEM_BYTES),
        name="emit_results",
    )(*arrays, sums)


def device_pairs(shards, move):
    line = shards // 4
    pairs = []
    for shard in range(shards):
        chip, core = divmod(shard, 2)
        target = move(*divmod(chip, 2))
        if target is not None and 0 <= target[0] < line:
            pairs.append((shard, (2 * target[0] + target[1]) * 2 + core))
    return pairs


def body(
    shards,
    layer_input,
    positions,
    norm1_gain,
    w_q,
    w_k,
    w_v,
    w_o,
    norm2_gain,
    w_gate,
    w_up,
    w_down,
    out_grad,
):
    tokens, depth = layer_input.shape
    rows = w_q.shape[0]
    head_count = w_q.shape[1] // HD
    kv_count = w_k.shape[1] // HD
    query_cols = head_count * HD
    kv_cols = kv_count * HD

    def hop(value, move):
        return lax.ppermute(value, "dp", device_pairs(shards, move))

    half_line = shards // 8

    gains = jnp.stack([norm1_gain, norm2_gain]).astype(jnp.float32)
    gains = jnp.pad(gains, ((0, 6), (0, max(128 - rows, 0))))
    gains_all, qkv_all, out_all, same, other = gather_shards(
        shards, gains, w_q, w_k, w_v, w_o, w_gate, w_up, w_down
    )
    gain_one = gains_all[:, 0, :rows].reshape(1, depth)
    gain_two = gains_all[:, 1, :rows].reshape(1, depth)
    qkv_w = qkv_all.reshape(depth, query_cols + 2 * kv_cols)
    out_w = out_all.reshape(depth, query_cols)
    below = hop(other, lambda row, side: (row + 1, side))
    above = hop(other, lambda row, side: (row - 1, side))
    across = hop(same, lambda row, side: (row, 1 - side))

    inv_one, norm_one = rms_parts(layer_input)
    normed_one = (norm_one * gain_one).astype(jnp.bfloat16)
    cos_table, sin_table = rope_tables(positions, HD)
    qkv = matmul(normed_one, qkv_w)
    queries = rotate(
        qkv[:, :query_cols].reshape(tokens, head_count, HD), cos_table, sin_table, 1.0
    ).astype(jnp.bfloat16)
    key_rows = rotate(
        qkv[:, query_cols : query_cols + kv_cols].reshape(tokens, kv_count, HD),
        cos_table,
        sin_table,
        1.0,
    ).astype(jnp.bfloat16)
    value_rows = qkv[:, query_cols + kv_cols :].astype(jnp.bfloat16).reshape(tokens, kv_count, HD)
    seq_count = tokens // L
    query_seq = queries.reshape(seq_count, L, head_count, HD)
    key_seq = key_rows.reshape(seq_count, L, kv_count, HD)
    value_seq = value_rows.reshape(seq_count, L, kv_count, HD)
    attended, log_total = lax.map(
        lambda block_in: attend(block_in[0], block_in[1], block_in[2]),
        (query_seq, key_seq, value_seq),
    )
    attended_rows = attended.reshape(tokens, query_cols)
    part = matmul_nt(attended_rows, out_w).astype(jnp.bfloat16)
    grad_rows = out_grad.astype(jnp.bfloat16)

    hidden, norm_part, norm_other, out_part, out_pair, partial, sums_early, sums_late, *both = ffn_pass(
        shards, layer_input, part, gain_two, grad_rows, (same, below, above, across)
    )
    partial = hop(partial, lambda row, side: (row, 1 - side))
    from_below = hop(
        sums_early, lambda row, side: (row + 2, side) if row < half_line else None
    )
    from_above = hop(sums_early, lambda row, side: (row - 2, side) if row >= half_line else None)
    inv_two, norm_two = rms_parts(hidden)
    d_norm_two = norm_part.astype(jnp.float32) + norm_other.astype(jnp.float32)
    grad_gain_two = jnp.sum(d_norm_two * norm_two, axis=0)
    e_two = d_norm_two * gain_two
    d_hidden = out_grad + inv_two * (
        e_two - norm_two * jnp.mean(e_two * norm_two, axis=-1, keepdims=True)
    )
    hidden_rows = d_hidden.astype(jnp.bfloat16)
    d_attended = matmul(hidden_rows, out_w).astype(jnp.bfloat16)
    d_query, d_keys, d_values = lax.map(
        lambda block_in: attend_back(
            block_in[0], block_in[1], block_in[2], block_in[3], block_in[4], block_in[5]
        ),
        (
            query_seq,
            key_seq,
            value_seq,
            attended,
            d_attended.reshape(seq_count, L, query_cols),
            log_total,
        ),
    )
    dq_raw = (
        rotate(d_query.reshape(tokens, head_count, HD), cos_table, sin_table, -1.0)
        .astype(jnp.bfloat16)
        .reshape(tokens, query_cols)
    )
    dk_raw = (
        rotate(d_keys.reshape(tokens, kv_count, HD), cos_table, sin_table, -1.0)
        .astype(jnp.bfloat16)
        .reshape(tokens, kv_cols)
    )
    dv_rows = d_values.astype(jnp.bfloat16).reshape(tokens, kv_cols)
    d_qkv = jnp.concatenate([dq_raw, dk_raw, dv_rows], axis=1)
    norm_one_part = matmul_nt(d_qkv, qkv_w).astype(jnp.bfloat16)

    sums = grad_gain_two.reshape(shards, 1, rows)
    sums = jnp.pad(sums, ((0, 0), (0, 7), (0, max(128 - rows, 0))))
    (
        layer_output,
        x_grad,
        shard_gate,
        shard_up,
        shard_down,
        shard_out,
        shard_qkv,
        sums_out,
    ) = reduce_pass(
        shards,
        both,
        (hidden_rows, normed_one, attended_rows, d_qkv),
        (partial, sums_late, from_below, from_above),
        out_part,
        out_pair,
        norm_one_part,
        (hidden, d_hidden, norm_one),
        inv_one,
        gain_one,
        sums,
    )
    cuts = [((0, array.shape[1]),) for array in (layer_output, x_grad)]
    cuts.append(
        ((0, query_cols), (query_cols, kv_cols), (query_cols + kv_cols, kv_cols))
    )
    cuts += [((0, array.shape[1]),) for array in (shard_out, shard_gate, shard_up, shard_down)]
    (
        layer_output,
        x_grad,
        shard_query,
        shard_key,
        shard_value,
        shard_out,
        shard_gate,
        shard_up,
        shard_down,
        sums_one,
        sums_two,
    ) = emit(
        (layer_output, x_grad, shard_qkv, shard_out, shard_gate, shard_up, shard_down),
        cuts,
        sums_out,
        rows,
    )
    return (
        layer_output,
        x_grad,
        sums_one,
        shard_query,
        shard_key,
        shard_value,
        shard_out,
        sums_two,
        shard_gate,
        shard_up,
        shard_down,
    )


def solution(mesh):
    in_specs = (
        P("dp", None),
        P("dp"),
        P("dp"),
        P("dp", "tensor"),
        P("dp", "tensor"),
        P("dp", "tensor"),
        P("tensor", "dp"),
        P("dp"),
        P("dp", "tensor"),
        P("dp", "tensor"),
        P("tensor", "dp"),
        P("dp", None),
    )
    out_specs = (
        P("dp", None),
        P("dp", None),
        P("dp"),
        P("dp", "tensor"),
        P("dp", "tensor"),
        P("dp", "tensor"),
        P("tensor", "dp"),
        P("dp"),
        P("dp", "tensor"),
        P("dp", "tensor"),
        P("tensor", "dp"),
    )

    def layer(*args):
        return body(mesh.shape["dp"], *args)

    return jax.shard_map(
        layer, mesh=mesh, in_specs=in_specs, out_specs=out_specs, check_vma=False
    )
```

time: 497 us -> 469 us (0.944)
  the two profiles are of different devices: /device:TPU:0 before, /device:TPU:10 now
where the time goes in v4:
time: 469 us; the launch traced here: 462 us
  Pallas kernels  379 us (81%)
  matrix products  24.4 us (5%)
  other arithmetic  16.8 us (4%)
  waiting for transfers between devices  14.5 us (3%)
  starting transfers between devices  13.6 us (3%)
  local copies, waits for them, and re-layouts  12.7 us (3%)
    pallas_call x1, Pallas kernels, reduce_pass(): pl.pallas_call(functools.partial(reduce_kernel, shards, ffn_chunks, head_...  162 us
    pallas_call x1, Pallas kernels, ffn_pass(): pl.pallas_call(functools.partial(ffn_kernel, shards, groups, chunks), out...  156 us
    pallas_call x1, Pallas kernels, gather_shards(): pl.pallas_call(functools.partial(gather_kernel, shards), out_shape=(jax.S...  52.6 us
    ppermute x6, waiting for transfers between devices, hop(): return lax.ppermute(value, 'dp', device_pairs(shards, move))  14.5 us
    ppermute x6, starting transfers between devices, hop(): return lax.ppermute(value, 'dp', device_pairs(shards, move))  13.6 us
    dot_general x2, matrix products, matmul_nt(): lax.dot_general(left_side, right_side, (((1,), (1,)), ((), ())), preferre...  9.47 us
  transfers between devices with their start and end apart: 6, of which 2 were waited for; matrix products, arithmetic and copies ran while one was open for 7% of the time, Pallas kernels for 0%

profile of v4, /device:TPU:10, one launch (start us, length us, event | category | flops | bytes accessed | tf_op | source)
XLA Modules:
  0.0 462.4 jit_solution(1798340386737305745)
XLA Ops:
  0.6 1.3 fusion.14.refs_0_
  1.9 52.6 %gather_attention.1 = (f32[16,8,128]{2,1,0:T(8,128)}, bf16[16,128,1280]{2,1,0:T(8,128)(2,1)}, bf16[16,128,1024]{2,1,0:T(8,128)(2,1)}, bf16[128,4224]{1,0:T(8,128)(2,1)}, bf16[128,4224]{1,0:T(8,128)(2,1)}) custom-call(f32[8,128]{1,0:T(8,128)} %fusion.14.refs_0_, bf16[128,1024]{1,0:T(8,128)(2,1)} %refs_1_.1, bf16[128,128]{1,0:T(8,128)(2,1)} %refs_2_.1, ...), custom_call_target="tpu_custom_call" | custom-call | tf_op jit(solution)/shard_map/gather_attention/pallas_call | solution.py:354
  54.5 3.0 collective-permute-start
  57.5 3.9 collective-permute-start.1
  61.5 1.1 collective-permute-start.2
  62.6 1.5 slice_bitcast_fusion.1
  64.1 1.8 multiply_reduce_fusion.3
  66.0 1.6 multiply_convert_fusion
  67.6 2.0 copy-done.34
  69.6 1.5 fusion.23
  74.8 1.5 exponential_reduce_fusion
  77.9 1.1 convert_element_type.92.refs_3_
  79.0 3.3 convolution_convert_fusion.3
  82.3 1.0 copy.53.refs_7_
  84.1 4.5 convolution_convert_fusion.refs_1_
  88.6 156.1 %ffn_pairs.1 = (f32[256,2048]{1,0:T(8,128)}, bf16[256,2048]{1,0:T(8,128)(2,1)}, bf16[256,2048]{1,0:T(8,128)(2,1)}, bf16[256,2048]{1,0:T(8,128)(2,1)}, bf16[256,2...) custom-call(f32[256,2048]{1,0:T(8,128)} %refs_0_.1, ...), custom_call_target="tpu_custom_call" | custom-call | tf_op jit(solution)/shard_map/ffn_pairs/pallas_call | solution.py:1077
  244.7 2.0 multiply_reduce_fusion.2
  246.9 2.5 multiply_reduce_fusion
  249.7 2.1 fusion.22
  251.7 1.0 copy-done.7
  252.7 1.3 convolution_convert_fusion.2
  254.9 3.6 fusion.2
  260.6 3.3 collective-permute-start.4
  263.9 1.3 collective-permute-start.5
  266.4 0.9 collective-permute-start.3
  267.4 3.2 fusion.6
  270.7 0.9 pad_maximum_fusion.refs_8_
  272.2 5.0 %convolution_convert_fusion.1.refs_15_ = bf16[256,2048]{1,0:T(8,128)(2,1)} fusion(bf16[2048,1280]{1,0:T(8,128)(2,1)} %bitcast.111, bf16[256,128]{1,0:T(8,128)(2,1)S(1)} %copy.52, bf16[256,128]{1,0:T(8,128)(2,1)S(1)} %copy.51, bf16[256,1024]{1,0:T(8,128)(2,1)S(1)} %copy.50), kind=kOutput, calls=%fused_computation.10 | convolution fusion | flops 1344667648 | bytes 6946816 | tf_op jit(solution)/shard_map/dot_general | solution.py:29
  277.2 9.5 %collective-permute-done.4.refs_11_ = bf16[128,2176]{1,0:T(8,128)(2,1)} collective-permute-done((bf16[128,2176]{1,0:T(8,128)(2,1)S(1)}, bf16[128,2176]{1,0:T(8,128)(2,1)}, u32[]{:S(2)}, u32[]{:S(2)}) %collective-permute-start.4) | collective-permute-done | bytes 557088 | tf_op jit(solution)/shard_map/ppermute | solution.py:1861
  286.7 5.0 %collective-permute-done.3.refs_9_ = bf16[128,4224]{1,0:T(8,128)(2,1)} collective-permute-done((bf16[128,4224]{1,0:T(8,128)(2,1)S(1)}, bf16[128,4224]{1,0:T(8,128)(2,1)}, u32[]{:S(2)}, u32[]{:S(2)}) %collective-permute-start.3) | collective-permute-done | bytes 1081376 | tf_op jit(solution)/shard_map/ppermute | solution.py:1861
  291.7 161.6 %reduce_pairs.1 = (f32[256,2048]{1,0:T(8,128)}, f32[256,2048]{1,0:T(8,128)}, f32[128,2816]{1,0:T(8,128)}, f32[128,2816]{1,0:T(8,128)}, f32[2816,128]{1,0:T(8,128...) custom-call(bf16[1024,2048]{1,0:T(8,128)(2,1)} %get-tuple-element.101.refs_0_, ...), custom_call_target="tpu_custom_call" | custom-call | tf_op jit(solution)/shard_map/reduce_pairs/pallas_call | solution.py:1693
  453.4 8.6 %emit_results.1 = (f32[256,2048]{1,0:T(8,128)}, f32[256,2048]{1,0:T(8,128)}, f32[128,1024]{1,0:T(8,128)}, f32[128,128]{1,0:T(8,128)}, f32[128,128]{1,0:T(8,128)}...) custom-call(f32[256,2048]{1,0:T(8,128)} %get-tuple-element.114.refs_, ...), custom_call_target="tpu_custom_call" | custom-call | tf_op jit(solution)/shard_map/emit_results/pallas_call | solution.py:1815
  (108 shorter events, 11.2 us)
Async XLA Ops:
  54.5 11.5 %copy-start.1 = (f32[256,2048]{1,0:T(8,128)S(1)}, f32[256,2048]{1,0:T(8,128)}, u32[]{:S(2)}) copy-start(f32[256,2048]{1,0:T(8,128)} %refs_0_.1) | copy-start | bytes 6291460
  54.5 34.0 %collective-permute-start = (bf16[128,4224]{1,0:T(8,128)(2,1)}, bf16[128,4224]{1,0:T(8,128)(2,1)}, u32[]{:S(2)}, u32[]{:S(2)}) collective-permute-start(bf16[128,4224]{1,0:T(8,128)(2,1)} %get-tuple-element.100), channel_id=1, source_target_pairs={{0,8},{2,10},{4,12},{6,14},{8,16},{10,18},{12,20},{14,22},{16,24},... | collective-permute-start | bytes 3244040 | tf_op jit(solution)/shard_map/ppermute | solution.py:1861
  57.5 31.0 %collective-permute-start.1 = (bf16[128,4224]{1,0:T(8,128)(2,1)}, bf16[128,4224]{1,0:T(8,128)(2,1)}, u32[]{:S(2)}, u32[]{:S(2)}) collective-permute-start(bf16[128,4224]{1,0:T(8,128)(2,1)} %get-tuple-element.100), channel_id=1, source_target_pairs={{8,0},{10,2},{12,4},{14,6},{16,8},{18,10},{20,12},{22,14},{24,16},... | collective-permute-start | bytes 3244040 | tf_op jit(solution)/shard_map/ppermute | solution.py:1861
  61.5 27.1 %collective-permute-start.2 = (bf16[128,4224]{1,0:T(8,128)(2,1)}, bf16[128,4224]{1,0:T(8,128)(2,1)}, u32[]{:S(2)}, u32[]{:S(2)}) collective-permute-start(bf16[128,4224]{1,0:T(8,128)(2,1)} %get-tuple-element.99.refs_4_), channel_id=1, source_target_pairs={{0,4},{2,6},{4,0},{6,2},{8,12},{10,14},{12,8},{14,10},{16,20},{18,... | collective-permute-start | bytes 3244040 | tf_op jit(solution)/shard_map/ppermute | solution.py:1861
  66.0 1.6 copy-start.31
  66.0 3.6 copy-start.34
  67.6 3.6 copy-start.8
  72.3 1.5 copy-start.18
  73.4 1.3 copy-start.11
  73.4 1.3 copy-start.13
  74.7 2.2 copy-start.4
  74.7 3.1 copy-start.2
  76.9 2.1 copy-start.26
  77.9 4.4 copy-start.27
  79.0 3.3 copy-start.29
  79.0 4.3 copy-start.32
  82.3 6.3 %copy-start.9 = (bf16[2,64,8,256]{3,1,2,0:T(8,128)(2,1)}, bf16[2,64,8,256]{3,1,2,0:T(8,128)(2,1)S(1)}, u32[]{:S(2)}) copy-start(bf16[2,64,8,256]{3,1,2,0:T(8,128)(2,1)S(1)} %convolution_convert_fusion.3) | copy-start | bytes 1572868
  244.7 2.2 copy-start
  244.7 2.2 copy-start.25
  246.9 2.5 copy-start.3
  246.9 2.6 copy-start.5
  246.9 2.8 copy-start.6
  249.7 3.0 copy-start.35
  252.7 1.5 copy-start.10
  254.9 3.6 copy-start.22
  254.9 3.6 copy-start.24
  259.6 5.6 %copy-start.16 = (f32[256,32]{0,1:T(8,128)S(1)}, f32[256,32]{0,1:T(8,128)}, u32[]{:S(2)}) copy-start(f32[256,32]{0,1:T(8,128)} %copy-done.15) | copy-start | bytes 98308
  259.6 5.6 %copy-start.17 = (f32[256,32]{0,1:T(8,128)S(1)}, f32[256,32]{0,1:T(8,128)}, u32[]{:S(2)}) copy-start(f32[256,32]{0,1:T(8,128)} %get-tuple-element.151) | copy-start | bytes 98308
  260.6 26.1 %collective-permute-start.4 = (bf16[128,2176]{1,0:T(8,128)(2,1)S(1)}, bf16[128,2176]{1,0:T(8,128)(2,1)}, u32[]{:S(2)}, u32[]{:S(2)}) collective-permute-start(bf16[128,2176]{1,0:T(8,128)(2,1)S(1)} %copy-done.37), channel_id=1, source_target_pairs={{0,16},{2,18},{4,20},{6,22},{8,24},{10,26},{12,28},{14,30},{1,17},... | collective-permute-start | bytes 1671176 | tf_op jit(solution)/shard_map/ppermute | solution.py:1861
  263.9 22.9 %collective-permute-start.5 = (bf16[128,2176]{1,0:T(8,128)(2,1)S(1)}, bf16[128,2176]{1,0:T(8,128)(2,1)}, u32[]{:S(2)}, u32[]{:S(2)}) collective-permute-start(bf16[128,2176]{1,0:T(8,128)(2,1)S(1)} %copy-done.37), channel_id=1, source_target_pairs={{16,0},{18,2},{20,4},{22,6},{24,8},{26,10},{28,12},{30,14},{17,1},... | collective-permute-start | bytes 1671176 | tf_op jit(solution)/shard_map/ppermute | solution.py:1861
  265.2 1.2 copy-start.36
  266.4 25.3 %collective-permute-start.3 = (bf16[128,4224]{1,0:T(8,128)(2,1)S(1)}, bf16[128,4224]{1,0:T(8,128)(2,1)}, u32[]{:S(2)}, u32[]{:S(2)}) collective-permute-start(bf16[128,4224]{1,0:T(8,128)(2,1)S(1)} %copy-done.36), channel_id=1, source_target_pairs={{0,4},{2,6},{4,0},{6,2},{8,12},{10,14},{12,8},{14,10},{16,20},{18,... | collective-permute-start | bytes 3244040 | tf_op jit(solution)/shard_map/ppermute | solution.py:1861
  (12 other events, 11.6 us)
